TPU v7x, 128 devices: a whole 4x4x4 slice. The times are simulated.
128 devices in a mesh: row: 8 (over x, core), col: 16 (over z, y).
Axes of the slice: x: 4, y: 4, z: 4, core: 2. Of those that a mesh axis runs over, the one named last changes fastest.
Arguments:
- covariates: float32 [16, 32768], P(None, ('row', 'col')), may hold values from -6 to 6
- lengthscale: float32 [16], replicated, may hold values from 1 to 3
- nugget: float32 [32768], P(('row', 'col')), may hold values from 0.5 to 2
- patch_values: bfloat16 [32768, 16, 128], P(('row', 'col')), may hold values from -6 to 6
- patch_weights: bfloat16 [32768, 8, 128], P(('row', 'col')), may hold values from 0 to 0.1796875
- block_index: int32 [32768, 8], P(('row', 'col')), may hold values from 0 to 255
- slot_count: int32 [32768], P(('row', 'col')), may hold values from 1 to 8
- owner: int32 [32768, 1], P(('row', 'col')), may hold values from 0 to 127; in each aligned block of 256 rows (0 to 255, 256 to 511, ...) at most 4 rows name the same one
Outputs:
- solution: float32 [16, 32768], P(None, ('row', 'col'))
- residual: float32 [16, 32768], P(None, ('row', 'col'))
Inputs may be any that keep to these rules, and one draw needn't show every extreme that they name: Among the 256 patches held by one device, no owner is named more than 4 times.
All inputs are finite; a program needn't handle non-finite values.
Results may differ from a plain program's by a relative error of at most 0.00045.
Values may be sent and summed in bfloat16 or wider, within the bound.
No kernel may reach another device: no remote copies, remote signals or barrier semaphores. Data moves between devices by JAX's collectives and lax.ppermute only.
A program may use at most 64 MiB of HBM per device.

v0:
```python
import math

import jax
import jax.numpy as jnp
from jax import lax
from jax.sharding import Mesh
from jax.sharding import PartitionSpec as P

ITERS = 2
ROW_COL = ("row_0", "row_1", "col_0", "col_1")
COL = ("col_0", "col_1")
ROW = ("row_0", "row_1")


ROOT_FIVE = 5.0**0.5
HIGH = lax.Precision.HIGHEST


def over_axes(shard, axes):
    for axis in axes:
        shard = lax.psum(shard, axis)
    return shard


def in_one_piece(arrays, axis, dim, along):
    both = jnp.concatenate(arrays, axis=along)
    filled, at, outs = (lax.all_gather(both, axis, axis=dim, tiled=True), 0, [])
    for a in arrays:
        outs.append(lax.slice_in_dim(filled, at, at + a.shape[along], axis=along))
        at += a.shape[along]
    return tuple(outs)


def split_up(shard, dim, devices):
    before, after = (shard.shape[:dim], shard.shape[dim + 1 :])
    return jnp.moveaxis(shard.reshape(*before, devices, -1, *after), dim, 0)


def sum_at_owner(shard, axis, dim):
    devices = lax.axis_size(axis)
    blocks = lax.all_to_all(split_up(shard, dim, devices), axis, 0, 0, tiled=True)
    return jnp.sum(blocks, axis=0)


def matern(left, right):
    cross = lax.dot_general(
        left, right, (((0,), (0,)), ((), ())), precision=HIGH, preferred_element_type=jnp.float32
    )
    squared = (
        jnp.sum(left * left, axis=0)[:, None]
        + jnp.sum(right * right, axis=0)[None, :]
        - 2.0 * cross
    )
    scaled = ROOT_FIVE * jnp.sqrt(jnp.maximum(squared, 0.0))
    return (1.0 + scaled + scaled * scaled / 3.0) * jnp.exp(-scaled)


def slot_table(owner, capacity, devices):
    target = owner[:, 0]
    held = target.shape[0]
    earlier = jnp.arange(held)[None, :] < jnp.arange(held)[:, None]
    rank = jnp.sum(((target[:, None] == target[None, :]) & earlier).astype(jnp.int32), axis=1)
    position = target * capacity + rank
    return position[None, :] == jnp.arange(devices * capacity)[:, None]


def interpolate(pieces):
    values, weights, index, valid = pieces
    terms = jnp.einsum("dksc,dkmc->dkms", weights, values, preferred_element_type=jnp.float32)
    live = (jnp.arange(index.shape[-1])[None, None, :] < valid[:, :, None]).astype(jnp.float32)
    return (terms * live[:, :, None, :], index)


def both_products(residual, image):
    return (
        over_axes(jnp.sum(residual * residual, axis=1), ROW_COL),
        over_axes(jnp.sum(residual * image, axis=1), ROW_COL),
    )


def local(
    covariates, lengthscale, nugget, patch_values, patch_weights, block_index, slot_count, owner
):
    devices = lax.axis_size(ROW_COL)
    held, members, cells = patch_values.shape
    slots = patch_weights.shape[1]
    stations = nugget.shape[0]
    capacity = max(2, 2 * held // devices)
    table = slot_table(owner, capacity, devices)
    table_int = table.astype(jnp.int32)
    placed_index = jnp.dot(table_int, block_index, preferred_element_type=jnp.int32).reshape(
        devices, capacity, slots
    )
    table_half = table.astype(jnp.bfloat16)
    placed_values = jnp.dot(
        table_half, patch_values.reshape(held, members * cells), preferred_element_type=jnp.float32
    )
    placed_values = placed_values.astype(jnp.bfloat16).reshape(devices, capacity, members, cells)
    placed_weights = jnp.dot(
        table_half, patch_weights.reshape(held, slots * cells), preferred_element_type=jnp.float32
    )
    placed_weights = placed_weights.astype(jnp.bfloat16).reshape(devices, capacity, slots, cells)
    placed_count = jnp.dot(
        table_int, slot_count[:, None], preferred_element_type=jnp.int32
    ).reshape(devices, capacity)
    terms, index = interpolate(
        (
            lax.all_to_all(placed_values, ROW_COL, split_axis=0, concat_axis=0, tiled=True),
            lax.all_to_all(placed_weights, ROW_COL, split_axis=0, concat_axis=0, tiled=True),
            lax.all_to_all(placed_index, ROW_COL, split_axis=0, concat_axis=0, tiled=True),
            lax.all_to_all(placed_count, ROW_COL, split_axis=0, concat_axis=0, tiled=True),
        )
    )
    flat_terms = jnp.transpose(terms.reshape(-1, members, slots), (1, 0, 2)).reshape(members, -1)
    onehot = (index.reshape(-1)[:, None] == jnp.arange(stations)[None, :]).astype(jnp.float32)
    rhs = jnp.dot(flat_terms, onehot, precision=HIGH, preferred_element_type=jnp.float32)
    scaled_cov = covariates / lengthscale[:, None]
    row_cov = lax.all_gather(scaled_cov, COL, axis=1, tiled=True)

    def operate(direction):
        empty = jnp.zeros((direction.shape[0], row_cov.shape[1]), jnp.float32)
        column_cov, vector = in_one_piece((scaled_cov, direction), ROW, 1, 0)
        width = math.gcd(vector.shape[1], 128)

        def one_block(step, acc):
            block_cov = lax.dynamic_slice_in_dim(column_cov, step * width, width, 1)
            block_vec = lax.dynamic_slice_in_dim(vector, step * width, width, 1)
            kernel = matern(block_cov, row_cov)
            return acc + jnp.dot(
                block_vec, kernel, precision=HIGH, preferred_element_type=jnp.float32
            )

        partial_value = lax.fori_loop(0, vector.shape[1] // width, one_block, empty)
        image = sum_at_owner(partial_value, COL, 1)
        return image + nugget[None, :] * direction

    solution = jnp.zeros_like(rhs)
    residual = rhs
    image = operate(residual)
    norm_now, product = both_products(residual, image)
    alpha = norm_now / product
    direction = residual
    along = image
    for step in range(ITERS):
        solution = solution + alpha[:, None] * direction
        residual = residual - alpha[:, None] * along
        if step + 1 < ITERS:
            image = operate(residual)
            norm_next, product = both_products(residual, image)
            ratio = norm_next / norm_now
            alpha = norm_next / (product - ratio * norm_next / alpha)
            direction = residual + ratio[:, None] * direction
            along = image + ratio[:, None] * along
            norm_now = norm_next
    return (solution, residual)


def solution(mesh):
    torus = Mesh(mesh.devices.reshape(4, 2, 4, 4), ("row_0", "row_1", "col_0", "col_1"))
    placed = (
        P(None, ROW_COL),
        P(),
        P(ROW_COL),
        P(ROW_COL, None, None),
        P(ROW_COL, None, None),
        P(ROW_COL, None),
        P(ROW_COL),
        P(ROW_COL, None),
    )
    return jax.shard_map(
        local,
        mesh=torus,
        in_specs=placed,
        out_specs=(P(None, ROW_COL), P(None, ROW_COL)),
        check_vma=False,
    )
```

profile of v0, /device:TPU:1, one launch (start us, length us, event | category | flops | bytes accessed | tf_op | source)
XLA Modules:
  0.0 360.3 jit_solution(3943338663045249223)
XLA Ops:
  4.3 11.5 %all-to-all-start.2 = ((s32[128,1,4]{2,1,0:T(1,128)}), s32[128,1,4]{2,1,0:T(1,128)S(1)}, u32[]{:S(2)}, u32[]{:S(2)}) async-start(s32[128,1,4]{2,1,0:T(1,128)} %bitcast.3), calls=%async_computation.2 | async-start | bytes 131072 | tf_op jit(solution)/shard_map/all_to_all | solution.py:111
  16.9 8.7 %all-to-all-done.2 = s32[128,1,4]{2,1,0:T(1,128)S(1)} async-done(((s32[128,1,4]{2,1,0:T(1,128)}), s32[128,1,4]{2,1,0:T(1,128)S(1)}, u32[]{:S(2)}, u32[]{:S(2)}) %all-to-all-start.2) | async-done | bytes 2080 | tf_op jit(solution)/shard_map/all_to_all | solution.py:111
  25.6 4.3 %all-to-all-start.3 = ((s32[128,4,8]{2,1,0:T(4,128)}), s32[128,4,8]{2,1,0:T(4,128)S(1)}, u32[]{:S(2)}, u32[]{:S(2)}) async-start(s32[128,4,8]{2,1,0:T(4,128)} %bitcast.8), calls=%async_computation.3 | async-start | bytes 524288 | tf_op jit(solution)/shard_map/all_to_all | solution.py:110
  32.7 8.7 %all-to-all-done.3 = s32[128,4,8]{2,1,0:T(4,128)S(1)} async-done(((s32[128,4,8]{2,1,0:T(4,128)}), s32[128,4,8]{2,1,0:T(4,128)S(1)}, u32[]{:S(2)}, u32[]{:S(2)}) %all-to-all-start.3) | async-done | bytes 16416 | tf_op jit(solution)/shard_map/all_to_all | solution.py:110
  41.3 4.0 %all-to-all-start.1 = ((bf16[128,4,8,128]{3,2,1,0:T(8,128)(2,1)}), bf16[128,4,8,128]{3,2,1,0:T(8,128)(2,1)S(1)}, u32[]{:S(2)}, u32[]{:S(2)}) async-start(bf16[128,4,8,128]{3,2,1,0:T(8,128)(2,1)} %bitcast.22), calls=%async_computation.1 | async-start | bytes 2097152 | tf_op jit(solution)/shard_map/all_to_all | solution.py:109
  48.1 16.2 %all-to-all-done.1 = bf16[128,4,8,128]{3,2,1,0:T(8,128)(2,1)S(1)} async-done(((bf16[128,4,8,128]{3,2,1,0:T(8,128)(2,1)}), bf16[128,4,8,128]{3,2,1,0:T(8,128)(2,1)S(1)}, u32[]{:S(2)}, u32[]{:S(2)}) %all-to-all-start.1) | async-done | bytes 1048608 | tf_op jit(solution)/shard_map/all_to_all | solution.py:109
  64.3 4.8 %all-to-all-start = ((bf16[128,4,16,128]{3,2,1,0:T(8,128)(2,1)}), bf16[128,4,16,128]{3,2,1,0:T(8,128)(2,1)S(1)}, u32[]{:S(2)}, u32[]{:S(2)}) async-start(bf16[128,4,16,128]{3,2,1,0:T(8,128)(2,1)} %bitcast.17), calls=%async_computation | async-start | bytes 4194304 | tf_op jit(solution)/shard_map/all_to_all | solution.py:108
  69.2 35.5 %all_gather.10 = f32[16,4096]{1,0:T(8,128)S(1)} all-gather(f32[16,256]{1,0:T(8,128)S(1)} %broadcast_divide_fusion), channel_id=1, replica_groups=mesh['row_0'=4,'row_1'=2,'col_0'=4,'col_1'=4] {'col_0','col_1'}, dimensions={1}, use_global_device_ids=true | all-gather | bytes 278528 | tf_op jit(solution)/shard_map/all_gather | solution.py:118
  111.5 21.5 %all_gather.9 = f32[32,2048]{1,0:T(8,128)S(1)} all-gather(f32[32,256]{1,0:T(8,128)S(1)} %pad_maximum_fusion.1), channel_id=1, replica_groups=mesh['row_0'=4,'row_1'=2,'col_0'=4,'col_1'=4] {'row_0','row_1'}, dimensions={1}, use_global_device_ids=true | all-gather | bytes 294912 | tf_op jit(solution)/shard_map/all_gather | solution.py:27
  133.0 67.0 %while.32 = (s32[]{:T(128)}, f32[16,4096]{1,0:T(8,128)S(1)}, f32[16,2048]{1,0:T(8,128)S(1)}, f32[16,2048]{1,0:T(8,128)S(1)}, f32[4096]{0:T(1024)S(1)}, /*index=5...) while((s32[]{:T(128)}, f32[16,4096]{1,0:T(8,128)S(1)}, ...), condition=%wide.region_9.0_spmd.clone, body=%wide.region_7.9_spmd.clone.sunk | while | flops 207228800 | bytes 5022889 | solution.py:133
  141.4 2.6 fusion.77
  158.2 2.6 fusion.77
  174.9 2.6 fusion.77
  191.7 2.6 fusion.77
  201.0 3.9 %all-to-all-start.4 = ((f32[16,16,256]{2,1,0:T(8,128)}), f32[16,16,256]{2,1,0:T(8,128)S(1)}, u32[]{:S(2)}, u32[]{:S(2)}) async-start(f32[16,16,256]{2,1,0:T(8,128)} %copy.16), calls=%async_computation.4 | async-start | bytes 524288 | tf_op jit(solution)/shard_map/all_to_all | solution.py:41
  204.9 8.3 %all-to-all-done.4 = f32[16,16,256]{2,1,0:T(8,128)S(1)} async-done(((f32[16,16,256]{2,1,0:T(8,128)}), f32[16,16,256]{2,1,0:T(8,128)S(1)}, u32[]{:S(2)}, u32[]{:S(2)}) %all-to-all-start.4) | async-done | bytes 262176 | tf_op jit(solution)/shard_map/all_to_all | solution.py:41
  213.4 7.1 %all-reduce.5 = (f32[16]{0:T(128)S(1)}, f32[16]{0:T(128)S(1)}) all-reduce(f32[16]{0:T(128)S(1)} %get-tuple-element.315, f32[16]{0:T(128)S(1)} %get-tuple-element.314), channel_id=1, replica_groups=mesh['row_0'=4,'row_1'=2,'col_0'=4,'col_1'=4] {'row_0'}, use_global_device_ids=true, to_apply=%region_2.3 | all-reduce | flops 32 | bytes 256 | tf_op jit(solution)/shard_map/psum | solution.py:21
  220.5 5.4 %all-reduce.7 = (f32[16]{0:T(128)S(1)}, f32[16]{0:T(128)S(1)}) all-reduce(f32[16]{0:T(128)S(1)} %get-tuple-element.350, f32[16]{0:T(128)S(1)} %get-tuple-element.351), channel_id=1, replica_groups=mesh['row_0'=4,'row_1'=2,'col_0'=4,'col_1'=4] {'row_1'}, use_global_device_ids=true, to_apply=%region_3.4 | all-reduce | flops 32 | bytes 256 | tf_op jit(solution)/shard_map/psum | solution.py:21
  225.9 6.5 %all-reduce.3 = (f32[16]{0:T(128)S(1)}, f32[16]{0:T(128)S(1)}) all-reduce(f32[16]{0:T(128)S(1)} %get-tuple-element.354, f32[16]{0:T(128)S(1)} %get-tuple-element.355), channel_id=1, replica_groups=mesh['row_0'=4,'row_1'=2,'col_0'=4,'col_1'=4] {'col_0'}, use_global_device_ids=true, to_apply=%region_4.0 | all-reduce | flops 32 | bytes 256 | tf_op jit(solution)/shard_map/psum | solution.py:21
  232.4 6.6 %all-reduce.1 = (f32[16]{0:T(128)S(1)}, f32[16]{0:T(128)S(1)}) all-reduce(f32[16]{0:T(128)S(1)} %get-tuple-element.346, f32[16]{0:T(128)S(1)} %get-tuple-element.347), channel_id=1, replica_groups=mesh['row_0'=4,'row_1'=2,'col_0'=4,'col_1'=4] {'col_1'}, use_global_device_ids=true, to_apply=%region_5.0 | all-reduce | flops 32 | bytes 256 | tf_op jit(solution)/shard_map/psum | solution.py:21
  239.1 17.0 %all_gather.11 = f32[32,2048]{1,0:T(8,128)S(1)} all-gather(f32[32,256]{1,0:T(8,128)S(1)} %pad_maximum_fusion), channel_id=1, replica_groups=mesh['row_0'=4,'row_1'=2,'col_0'=4,'col_1'=4] {'row_0','row_1'}, dimensions={1}, use_global_device_ids=true | all-gather | bytes 294912 | tf_op jit(solution)/shard_map/all_gather | solution.py:27
  256.2 67.1 %while.33 = (s32[]{:T(128)}, f32[16,4096]{1,0:T(8,128)S(1)}, f32[16,2048]{1,0:T(8,128)S(1)}, f32[16,2048]{1,0:T(8,128)S(1)}, f32[4096]{0:T(1024)S(1)}, /*index=5...) while((s32[]{:T(128)}, f32[16,4096]{1,0:T(8,128)S(1)}, ...), condition=%wide.region_23.0_spmd.clone, body=%wide.region_21.23_spmd.clone.sunk | while | flops 207228800 | bytes 5022889 | solution.py:133
  260.4 2.6 fusion.82
  264.6 2.6 fusion.82
  277.2 2.6 fusion.82
  281.4 2.6 fusion.82
  294.0 2.6 fusion.82
  323.5 11.0 %all_to_all.34 = f32[16,16,256]{2,1,0:T(8,128)S(1)} all-to-all(f32[16,16,256]{2,1,0:T(8,128)S(1)} %copy.17), channel_id=1, replica_groups=mesh['row_0'=4,'row_1'=2,'col_0'=4,'col_1'=4] {'col_0','col_1'}, dimensions={0} | all-to-all | bytes 524288 | tf_op jit(solution)/shard_map/all_to_all | solution.py:41
  334.6 6.4 %all-reduce.4 = (f32[16]{0:T(128)S(1)}, f32[16]{0:T(128)S(1)}) all-reduce(f32[16]{0:T(128)S(1)} %get-tuple-element.313, f32[16]{0:T(128)S(1)} %get-tuple-element.312), channel_id=1, replica_groups=mesh['row_0'=4,'row_1'=2,'col_0'=4,'col_1'=4] {'row_0'}, use_global_device_ids=true, to_apply=%region_17.18 | all-reduce | flops 32 | bytes 256 | tf_op jit(solution)/shard_map/psum | solution.py:21
  341.0 5.4 %all-reduce.6 = (f32[16]{0:T(128)S(1)}, f32[16]{0:T(128)S(1)}) all-reduce(f32[16]{0:T(128)S(1)} %get-tuple-element.348, f32[16]{0:T(128)S(1)} %get-tuple-element.349), channel_id=1, replica_groups=mesh['row_0'=4,'row_1'=2,'col_0'=4,'col_1'=4] {'row_1'}, use_global_device_ids=true, to_apply=%region_18.19 | all-reduce | flops 32 | bytes 256 | tf_op jit(solution)/shard_map/psum | solution.py:21
  346.4 6.5 %all-reduce.2 = (f32[16]{0:T(128)S(1)}, f32[16]{0:T(128)S(1)}) all-reduce(f32[16]{0:T(128)S(1)} %get-tuple-element.352, f32[16]{0:T(128)S(1)} %get-tuple-element.353), channel_id=1, replica_groups=mesh['row_0'=4,'row_1'=2,'col_0'=4,'col_1'=4] {'col_0'}, use_global_device_ids=true, to_apply=%region_19.0 | all-reduce | flops 32 | bytes 256 | tf_op jit(solution)/shard_map/psum | solution.py:21
  352.9 6.6 %all-reduce = (f32[16]{0:T(128)S(1)}, f32[16]{0:T(128)S(1)}) all-reduce(f32[16]{0:T(128)S(1)} %get-tuple-element.344, f32[16]{0:T(128)S(1)} %get-tuple-element.345), channel_id=1, replica_groups=mesh['row_0'=4,'row_1'=2,'col_0'=4,'col_1'=4] {'col_1'}, use_global_device_ids=true, to_apply=%region_20.0 | all-reduce | flops 32 | bytes 256 | tf_op jit(solution)/shard_map/psum | solution.py:21
  (137 shorter events, 129.1 us)
Async XLA Ops:
  0.6 15.2 %copy-start = (s32[256,8]{0,1:T(8,128)S(1)}, s32[256,8]{0,1:T(8,128)}, u32[]{:S(2)}) copy-start(s32[256,8]{0,1:T(8,128)} %param.17) | copy-start | bytes 24580
  4.3 21.3 %all-to-all-start.2 = ((s32[128,1,4]{2,1,0:T(1,128)}), s32[128,1,4]{2,1,0:T(1,128)S(1)}, u32[]{:S(2)}, u32[]{:S(2)}) async-start(s32[128,1,4]{2,1,0:T(1,128)} %bitcast.3), calls=%async_computation.2 | async-start | bytes 131072 | tf_op jit(solution)/shard_map/all_to_all | solution.py:111
  25.6 15.7 %all-to-all-start.3 = ((s32[128,4,8]{2,1,0:T(4,128)}), s32[128,4,8]{2,1,0:T(4,128)S(1)}, u32[]{:S(2)}, u32[]{:S(2)}) async-start(s32[128,4,8]{2,1,0:T(4,128)} %bitcast.8), calls=%async_computation.3 | async-start | bytes 524288 | tf_op jit(solution)/shard_map/all_to_all | solution.py:110
  31.4 13.9 %copy-start.1 = (bf16[256,16,128]{2,1,0:T(8,128)(2,1)S(1)}, bf16[256,16,128]{2,1,0:T(8,128)(2,1)}, u32[]{:S(2)}) copy-start(bf16[256,16,128]{2,1,0:T(8,128)(2,1)} %param.15) | copy-start | bytes 3145732
  41.3 4.7 %copy-start.2 = (s32[128,4,8]{2,1,0:T(4,128)}, s32[128,4,8]{2,1,0:T(4,128)S(1)}, u32[]{:S(2)}) copy-start(s32[128,4,8]{2,1,0:T(4,128)S(1)} %all-to-all-done.3) | copy-start | bytes 49156
  41.3 23.0 %all-to-all-start.1 = ((bf16[128,4,8,128]{3,2,1,0:T(8,128)(2,1)}), bf16[128,4,8,128]{3,2,1,0:T(8,128)(2,1)S(1)}, u32[]{:S(2)}, u32[]{:S(2)}) async-start(bf16[128,4,8,128]{3,2,1,0:T(8,128)(2,1)} %bitcast.22), calls=%async_computation.1 | async-start | bytes 2097152 | tf_op jit(solution)/shard_map/all_to_all | solution.py:109
  64.3 4.8 %copy-start.5 = (f32[16,256]{1,0:T(8,128)S(1)}, f32[16,256]{1,0:T(8,128)}, u32[]{:S(2)}) copy-start(f32[16,256]{1,0:T(8,128)} %param.12) | copy-start | bytes 49156
  64.3 4.8 %copy-start.6 = (f32[16]{0:T(128)S(1)}, f32[16]{0:T(128)}, u32[]{:S(2)}) copy-start(f32[16]{0:T(128)} %param.13) | copy-start | bytes 196
  64.3 42.5 %all-to-all-start = ((bf16[128,4,16,128]{3,2,1,0:T(8,128)(2,1)}), bf16[128,4,16,128]{3,2,1,0:T(8,128)(2,1)S(1)}, u32[]{:S(2)}, u32[]{:S(2)}) async-start(bf16[128,4,16,128]{3,2,1,0:T(8,128)(2,1)} %bitcast.17), calls=%async_computation | async-start | bytes 4194304 | tf_op jit(solution)/shard_map/all_to_all | solution.py:108
  109.1 23.9 %copy-start.3 = (f32[16,4096]{1,0:T(8,128)S(1)}, f32[16,4096]{1,0:T(8,128)}, u32[]{:S(2)}) copy-start(f32[16,4096]{1,0:T(8,128)} %custom-call) | copy-start | bytes 786436
  133.0 80.3 %copy-start.4 = (f32[256]{0:T(256)S(1)}, f32[256]{0:T(256)}, u32[]{:S(2)}) copy-start(f32[256]{0:T(256)} %param.14) | copy-start | bytes 3076
  201.0 12.2 %all-to-all-start.4 = ((f32[16,16,256]{2,1,0:T(8,128)}), f32[16,16,256]{2,1,0:T(8,128)S(1)}, u32[]{:S(2)}, u32[]{:S(2)}) async-start(f32[16,16,256]{2,1,0:T(8,128)} %copy.16), calls=%async_computation.4 | async-start | bytes 524288 | tf_op jit(solution)/shard_map/all_to_all | solution.py:41
where the time goes:
time: 364 us; the launch traced here: 360 us
  matrix products  141 us (39%)
  blocking collectives  136 us (37%)
  waiting for transfers between devices  41.9 us (12%)
  starting transfers between devices  28.4 us (8%)
  local copies, waits for them, and re-layouts  6.42 us (2%)
  other arithmetic  4.75 us (1%)
    dot_general x32, matrix products, matern(): lax.dot_general(left, right, (((0,), (0,)), ((), ())), precision=HIGH, pr...  82.9 us
    psum x8, blocking collectives, over_axes(): shard = lax.psum(shard, axis)  50.6 us
    dot_general x32, matrix products, one_block(): jnp.dot(block_vec, kernel, precision=HIGH, preferred_element_type=jnp.flo...  49.3 us
    all_gather x2, blocking collectives, in_one_piece(): filled, at, outs = (lax.all_gather(both, axis, axis=dim, tiled=True), 0, [])  38.5 us
    all_gather x1, blocking collectives, local(): row_cov = lax.all_gather(scaled_cov, COL, axis=1, tiled=True)  35.5 us
    all_to_all x1, waiting for transfers between devices, local(): lax.all_to_all(placed_weights, ROW_COL, split_axis=0, concat_axis=0, tile...  16.2 us
    all_to_all x1, starting transfers between devices, local(): lax.all_to_all(placed_count, ROW_COL, split_axis=0, concat_axis=0, tiled=...  11.5 us
    all_to_all x1, blocking collectives, sum_at_owner(): lax.all_to_all(split_up(shard, dim, devices), axis, 0, 0, tiled=True)  11 us
  transfers between devices with their start and end apart: 5, of which 4 were waited for; matrix products, arithmetic and copies ran while one was open for 2% of the time, Pallas kernels for 0%

commit v1 on v0

v1 whole, which is shorter than its diff:
```python
import math

import jax
import jax.numpy as jnp
from jax import lax
from jax.experimental import pallas as pl
from jax.experimental.pallas import tpu as pltpu
from jax.sharding import Mesh
from jax.sharding import PartitionSpec as P

ALL = ("row_0", "row_1", "col_0", "col_1")
COL = ("col_0", "col_1")
ROW = ("row_0", "row_1")

HIGH = lax.Precision.HIGHEST
LN2 = math.log(2.0)
SCALE = math.sqrt(5.0) / LN2
FACTOR = LN2 * LN2 / 3.0
LINEAR = 3.0 / LN2
CONST = 3.0 / (LN2 * LN2)
TINY = 1e-30
VMEM = pltpu.MemorySpace.VMEM
MIB = 1 << 20


def spread(shard, axes):
    copies = jnp.broadcast_to(shard[None], (lax.axis_size(axes),) + shard.shape)
    return lax.all_to_all(copies, axes, split_axis=0, concat_axis=0, tiled=True)


def halves(x):
    high = x.astype(jnp.bfloat16).astype(jnp.float32)
    return high, x - high


def thirds(x):
    high, rest = halves(x)
    middle, low = halves(rest)
    return high, middle, low


def features(z, left):
    high, middle, low = thirds(z)
    norm = jnp.sum(z * z, axis=0, keepdims=True)
    n_high, n_middle, n_low = thirds(norm)
    row = lax.broadcasted_iota(jnp.int32, z.shape, 0)
    base = 0 if left else 3
    rest = jnp.zeros_like(z)
    for at, part in ((base, n_high), (base + 1, n_middle), (base + 2, n_low)):
        rest = jnp.where(row == at, jnp.broadcast_to(part, z.shape), rest)
    rest = jnp.where((row >= 3 - base) & (row < 6 - base), 1.0, rest)
    if left:
        parts = [high, high, high, middle, middle, low]
    else:
        parts = [-2.0 * part for part in (high, middle, low, high, middle, high)]
    return jnp.concatenate(parts + [rest, jnp.zeros_like(z)], axis=0)


def kernel_body(zj_ref, zi_ref, high_ref, low_ref, fj_ref, fi_ref):
    width = zj_ref.shape[2]
    for r in range(zj_ref.shape[0]):
        block = features(zj_ref[r] * SCALE, True)
        fj_ref[r * width : (r + 1) * width, :] = jnp.transpose(block).astype(jnp.bfloat16)
    for c in range(zi_ref.shape[0]):
        block = features(zi_ref[c] * SCALE, False)
        fi_ref[:, c * width : (c + 1) * width] = block.astype(jnp.bfloat16)
    tall, wide = 256, 1024
    across = fi_ref.shape[1] // wide

    @pl.loop(0, (fj_ref.shape[0] // tall) * across)
    def _(step):
        rows = pl.ds(pl.multiple_of((step // across) * tall, tall), tall)
        columns = pl.ds(pl.multiple_of((step % across) * wide, wide), wide)
        squared = jnp.dot(
            fj_ref[rows, :], fi_ref[:, columns], preferred_element_type=jnp.float32
        )
        squared = jnp.maximum(squared, TINY)
        root = squared * lax.rsqrt(squared)
        value = (squared + (LINEAR * root + CONST)) * jnp.exp2(-root)
        high = value.astype(jnp.bfloat16)
        high_ref[rows, columns] = high
        low_ref[rows, columns] = (value - high.astype(jnp.float32)).astype(jnp.bfloat16)


def build_kernel(zj, zi):
    rows, columns = zj.shape[0] * zj.shape[2], zi.shape[0] * zi.shape[2]
    return pl.pallas_call(
        kernel_body,
        out_shape=[pltpu.VMEM((rows, columns), jnp.bfloat16)] * 2,
        in_specs=[pl.BlockSpec(memory_space=VMEM)] * 2,
        out_specs=[pl.BlockSpec(memory_space=VMEM)] * 2,
        scratch_shapes=[
            pltpu.VMEM((rows, 128), jnp.bfloat16),
            pltpu.VMEM((128, columns), jnp.bfloat16),
        ],
        compiler_params=pltpu.CompilerParams(vmem_limit_bytes=12 * MIB),
        cost_estimate=pl.CostEstimate(
            flops=40 * rows * columns, bytes_accessed=4 * rows * columns, transcendentals=0
        ),
        name="matern",
    )(zj, zi)


def product_body(v_ref, high_ref, low_ref, out_ref, vv_ref):
    count, members, width = v_ref.shape
    for r in range(count):
        high, low = halves(v_ref[r])
        columns = slice(r * width, (r + 1) * width)
        vv_ref[:members, columns] = high.astype(jnp.bfloat16)
        vv_ref[members:, columns] = low.astype(jnp.bfloat16)
    wide = 2 * width

    @pl.loop(0, high_ref.shape[1] // wide)
    def _(step):
        columns = pl.ds(pl.multiple_of(step * wide, wide), wide)
        vv = vv_ref[...]
        both = jnp.dot(vv, high_ref[:, columns], preferred_element_type=jnp.float32)
        both += jnp.dot(vv, low_ref[:, columns], preferred_element_type=jnp.float32)
        total = FACTOR * (both[:members] + both[members:])
        for t in range(2):
            out_ref[step * 2 + t] = total[:, t * width : (t + 1) * width]


def kernel_product(v, high, low):
    count, members, width = v.shape
    rows, columns = high.shape
    return pl.pallas_call(
        product_body,
        out_shape=jax.ShapeDtypeStruct((columns // width, members, width), jnp.float32),
        in_specs=[pl.BlockSpec(memory_space=VMEM)] * 3,
        out_specs=pl.BlockSpec(memory_space=VMEM),
        scratch_shapes=[pltpu.VMEM((2 * members, rows), jnp.bfloat16)],
        compiler_params=pltpu.CompilerParams(vmem_limit_bytes=12 * MIB),
        cost_estimate=pl.CostEstimate(
            flops=128 * rows * columns, bytes_accessed=4 * rows * columns, transcendentals=0
        ),
        name="product",
    )(v, high, low)


def local(
    covariates, lengthscale, nugget, patch_values, patch_weights, block_index, slot_count, owner
):
    devices = lax.axis_size(ALL)
    held, members, cells = patch_values.shape
    slots = patch_weights.shape[1]
    stations = nugget.shape[0]
    capacity = max(2, 2 * held // devices)

    terms = jnp.einsum(
        "psc,pmc->psm", patch_weights, patch_values, preferred_element_type=jnp.float32
    )
    live = (jnp.arange(slots)[None, :] < slot_count[:, None]).astype(jnp.float32)
    terms = (terms * live[:, :, None]).reshape(held, slots * members)
    target = owner[:, 0]
    earlier = jnp.arange(held)[None, :] < jnp.arange(held)[:, None]
    rank = jnp.sum(((target[:, None] == target[None, :]) & earlier).astype(jnp.int32), axis=1)
    position = rank * devices + target
    table = (position[None, :] == jnp.arange(devices * capacity)[:, None]).astype(jnp.float32)
    payload = jnp.concatenate([terms, block_index.astype(jnp.float32)], axis=1)
    placed = jnp.dot(table, payload, precision=HIGH, preferred_element_type=jnp.float32)
    placed = placed.reshape(capacity, devices, payload.shape[1])
    message = jnp.concatenate(
        [placed[k, :, : slots * members] for k in range(capacity)]
        + [placed[k, :, slots * members :] for k in range(capacity)],
        axis=1,
    )
    message = lax.all_to_all(message, ALL, split_axis=0, concat_axis=0, tiled=True)

    scaled_cov = covariates / lengthscale[:, None]
    high, low = build_kernel(spread(scaled_cov, ROW), spread(scaled_cov, COL))

    entries = capacity * slots
    flat = message[:, : entries * members].reshape(devices, entries, members)
    index = message[:, entries * members :].astype(jnp.int32)
    onehot = (index.reshape(-1)[:, None] == jnp.arange(stations)[None, :]).astype(jnp.float32)
    rhs = lax.dot_general(
        flat.reshape(-1, members),
        onehot,
        (((0,), (0,)), ((), ())),
        precision=HIGH,
        preferred_element_type=jnp.float32,
    )

    def operate(v):
        partial_value = kernel_product(spread(v, ROW), high, low)
        shares = lax.all_to_all(partial_value, COL, split_axis=0, concat_axis=0, tiled=True)
        return jnp.sum(shares, axis=0) + nugget[None, :] * v

    first = operate(rhs)
    second = operate(first)

    def dot(a, b):
        return jnp.sum(a * b, axis=1)

    norm, energy = dot(rhs, rhs), dot(rhs, first)
    guess = jnp.where(energy > 0.5 * norm, norm / jnp.maximum(energy, TINY), 0.0)
    resid = rhs - guess[:, None] * first
    along = first - guess[:, None] * second
    sums = jnp.stack(
        [
            norm,
            energy,
            guess,
            dot(resid, resid),
            dot(resid, first),
            dot(first, first),
            dot(resid, along),
            dot(resid, second) + dot(first, along),
            dot(first, second),
        ]
    ).reshape(1, -1)
    sums = jnp.pad(sums, ((0, 0), (0, -sums.shape[1] % 128)))
    sums = spread(sums, ALL)[:, 0, : 9 * members].reshape(devices, 9, members)
    norm0 = jnp.sum(sums[:, 0], axis=0)
    alpha0 = norm0 / jnp.sum(sums[:, 1], axis=0)
    shift = alpha0[None, :] - sums[:, 2]
    norm1 = jnp.sum(sums[:, 3] - shift * (2.0 * sums[:, 4] - shift * sums[:, 5]), axis=0)
    energy1 = jnp.sum(sums[:, 6] - shift * (sums[:, 7] - shift * sums[:, 8]), axis=0)
    ratio = norm1 / norm0
    alpha1 = norm1 / (energy1 - ratio * norm1 / alpha0)
    residual = rhs - alpha0[:, None] * first
    direction = residual + ratio[:, None] * rhs
    along = (first - alpha0[:, None] * second) + ratio[:, None] * first
    solved = alpha0[:, None] * rhs + alpha1[:, None] * direction
    return (solved, residual - alpha1[:, None] * along)


def solution(mesh):
    torus = Mesh(mesh.devices.reshape(4, 2, 4, 4), ALL)
    placed = (
        P(None, ALL),
        P(),
        P(ALL),
        P(ALL, None, None),
        P(ALL, None, None),
        P(ALL, None),
        P(ALL),
        P(ALL, None),
    )
    return jax.shard_map(
        local,
        mesh=torus,
        in_specs=placed,
        out_specs=(P(None, ALL), P(None, ALL)),
        check_vma=False,
    )
```

time: 364 us -> 177 us (0.49)
  matrix products: 141 us -> 5.17 us
  blocking collectives: 136 us -> 36.9 us
  local copies, waits for them, and re-layouts: 6.42 us -> 40.2 us
  Pallas kernels: 0 us -> 32.7 us
  waiting for transfers between devices: 41.9 us -> 28.1 us
    dot_general x70 -> x3, matrix products: 141 us -> 5.17 us  [the longest x1 3.04 us: local(): lax.dot_general(flat.reshape(-1, members), onehot, (((0,), (0,)), ((), ()...]
    all_gather x3 -> x0, blocking collectives: 74 us -> none  [the longest x2 38.5 us: in_one_piece(): filled, at, outs = (lax.all_gather(both, axis, axis=dim, tiled=True), 0, [])]
    psum x8 -> x0, blocking collectives: 50.6 us -> none  [over_axes(): shard = lax.psum(shard, axis)]
    pallas_call x0 -> x3, Pallas kernels: none -> 32.7 us  [the longest x1 19.5 us: build_kernel(): pl.pallas_call(kernel_body, out_shape=[pltpu.VMEM((rows, columns), jnp.bf...]
    unnamed x18 -> x28, local copies, waits for them, and re-layouts: 3.45 us -> 34.7 us
    all_to_all x1 -> x3, blocking collectives: 11 us -> 36.9 us  [the longest x2 25.8 us: spread(): return lax.all_to_all(copies, axes, split_axis=0, concat_axis=0, tiled=True)]
    all_to_all x5, waiting for transfers between devices: 41.9 us -> 28.1 us  [the longest x1 12 us: local(): lax.all_to_all(message, ALL, split_axis=0, concat_axis=0, tiled=True)]
  transfers between devices with their start and end apart: 5 -> 5, of which waited for: 4 -> 4; matrix products, arithmetic and copies ran while one was open for 2% -> 3% of each run, Pallas kernels for 0% -> 11%
where the time goes in v1:
time: 177 us; the launch traced here: 176 us
  local copies, waits for them, and re-layouts  40.2 us (23%)
  blocking collectives  36.9 us (21%)
  Pallas kernels  32.7 us (18%)
  waiting for transfers between devices  28.1 us (16%)
  starting transfers between devices  27.3 us (15%)
  matrix products  5.17 us (3%)
  other arithmetic  4.69 us (3%)
    unnamed x28, local copies, waits for them, and re-layouts  34.7 us
    all_to_all x2, blocking collectives, spread(): return lax.all_to_all(copies, axes, split_axis=0, concat_axis=0, tiled=True)  25.8 us
    pallas_call x1, Pallas kernels, build_kernel(): pl.pallas_call(kernel_body, out_shape=[pltpu.VMEM((rows, columns), jnp.bf...  19.5 us
    pallas_call x2, Pallas kernels, kernel_product(): pl.pallas_call(product_body, out_shape=jax.ShapeDtypeStruct((columns // w...  13.2 us
    all_to_all x3, starting transfers between devices, spread(): return lax.all_to_all(copies, axes, split_axis=0, concat_axis=0, tiled=True)  12.3 us
    all_to_all x1, waiting for transfers between devices, local(): lax.all_to_all(message, ALL, split_axis=0, concat_axis=0, tiled=True)  12 us
    all_to_all x1, starting transfers between devices, local(): lax.all_to_all(message, ALL, split_axis=0, concat_axis=0, tiled=True)  11.5 us
    all_to_all x1, blocking collectives, operate(): lax.all_to_all(partial_value, COL, split_axis=0, concat_axis=0, tiled=True)  11 us
  transfers between devices with their start and end apart: 5, of which 4 were waited for; matrix products, arithmetic and copies ran while one was open for 3% of the time, Pallas kernels for 11%

profile of v1, /device:TPU:1, one launch (start us, length us, event | category | flops | bytes accessed | tf_op | source)
XLA Modules:
  0.0 176.0 jit_solution(9044494788328166039)
XLA Ops:
  0.7 1.0 convert_reduce_fusion
  1.6 0.7 multiply_add_fusion.3
  2.3 0.7 convert_element_type.22
  3.0 0.8 fusion.8
  3.8 1.7 convolution_multiply_fusion
  6.7 0.9 copy.62
  7.6 11.5 %all-to-all-start = ((f32[128,1,544]{2,1,0:T(1,128)}), f32[128,1,544]{2,1,0:T(1,128)S(1)}, u32[]{:S(2)}, u32[]{:S(2)}) async-start(f32[128,1,544]{2,1,0:T(1,128)} %copy.62), calls=%async_computation | async-start | bytes 655360 | tf_op jit(solution)/shard_map/all_to_all | solution.py:168
  19.2 12.0 %all-to-all-done = f32[128,1,544]{2,1,0:T(1,128)S(1)} async-done(((f32[128,1,544]{2,1,0:T(1,128)}), f32[128,1,544]{2,1,0:T(1,128)S(1)}, u32[]{:S(2)}, u32[]{:S(2)}) %all-to-all-start) | async-done | bytes 278560 | tf_op jit(solution)/shard_map/all_to_all | solution.py:168
  31.8 3.8 %all-to-all-start.2 = ((f32[8,16,256]{2,1,0:T(8,128)}), f32[8,16,256]{2,1,0:T(8,128)S(1)}, u32[]{:S(2)}, u32[]{:S(2)}) async-start(f32[8,16,256]{2,1,0:T(8,128)} %broadcast_in_dim.18), calls=%async_computation.2 | async-start | bytes 262144 | tf_op jit(solution)/shard_map/all_to_all | solution.py:28
  36.1 0.7 eq.50
  36.8 0.7 reshape_reshape.3
  37.5 3.4 %all-to-all-done.2.zj_ref = f32[8,16,256]{2,1,0:T(8,128)S(1)} async-done(((f32[8,16,256]{2,1,0:T(8,128)}), f32[8,16,256]{2,1,0:T(8,128)S(1)}, u32[]{:S(2)}, u32[]{:S(2)}) %all-to-all-start.2) | async-done | bytes 131104 | tf_op jit(solution)/shard_map/all_to_all | solution.py:28
  40.9 0.7 broadcast_in_dim.19
  41.6 3.5 %all-to-all-start.3 = ((f32[16,16,256]{2,1,0:T(8,128)}), f32[16,16,256]{2,1,0:T(8,128)S(1)}, u32[]{:S(2)}, u32[]{:S(2)}) async-start(f32[16,16,256]{2,1,0:T(8,128)} %broadcast_in_dim.19), calls=%async_computation.3 | async-start | bytes 524288 | tf_op jit(solution)/shard_map/all_to_all | solution.py:28
  45.1 3.0 %fusion = f32[16,256]{1,0:T(8,128)S(1)} fusion(f32[4096,16]{1,0:T(8,128)S(1)} %reshape_reshape.3, s32[4096]{0:T(1024)} %eq.50), kind=kOutput, calls=%fused_computation.1 | convolution fusion | flops 202375168 | bytes 294912 | tf_op jit(solution)/shard_map/dot_general | solution.py:177
  48.2 4.8 %all-to-all-done.3.zi_ref = f32[16,16,256]{2,1,0:T(8,128)S(1)} async-done(((f32[16,16,256]{2,1,0:T(8,128)}), f32[16,16,256]{2,1,0:T(8,128)S(1)}, u32[]{:S(2)}, u32[]{:S(2)}) %all-to-all-start.3) | async-done | bytes 262176 | tf_op jit(solution)/shard_map/all_to_all | solution.py:28
  53.7 5.0 %all-to-all-start.1 = ((f32[8,16,256]{2,1,0:T(8,128)}), f32[8,16,256]{2,1,0:T(8,128)S(1)}, u32[]{:S(2)}, u32[]{:S(2)}) async-start(f32[8,16,256]{2,1,0:T(8,128)} %broadcast_in_dim.17), calls=%async_computation.1 | async-start | bytes 262144 | tf_op jit(solution)/shard_map/all_to_all | solution.py:28
  58.7 19.5 %matern.1 = (bf16[2048,4096]{1,0:T(8,128)(2,1)S(1)}, bf16[2048,4096]{1,0:T(8,128)(2,1)S(1)}) custom-call(f32[8,16,256]{2,1,0:T(8,128)S(1)} %all-to-all-done.2.zj_ref, f32[16,16,256]{2,1,0:T(8,128)S(1)} %all-to-all-done.3.zi_ref), custom_call_target="tpu_custom_call" | custom-call | flops 335544320 | bytes 33554432 | tf_op jit(solution)/shard_map/matern/pallas_call | solution.py:87
  78.2 5.7 %copy-done.1 = bf16[2048,4096]{1,0:T(8,128)(2,1)} copy-done((bf16[2048,4096]{1,0:T(8,128)(2,1)}, bf16[2048,4096]{1,0:T(8,128)(2,1)S(1)}, u32[]{:S(2)}) %copy-start.1) | copy-done | bytes 16777240
  83.9 5.7 %copy-done.4 = bf16[2048,4096]{1,0:T(8,128)(2,1)} copy-done((bf16[2048,4096]{1,0:T(8,128)(2,1)}, bf16[2048,4096]{1,0:T(8,128)(2,1)S(1)}, u32[]{:S(2)}) %copy-start.4) | copy-done | bytes 16777240
  89.6 5.8 %copy-done.2 = bf16[2048,4096]{1,0:T(8,128)(2,1)S(1)} copy-done((bf16[2048,4096]{1,0:T(8,128)(2,1)S(1)}, bf16[2048,4096]{1,0:T(8,128)(2,1)}, u32[]{:S(2)}) %copy-start.2) | copy-done | bytes 16777240
  95.4 5.8 %copy-done.5 = bf16[2048,4096]{1,0:T(8,128)(2,1)S(1)} copy-done((bf16[2048,4096]{1,0:T(8,128)(2,1)S(1)}, bf16[2048,4096]{1,0:T(8,128)(2,1)}, u32[]{:S(2)}) %copy-start.5) | copy-done | bytes 16777240
  101.2 6.2 %product.2 = f32[16,16,256]{2,1,0:T(8,128)S(1)} custom-call(f32[8,16,256]{2,1,0:T(8,128)S(1)} %all-to-all-done.1.v_ref, bf16[2048,4096]{1,0:T(8,128)(2,1)S(1)} %copy-done.2, bf16[2048,4096]{1,0:T(8,128)(2,1)S(1)} %copy-done.5), custom_call_target="tpu_custom_call" | custom-call | flops 1073741824 | bytes 33554432 | tf_op jit(solution)/shard_map/product/pallas_call | solution.py:127
  107.4 11.0 %all_to_all.47 = f32[16,16,256]{2,1,0:T(8,128)S(1)} all-to-all(f32[16,16,256]{2,1,0:T(8,128)S(1)} %product.2), channel_id=1, replica_groups=mesh['row_0'=4,'row_1'=2,'col_0'=4,'col_1'=4] {'col_0','col_1'}, dimensions={0} | all-to-all | bytes 524288 | tf_op jit(solution)/shard_map/all_to_all | solution.py:187
  118.6 10.7 %all_to_all.48.v_ref = f32[8,16,256]{2,1,0:T(8,128)S(1)} all-to-all(f32[8,16,256]{2,1,0:T(8,128)S(1)} %broadcast_in_dim.22), channel_id=1, replica_groups=mesh['row_0'=4,'row_1'=2,'col_0'=4,'col_1'=4] {'row_0','row_1'}, dimensions={0} | all-to-all | bytes 262144 | tf_op jit(solution)/shard_map/all_to_all | solution.py:28
  129.3 5.8 %copy-done.3 = bf16[2048,4096]{1,0:T(8,128)(2,1)S(1)} copy-done((bf16[2048,4096]{1,0:T(8,128)(2,1)S(1)}, bf16[2048,4096]{1,0:T(8,128)(2,1)}, u32[]{:S(2)}) %copy-start.3) | copy-done | bytes 16777240
  135.1 5.8 %copy-done.6 = bf16[2048,4096]{1,0:T(8,128)(2,1)S(1)} copy-done((bf16[2048,4096]{1,0:T(8,128)(2,1)S(1)}, bf16[2048,4096]{1,0:T(8,128)(2,1)}, u32[]{:S(2)}) %copy-start.6) | copy-done | bytes 16777240
  140.9 6.9 %product.3 = f32[16,16,256]{2,1,0:T(8,128)} custom-call(f32[8,16,256]{2,1,0:T(8,128)S(1)} %all_to_all.48.v_ref, bf16[2048,4096]{1,0:T(8,128)(2,1)S(1)} %copy-done.3, bf16[2048,4096]{1,0:T(8,128)(2,1)S(1)} %copy-done.6), custom_call_target="tpu_custom_call" | custom-call | flops 1073741824 | bytes 33554432 | tf_op jit(solution)/shard_map/product/pallas_call | solution.py:127
  147.8 3.5 %all-to-all-start.6 = ((f32[16,16,256]{2,1,0:T(8,128)}), f32[16,16,256]{2,1,0:T(8,128)S(1)}, u32[]{:S(2)}, u32[]{:S(2)}) async-start(f32[16,16,256]{2,1,0:T(8,128)} %product.3), calls=%async_computation.6 | async-start | bytes 524288 | tf_op jit(solution)/shard_map/all_to_all | solution.py:187
  151.4 7.8 %all-to-all-done.6 = f32[16,16,256]{2,1,0:T(8,128)S(1)} async-done(((f32[16,16,256]{2,1,0:T(8,128)}), f32[16,16,256]{2,1,0:T(8,128)S(1)}, u32[]{:S(2)}, u32[]{:S(2)}) %all-to-all-start.6) | async-done | bytes 262176 | tf_op jit(solution)/shard_map/all_to_all | solution.py:187
  159.8 15.1 %all_to_all.49 = f32[128,1,256]{2,1,0:T(1,128)S(1)} all-to-all(f32[128,1,256]{2,1,0:T(1,128)S(1)} %broadcast_in_dim.24), channel_id=1, replica_groups=mesh['row_0'=4,'row_1'=2,'col_0'=4,'col_1'=4] {'row_0','row_1','col_0','..., dimensions={0} | all-to-all | bytes 262144 | tf_op jit(solution)/shard_map/all_to_all | solution.py:28
  175.3 0.7 multiply_subtract_fusion
  (53 shorter events, 4.0 us)
Async XLA Ops:
  0.6 3.2 %copy-start = (bf16[256,16,128]{2,1,0:T(8,128)(2,1)S(1)}, bf16[256,16,128]{2,1,0:T(8,128)(2,1)}, u32[]{:S(2)}) copy-start(bf16[256,16,128]{2,1,0:T(8,128)(2,1)} %param.11) | copy-start | bytes 3145732
  0.6 18.5 %copy-start.9 = (f32[16]{0:T(128)S(1)}, f32[16]{0:T(128)}, u32[]{:S(2)}) copy-start(f32[16]{0:T(128)} %param.9) | copy-start | bytes 196
  0.7 18.5 %copy-start.7 = (f32[16,256]{1,0:T(8,128)S(1)}, f32[16,256]{1,0:T(8,128)}, u32[]{:S(2)}) copy-start(f32[16,256]{1,0:T(8,128)} %param.8) | copy-start | bytes 49156
  7.6 23.6 %all-to-all-start = ((f32[128,1,544]{2,1,0:T(1,128)}), f32[128,1,544]{2,1,0:T(1,128)S(1)}, u32[]{:S(2)}, u32[]{:S(2)}) async-start(f32[128,1,544]{2,1,0:T(1,128)} %copy.62), calls=%async_computation | async-start | bytes 655360 | tf_op jit(solution)/shard_map/all_to_all | solution.py:168
  31.8 9.1 %all-to-all-start.2 = ((f32[8,16,256]{2,1,0:T(8,128)}), f32[8,16,256]{2,1,0:T(8,128)S(1)}, u32[]{:S(2)}, u32[]{:S(2)}) async-start(f32[8,16,256]{2,1,0:T(8,128)} %broadcast_in_dim.18), calls=%async_computation.2 | async-start | bytes 262144 | tf_op jit(solution)/shard_map/all_to_all | solution.py:28
  41.6 11.4 %all-to-all-start.3 = ((f32[16,16,256]{2,1,0:T(8,128)}), f32[16,16,256]{2,1,0:T(8,128)S(1)}, u32[]{:S(2)}, u32[]{:S(2)}) async-start(f32[16,16,256]{2,1,0:T(8,128)} %broadcast_in_dim.19), calls=%async_computation.3 | async-start | bytes 524288 | tf_op jit(solution)/shard_map/all_to_all | solution.py:28
  53.7 36.0 %all-to-all-start.1 = ((f32[8,16,256]{2,1,0:T(8,128)}), f32[8,16,256]{2,1,0:T(8,128)S(1)}, u32[]{:S(2)}, u32[]{:S(2)}) async-start(f32[8,16,256]{2,1,0:T(8,128)} %broadcast_in_dim.17), calls=%async_computation.1 | async-start | bytes 262144 | tf_op jit(solution)/shard_map/all_to_all | solution.py:28
  78.2 5.7 %copy-start.1 = (bf16[2048,4096]{1,0:T(8,128)(2,1)}, bf16[2048,4096]{1,0:T(8,128)(2,1)S(1)}, u32[]{:S(2)}) copy-start(bf16[2048,4096]{1,0:T(8,128)(2,1)S(1)} %get-tuple-element.4.high_ref) | copy-start | bytes 50331652
  83.9 5.7 %copy-start.4 = (bf16[2048,4096]{1,0:T(8,128)(2,1)}, bf16[2048,4096]{1,0:T(8,128)(2,1)S(1)}, u32[]{:S(2)}) copy-start(bf16[2048,4096]{1,0:T(8,128)(2,1)S(1)} %get-tuple-element.5.low_ref) | copy-start | bytes 50331652
  89.6 5.8 %copy-start.2 = (bf16[2048,4096]{1,0:T(8,128)(2,1)S(1)}, bf16[2048,4096]{1,0:T(8,128)(2,1)}, u32[]{:S(2)}) copy-start(bf16[2048,4096]{1,0:T(8,128)(2,1)} %copy-done.1) | copy-start | bytes 50331652
  95.4 5.8 %copy-start.5 = (bf16[2048,4096]{1,0:T(8,128)(2,1)S(1)}, bf16[2048,4096]{1,0:T(8,128)(2,1)}, u32[]{:S(2)}) copy-start(bf16[2048,4096]{1,0:T(8,128)(2,1)} %copy-done.4) | copy-start | bytes 50331652
  101.2 17.3 %copy-start.8 = (f32[256]{0:T(256)S(1)}, f32[256]{0:T(256)}, u32[]{:S(2)}) copy-start(f32[256]{0:T(256)} %param.10) | copy-start | bytes 3076
  129.3 5.8 %copy-start.3 = (bf16[2048,4096]{1,0:T(8,128)(2,1)S(1)}, bf16[2048,4096]{1,0:T(8,128)(2,1)}, u32[]{:S(2)}) copy-start(bf16[2048,4096]{1,0:T(8,128)(2,1)} %copy-done.1) | copy-start | bytes 50331652
  135.1 5.8 %copy-start.6 = (bf16[2048,4096]{1,0:T(8,128)(2,1)S(1)}, bf16[2048,4096]{1,0:T(8,128)(2,1)}, u32[]{:S(2)}) copy-start(bf16[2048,4096]{1,0:T(8,128)(2,1)} %copy-done.4) | copy-start | bytes 50331652
  147.8 11.4 %all-to-all-start.6 = ((f32[16,16,256]{2,1,0:T(8,128)}), f32[16,16,256]{2,1,0:T(8,128)S(1)}, u32[]{:S(2)}, u32[]{:S(2)}) async-start(f32[16,16,256]{2,1,0:T(8,128)} %product.3), calls=%async_computation.6 | async-start | bytes 524288 | tf_op jit(solution)/shard_map/all_to_all | solution.py:187

commit v2 on v1

--- a/solution.py
+++ b/solution.py
@@ -138,6 +138,130 @@
     )(v, high, low)
 
 
+def total_body(shares_ref, v_ref, nugget_ref, out_ref, copies_ref):
+    total = nugget_ref[...] * v_ref[...]
+    for c in range(shares_ref.shape[0]):
+        total += shares_ref[c]
+    out_ref[...] = total
+    for r in range(copies_ref.shape[0]):
+        copies_ref[r] = total
+
+
+def total_of(shares, v, nugget, copies):
+    return pl.pallas_call(
+        total_body,
+        out_shape=[
+            jax.ShapeDtypeStruct(v.shape, jnp.float32),
+            jax.ShapeDtypeStruct((copies,) + v.shape, jnp.float32),
+        ],
+        in_specs=[pl.BlockSpec(memory_space=VMEM)] * 3,
+        out_specs=[pl.BlockSpec(memory_space=VMEM)] * 2,
+        compiler_params=pltpu.CompilerParams(vmem_limit_bytes=4 * MIB),
+        name="total",
+    )(shares, v, nugget)
+
+
+def guess_of(norm, energy):
+    usable = energy > 0.5 * norm
+    return jnp.where(usable, norm / jnp.where(usable, energy, 1.0), 0.0)
+
+
+def close_body(shares_ref, rhs_ref, first_ref, nugget_ref, second_ref, sums_ref):
+    rhs, first = rhs_ref[...], first_ref[...]
+    second = nugget_ref[...] * first
+    for c in range(shares_ref.shape[0]):
+        second += shares_ref[c]
+    second_ref[...] = second
+
+    def dot(a, b):
+        return jnp.sum(a * b, axis=1, keepdims=True)
+
+    norm, energy = dot(rhs, rhs), dot(rhs, first)
+    guess = guess_of(norm, energy)
+    resid = rhs - guess * first
+    along = first - guess * second
+    sums = [
+        norm,
+        energy,
+        dot(resid, resid),
+        dot(resid, first),
+        dot(first, first),
+        dot(resid, along),
+        dot(resid, second) + dot(first, along),
+        dot(first, second),
+    ]
+    members = rhs.shape[0]
+    shape = (members, len(sums) * members)
+    row = lax.broadcasted_iota(jnp.int32, shape, 0)
+    lane = lax.broadcasted_iota(jnp.int32, shape, 1)
+    spaced = jnp.zeros(shape, jnp.float32)
+    for at, column in enumerate(sums):
+        here = lane == row + at * members
+        spaced += jnp.where(here, jnp.broadcast_to(column, shape), 0.0)
+    sums_ref[...] = jnp.sum(spaced, axis=0, keepdims=True)
+
+
+def close(shares, rhs, first, nugget):
+    members = rhs.shape[0]
+    return pl.pallas_call(
+        close_body,
+        out_shape=[
+            jax.ShapeDtypeStruct(rhs.shape, jnp.float32),
+            jax.ShapeDtypeStruct((1, 8 * members), jnp.float32),
+        ],
+        in_specs=[pl.BlockSpec(memory_space=VMEM)] * 4,
+        out_specs=[pl.BlockSpec(memory_space=VMEM)] * 2,
+        compiler_params=pltpu.CompilerParams(vmem_limit_bytes=4 * MIB),
+        name="close",
+    )(shares, rhs, first, nugget)
+
+
+def finish_body(sums_ref, rhs_ref, first_ref, second_ref, solved_ref, residual_ref):
+    rhs, first, second = rhs_ref[...], first_ref[...], second_ref[...]
+    members = rhs.shape[0]
+    norm, energy, rr, rf, ff, ra, rs, fs = (
+        sums_ref[:, q * members : (q + 1) * members] for q in range(8)
+    )
+
+    def over(x):
+        return jnp.sum(x, axis=0, keepdims=True)
+
+    norm0 = over(norm)
+    alpha0 = norm0 / over(energy)
+    shift = alpha0 - guess_of(norm, energy)
+    norm1 = over(rr - shift * (2.0 * rf - shift * ff))
+    energy1 = over(ra - shift * (rs - shift * fs))
+    ratio = norm1 / norm0
+    alpha1 = norm1 / (energy1 - ratio * norm1 / alpha0)
+    shape = (members, members)
+    same = lax.broadcasted_iota(jnp.int32, shape, 0) == lax.broadcasted_iota(jnp.int32, shape, 1)
+
+    def column(x):
+        return jnp.sum(jnp.where(same, jnp.broadcast_to(x, shape), 0.0), axis=1, keepdims=True)
+
+    alpha0, alpha1, ratio = column(alpha0), column(alpha1), column(ratio)
+    residual = rhs - alpha0 * first
+    direction = residual + ratio * rhs
+    along = (first - alpha0 * second) + ratio * first
+    solved_ref[...] = alpha0 * rhs + alpha1 * direction
+    residual_ref[...] = residual - alpha1 * along
+
+
+def finish(sums, rhs, first, second):
+    return pl.pallas_call(
+        finish_body,
+        out_shape=[jax.ShapeDtypeStruct(rhs.shape, jnp.float32)] * 2,
+        in_specs=[pl.BlockSpec(memory_space=VMEM)] * 4,
+        out_specs=[pl.BlockSpec(memory_space=VMEM)] * 2,
+        compiler_params=pltpu.CompilerParams(vmem_limit_bytes=4 * MIB),
+        name="finish",
+    )(sums, rhs, first, second)
+
+
+def exchange(pieces, axes):
+    return lax.all_to_all(pieces, axes, split_axis=0, concat_axis=0, tiled=True)
+
+
 def local(
     covariates, lengthscale, nugget, patch_values, patch_weights, block_index, slot_count, owner
 ):
@@ -146,6 +270,9 @@
     slots = patch_weights.shape[1]
     stations = nugget.shape[0]
     capacity = max(2, 2 * held // devices)
+
+    scaled_cov = covariates / lengthscale[:, None]
+    column_cov, row_cov = spread(scaled_cov, ROW), spread(scaled_cov, COL)
 
     terms = jnp.einsum(
         "psc,pmc->psm", patch_weights, patch_values, preferred_element_type=jnp.float32
@@ -167,9 +294,6 @@
     )
     message = lax.all_to_all(message, ALL, split_axis=0, concat_axis=0, tiled=True)
 
-    scaled_cov = covariates / lengthscale[:, None]
-    high, low = build_kernel(spread(scaled_cov, ROW), spread(scaled_cov, COL))
-
     entries = capacity * slots
     flat = message[:, : entries * members].reshape(devices, entries, members)
     index = message[:, entries * members :].astype(jnp.int32)
@@ -182,48 +306,17 @@
         preferred_element_type=jnp.float32,
     )
 
-    def operate(v):
-        partial_value = kernel_product(spread(v, ROW), high, low)
-        shares = lax.all_to_all(partial_value, COL, split_axis=0, concat_axis=0, tiled=True)
-        return jnp.sum(shares, axis=0) + nugget[None, :] * v
-
-    first = operate(rhs)
-    second = operate(first)
-
-    def dot(a, b):
-        return jnp.sum(a * b, axis=1)
-
-    norm, energy = dot(rhs, rhs), dot(rhs, first)
-    guess = jnp.where(energy > 0.5 * norm, norm / jnp.maximum(energy, TINY), 0.0)
-    resid = rhs - guess[:, None] * first
-    along = first - guess[:, None] * second
-    sums = jnp.stack(
-        [
-            norm,
-            energy,
-            guess,
-            dot(resid, resid),
-            dot(resid, first),
-            dot(first, first),
-            dot(resid, along),
-            dot(resid, second) + dot(first, along),
-            dot(first, second),
-        ]
-    ).reshape(1, -1)
-    sums = jnp.pad(sums, ((0, 0), (0, -sums.shape[1] % 128)))
-    sums = spread(sums, ALL)[:, 0, : 9 * members].reshape(devices, 9, members)
-    norm0 = jnp.sum(sums[:, 0], axis=0)
-    alpha0 = norm0 / jnp.sum(sums[:, 1], axis=0)
-    shift = alpha0[None, :] - sums[:, 2]
-    norm1 = jnp.sum(sums[:, 3] - shift * (2.0 * sums[:, 4] - shift * sums[:, 5]), axis=0)
-    energy1 = jnp.sum(sums[:, 6] - shift * (sums[:, 7] - shift * sums[:, 8]), axis=0)
-    ratio = norm1 / norm0
-    alpha1 = norm1 / (energy1 - ratio * norm1 / alpha0)
-    residual = rhs - alpha0[:, None] * first
-    direction = residual + ratio[:, None] * rhs
-    along = (first - alpha0[:, None] * second) + ratio[:, None] * first
-    solved = alpha0[:, None] * rhs + alpha1[:, None] * direction
-    return (solved, residual - alpha1[:, None] * along)
+    gathered = spread(rhs, ROW)
+    gathered, column_cov, row_cov = lax.optimization_barrier((gathered, column_cov, row_cov))
+    high, low = build_kernel(column_cov, row_cov)
+    nugget = nugget[None, :]
+    shares = exchange(kernel_product(gathered, high, low), COL)
+    first, copies = total_of(shares, rhs, nugget, lax.axis_size(ROW))
+    shares = exchange(kernel_product(exchange(copies, ROW), high, low), COL)
+    second, sums = close(shares, rhs, first, nugget)
+    copies = jnp.broadcast_to(sums[None], (devices,) + sums.shape)
+    sums = exchange(copies, ALL).reshape(devices, sums.shape[1])
+    return finish(sums, rhs, first, second)
 
 
 def solution(mesh):

time: 177 us -> 142 us (0.80)
  local copies, waits for them, and re-layouts: 40.2 us -> 4.85 us
  blocking collectives: 36.9 us -> 54.7 us
  starting transfers between devices: 27.3 us -> 18.8 us
  waiting for transfers between devices: 28.1 us -> 20.2 us
    unnamed x28 -> x15, local copies, waits for them, and re-layouts: 34.7 us -> 0.06 us
    all_to_all x1 -> x4, blocking collectives: 11 us -> 45.4 us  [exchange(): return lax.all_to_all(pieces, axes, split_axis=0, concat_axis=0, tiled=True)]
    all_to_all x2 -> x1, blocking collectives: 25.8 us -> 9.35 us  [spread(): return lax.all_to_all(copies, axes, split_axis=0, concat_axis=0, tiled=True)]
    all_to_all x1 -> x0, waiting for transfers between devices: 7.85 us -> none  [operate(): lax.all_to_all(partial_value, COL, split_axis=0, concat_axis=0, tiled=True)]
    all_to_all x3 -> x2, starting transfers between devices: 12.3 us -> 7.33 us  [spread(): return lax.all_to_all(copies, axes, split_axis=0, concat_axis=0, tiled=True)]
    all_to_all x1 -> x0, starting transfers between devices: 3.53 us -> none  [operate(): lax.all_to_all(partial_value, COL, split_axis=0, concat_axis=0, tiled=True)]
    all_to_all x3 -> x2, waiting for transfers between devices: 8.26 us -> 8.25 us  [spread(): return lax.all_to_all(copies, axes, split_axis=0, concat_axis=0, tiled=True)]
  transfers between devices with their start and end apart: 5 -> 3, of which waited for: 4 -> 3; matrix products, arithmetic and copies ran while one was open for 3% -> 3% of each run, Pallas kernels for 11% -> 0%
where the time goes in v2:
time: 142 us; the launch traced here: 141 us
  blocking collectives  54.7 us (39%)
  Pallas kernels  33.6 us (24%)
  waiting for transfers between devices  20.2 us (14%)
  starting transfers between devices  18.8 us (13%)
  matrix products  5.17 us (4%)
  local copies, waits for them, and re-layouts  4.85 us (3%)
  other arithmetic  3.2 us (2%)
    all_to_all x4, blocking collectives, exchange(): return lax.all_to_all(pieces, axes, split_axis=0, concat_axis=0, tiled=True)  45.4 us
    pallas_call x1, Pallas kernels, build_kernel(): pl.pallas_call(kernel_body, out_shape=[pltpu.VMEM((rows, columns), jnp.bf...  19.5 us
    pallas_call x2, Pallas kernels, kernel_product(): pl.pallas_call(product_body, out_shape=jax.ShapeDtypeStruct((columns // w...  12.5 us
    all_to_all x1, waiting for transfers between devices, local(): lax.all_to_all(message, ALL, split_axis=0, concat_axis=0, tiled=True)  12 us
    all_to_all x1, starting transfers between devices, local(): lax.all_to_all(message, ALL, split_axis=0, concat_axis=0, tiled=True)  11.5 us
    all_to_all x1, blocking collectives, spread(): return lax.all_to_all(copies, axes, split_axis=0, concat_axis=0, tiled=True)  9.35 us
    all_to_all x2, waiting for transfers between devices, spread(): return lax.all_to_all(copies, axes, split_axis=0, concat_axis=0, tiled=True)  8.25 us
    all_to_all x2, starting transfers between devices, spread(): return lax.all_to_all(copies, axes, split_axis=0, concat_axis=0, tiled=True)  7.33 us
  transfers between devices with their start and end apart: 3, of which 3 were waited for; matrix products, arithmetic and copies ran while one was open for 3% of the time, Pallas kernels for 0%

profile of v2, /device:TPU:1, one launch (start us, length us, event | category | flops | bytes accessed | tf_op | source)
XLA Modules:
  0.0 141.5 jit_solution(4988738976347290569)
XLA Ops:
  0.7 1.0 convert_reduce_fusion
  1.6 0.7 multiply_add_fusion
  2.3 0.7 convert_element_type.20
  3.0 0.8 fusion.8
  3.8 1.7 %convolution_multiply_fusion = f32[256,8,16]{2,1,0:T(8,128)S(1)} fusion(bf16[256,8,128]{2,1,0:T(8,128)(2,1)} %param.12, bf16[256,16,128]{2,1,0:T(8,128)(2,1)S(1)} %copy-done, f32[256,8]{1,0:T(8,128)S(1)} %fusion.8), kind=kOutput, calls=%fused_computation.3 | convolution fusion | flops 8421376 | bytes 1712128 | tf_op jit(solution)/shard_map/psc,pmc->psm/dot_general | solution.py:277
  5.5 0.4 copy.45
  5.9 0.4 fusion.2
  6.4 0.2 fusion.11
  6.7 0.9 copy.54
  7.6 11.5 %all-to-all-start = ((f32[128,1,544]{2,1,0:T(1,128)}), f32[128,1,544]{2,1,0:T(1,128)S(1)}, u32[]{:S(2)}, u32[]{:S(2)}) async-start(f32[128,1,544]{2,1,0:T(1,128)} %copy.54), calls=%async_computation | async-start | bytes 655360 | tf_op jit(solution)/shard_map/all_to_all | solution.py:295
  19.2 12.0 %all-to-all-done = f32[128,1,544]{2,1,0:T(1,128)S(1)} async-done(((f32[128,1,544]{2,1,0:T(1,128)}), f32[128,1,544]{2,1,0:T(1,128)S(1)}, u32[]{:S(2)}, u32[]{:S(2)}) %all-to-all-start) | async-done | bytes 278560 | tf_op jit(solution)/shard_map/all_to_all | solution.py:295
  31.2 0.7 broadcast_in_dim.13
  31.8 3.8 %all-to-all-start.2 = ((f32[8,16,256]{2,1,0:T(8,128)}), f32[8,16,256]{2,1,0:T(8,128)S(1)}, u32[]{:S(2)}, u32[]{:S(2)}) async-start(f32[8,16,256]{2,1,0:T(8,128)} %broadcast_in_dim.13), calls=%async_computation.2 | async-start | bytes 262144 | tf_op jit(solution)/shard_map/all_to_all | solution.py:28
  35.6 0.2 copy.55
  35.8 0.1 copy.56
  36.1 0.7 eq.50
  36.8 0.7 reshape_reshape.3
  37.5 3.4 %all-to-all-done.2.zj_ref = f32[8,16,256]{2,1,0:T(8,128)S(1)} async-done(((f32[8,16,256]{2,1,0:T(8,128)}), f32[8,16,256]{2,1,0:T(8,128)S(1)}, u32[]{:S(2)}, u32[]{:S(2)}) %all-to-all-start.2) | async-done | bytes 131104 | tf_op jit(solution)/shard_map/all_to_all | solution.py:28
  40.9 0.7 broadcast_in_dim.14
  41.6 3.5 %all-to-all-start.3 = ((f32[16,16,256]{2,1,0:T(8,128)}), f32[16,16,256]{2,1,0:T(8,128)S(1)}, u32[]{:S(2)}, u32[]{:S(2)}) async-start(f32[16,16,256]{2,1,0:T(8,128)} %broadcast_in_dim.14), calls=%async_computation.3 | async-start | bytes 524288 | tf_op jit(solution)/shard_map/all_to_all | solution.py:28
  45.2 3.0 %fusion.v_ref.rhs_ref = f32[16,256]{1,0:T(8,128)S(1)} fusion(f32[4096,16]{1,0:T(8,128)S(1)} %reshape_reshape.3, s32[4096]{0:T(1024)} %eq.50), kind=kOutput, calls=%fused_computation.1 | convolution fusion | flops 202375168 | bytes 294912 | tf_op jit(solution)/shard_map/dot_general | solution.py:301
  48.2 4.8 %all-to-all-done.3.zi_ref = f32[16,16,256]{2,1,0:T(8,128)S(1)} async-done(((f32[16,16,256]{2,1,0:T(8,128)}), f32[16,16,256]{2,1,0:T(8,128)S(1)}, u32[]{:S(2)}, u32[]{:S(2)}) %all-to-all-start.3) | async-done | bytes 262176 | tf_op jit(solution)/shard_map/all_to_all | solution.py:28
  53.1 9.3 %all_to_all.47.v_ref = f32[8,16,256]{2,1,0:T(8,128)S(1)} all-to-all(f32[8,16,256]{2,1,0:T(8,128)S(1)} %broadcast_in_dim.12), channel_id=1, replica_groups=mesh['row_0'=4,'row_1'=2,'col_0'=4,'col_1'=4] {'row_0','row_1'}, dimensions={0} | all-to-all | bytes 262144 | tf_op jit(solution)/shard_map/all_to_all | solution.py:28
  62.4 19.5 %matern.1 = (bf16[2048,4096]{1,0:T(8,128)(2,1)S(1)}, bf16[2048,4096]{1,0:T(8,128)(2,1)S(1)}) custom-call(f32[8,16,256]{2,1,0:T(8,128)S(1)} %all-to-all-done.2.zj_ref, f32[16,16,256]{2,1,0:T(8,128)S(1)} %all-to-all-done.3.zi_ref), custom_call_target="tpu_custom_call" | custom-call | flops 335544320 | bytes 33554432 | tf_op jit(solution)/shard_map/matern/pallas_call | solution.py:87
  82.0 6.2 %product.2 = f32[16,16,256]{2,1,0:T(8,128)S(1)} custom-call(f32[8,16,256]{2,1,0:T(8,128)S(1)} %all_to_all.47.v_ref, bf16[2048,4096]{1,0:T(8,128)(2,1)S(1)} %get-tuple-element.14.high_ref, bf16[2048,4096]{1,0:T(8,128)(2,1)S(1)} %get-tuple-element.15.low_ref), custom_call_target="tpu_custom_call" | custom-call | flops 1073741824 | bytes 33554432 | tf_op jit(solution)/shard_map/product/pallas_call | solution.py:127
  88.2 10.2 %all_to_all.48.shares_ref = f32[16,16,256]{2,1,0:T(8,128)S(1)} all-to-all(f32[16,16,256]{2,1,0:T(8,128)S(1)} %product.2), channel_id=1, replica_groups=mesh['row_0'=4,'row_1'=2,'col_0'=4,'col_1'=4] {'col_0','col_1'}, dimensions={0} | all-to-all | bytes 524288 | tf_op jit(solution)/shard_map/all_to_all | solution.py:262
  98.5 9.9 %all_to_all.49.v_ref = f32[8,16,256]{2,1,0:T(8,128)S(1)} all-to-all(f32[8,16,256]{2,1,0:T(8,128)S(1)} %get-tuple-element.16), channel_id=1, replica_groups=mesh['row_0'=4,'row_1'=2,'col_0'=4,'col_1'=4] {'row_0','row_1'}, dimensions={0} | all-to-all | bytes 262144 | tf_op jit(solution)/shard_map/all_to_all | solution.py:262
  108.3 6.2 %product.3 = f32[16,16,256]{2,1,0:T(8,128)S(1)} custom-call(f32[8,16,256]{2,1,0:T(8,128)S(1)} %all_to_all.49.v_ref, bf16[2048,4096]{1,0:T(8,128)(2,1)S(1)} %get-tuple-element.14.high_ref, bf16[2048,4096]{1,0:T(8,128)(2,1)S(1)} %get-tuple-element.15.low_ref), custom_call_target="tpu_custom_call" | custom-call | flops 1073741824 | bytes 33554432 | tf_op jit(solution)/shard_map/product/pallas_call | solution.py:127
  114.6 10.2 %all_to_all.50.shares_ref = f32[16,16,256]{2,1,0:T(8,128)S(1)} all-to-all(f32[16,16,256]{2,1,0:T(8,128)S(1)} %product.3), channel_id=1, replica_groups=mesh['row_0'=4,'row_1'=2,'col_0'=4,'col_1'=4] {'col_0','col_1'}, dimensions={0} | all-to-all | bytes 524288 | tf_op jit(solution)/shard_map/all_to_all | solution.py:262
  124.8 0.2 close.1
  125.0 15.0 %all_to_all.51 = f32[128,1,128]{2,1,0:T(1,128)S(1)} all-to-all(f32[128,1,128]{2,1,0:T(1,128)S(1)} %broadcast_in_dim.17), channel_id=1, replica_groups=mesh['row_0'=4,'row_1'=2,'col_0'=4,'col_1'=4] {'row_0','row_1','col_0','..., dimensions={0} | all-to-all | bytes 131072 | tf_op jit(solution)/shard_map/all_to_all | solution.py:262
  140.1 1.4 %finish.1 = (f32[16,256]{1,0:T(8,128)}, f32[16,256]{1,0:T(8,128)}) custom-call(f32[128,128]{1,0:T(8,128)S(1)} %bitcast.36, f32[16,256]{1,0:T(8,128)S(1)} %fusion.v_ref.rhs_ref, f32[16,256]{1,0:T(8,128)S(1)} %get-tuple-element.17.first_ref, f32[16,256]{1,0:T(8,128)S(1)} %get-tuple-element.19.second_ref), custom_call_target="tpu_custom_call" | custom-call | tf_op jit(solution)/shard_map/finish/pallas_call | solution.py:251
  (25 shorter events, 0.4 us)
Async XLA Ops:
  0.6 3.2 %copy-start = (bf16[256,16,128]{2,1,0:T(8,128)(2,1)S(1)}, bf16[256,16,128]{2,1,0:T(8,128)(2,1)}, u32[]{:S(2)}) copy-start(bf16[256,16,128]{2,1,0:T(8,128)(2,1)} %param.11) | copy-start | bytes 3145732
  0.6 18.5 %copy-start.3 = (f32[16]{0:T(128)S(1)}, f32[16]{0:T(128)}, u32[]{:S(2)}) copy-start(f32[16]{0:T(128)} %param.9) | copy-start | bytes 196
  0.7 18.5 %copy-start.2 = (f32[16,256]{1,0:T(8,128)S(1)}, f32[16,256]{1,0:T(8,128)}, u32[]{:S(2)}) copy-start(f32[16,256]{1,0:T(8,128)} %param.8) | copy-start | bytes 49156
  7.6 23.6 %all-to-all-start = ((f32[128,1,544]{2,1,0:T(1,128)}), f32[128,1,544]{2,1,0:T(1,128)S(1)}, u32[]{:S(2)}, u32[]{:S(2)}) async-start(f32[128,1,544]{2,1,0:T(1,128)} %copy.54), calls=%async_computation | async-start | bytes 655360 | tf_op jit(solution)/shard_map/all_to_all | solution.py:295
  31.8 9.1 %all-to-all-start.2 = ((f32[8,16,256]{2,1,0:T(8,128)}), f32[8,16,256]{2,1,0:T(8,128)S(1)}, u32[]{:S(2)}, u32[]{:S(2)}) async-start(f32[8,16,256]{2,1,0:T(8,128)} %broadcast_in_dim.13), calls=%async_computation.2 | async-start | bytes 262144 | tf_op jit(solution)/shard_map/all_to_all | solution.py:28
  41.6 11.4 %all-to-all-start.3 = ((f32[16,16,256]{2,1,0:T(8,128)}), f32[16,16,256]{2,1,0:T(8,128)S(1)}, u32[]{:S(2)}, u32[]{:S(2)}) async-start(f32[16,16,256]{2,1,0:T(8,128)} %broadcast_in_dim.14), calls=%async_computation.3 | async-start | bytes 524288 | tf_op jit(solution)/shard_map/all_to_all | solution.py:28
  82.0 16.5 %copy-start.1 = (f32[256]{0:T(256)S(1)}, f32[256]{0:T(256)}, u32[]{:S(2)}) copy-start(f32[256]{0:T(256)} %param.10) | copy-start | bytes 3076

commit v3 on v2

--- a/solution.py
+++ b/solution.py
@@ -1,3 +1,4 @@
+import functools
 import math
 
 import jax
@@ -12,13 +13,13 @@
 COL = ("col_0", "col_1")
 ROW = ("row_0", "row_1")
 
-HIGH = lax.Precision.HIGHEST
 LN2 = math.log(2.0)
 SCALE = math.sqrt(5.0) / LN2
 FACTOR = LN2 * LN2 / 3.0
 LINEAR = 3.0 / LN2
 CONST = 3.0 / (LN2 * LN2)
 TINY = 1e-30
+TILE, TILES = 512, 4
 VMEM = pltpu.MemorySpace.VMEM
 MIB = 1 << 20
 
@@ -56,58 +57,103 @@
     return jnp.concatenate(parts + [rest, jnp.zeros_like(z)], axis=0)
 
 
-def kernel_body(zj_ref, zi_ref, high_ref, low_ref, fj_ref, fi_ref):
-    width = zj_ref.shape[2]
-    for r in range(zj_ref.shape[0]):
-        block = features(zj_ref[r] * SCALE, True)
-        fj_ref[r * width : (r + 1) * width, :] = jnp.transpose(block).astype(jnp.bfloat16)
+def value_of(squared):
+    squared = jnp.maximum(squared, TINY)
+    root = squared * lax.rsqrt(squared)
+    return (squared + (LINEAR * root + CONST)) * jnp.exp2(-root)
+
+
+def split_vector(v_ref, first, vv_ref):
+    width = v_ref.shape[2]
+    members = vv_ref.shape[0] // 2
+    for r in range(v_ref.shape[0]):
+        high, low = halves(v_ref[r, first : first + members])
+        columns = slice(r * width, (r + 1) * width)
+        vv_ref[:members, columns] = high.astype(jnp.bfloat16)
+        vv_ref[members:, columns] = low.astype(jnp.bfloat16)
+
+
+def build_body(
+    zv_ref, zi_ref, high_ref, low_ref, out_ref, fj_ref, fi_ref, vv_ref, acc_ref, ahead_ref
+):
+    feats, members, width = zi_ref.shape[1], vv_ref.shape[0] // 2, zi_ref.shape[2]
+    for r in range(zv_ref.shape[0]):
+        block = features(zv_ref[r, :feats] * SCALE, True)
+        fj_ref[r * width : (r + 1) * width, :] = jnp.transpose(block.astype(jnp.bfloat16))
     for c in range(zi_ref.shape[0]):
         block = features(zi_ref[c] * SCALE, False)
         fi_ref[:, c * width : (c + 1) * width] = block.astype(jnp.bfloat16)
-    tall, wide = 256, 1024
-    across = fi_ref.shape[1] // wide
-
-    @pl.loop(0, (fj_ref.shape[0] // tall) * across)
+    split_vector(zv_ref, feats, vv_ref)
+    acc_ref[...] = jnp.zeros_like(acc_ref)
+    tall, wide, tiles = width, TILE, TILES
+    across = fi_ref.shape[1] // (wide * tiles)
+    steps = across * (fj_ref.shape[0] // tall)
+
+    def place(step, tile):
+        rows = pl.ds(pl.multiple_of((step // across) * tall, tall), tall)
+        columns = ((step % across) * tiles + tile) * wide
+        return rows, pl.ds(pl.multiple_of(columns, wide), wide)
+
+    def squares(step, tile):
+        rows, columns = place(step, tile)
+        return jnp.dot(fj_ref[rows, :], fi_ref[:, columns], preferred_element_type=jnp.float32)
+
+    ahead_ref[...] = squares(0, 0)
+
+    @pl.loop(0, steps)
     def _(step):
-        rows = pl.ds(pl.multiple_of((step // across) * tall, tall), tall)
-        columns = pl.ds(pl.multiple_of((step % across) * wide, wide), wide)
-        squared = jnp.dot(
-            fj_ref[rows, :], fi_ref[:, columns], preferred_element_type=jnp.float32
-        )
-        squared = jnp.maximum(squared, TINY)
-        root = squared * lax.rsqrt(squared)
-        value = (squared + (LINEAR * root + CONST)) * jnp.exp2(-root)
-        high = value.astype(jnp.bfloat16)
-        high_ref[rows, columns] = high
-        low_ref[rows, columns] = (value - high.astype(jnp.float32)).astype(jnp.bfloat16)
-
-
-def build_kernel(zj, zi):
-    rows, columns = zj.shape[0] * zj.shape[2], zi.shape[0] * zi.shape[2]
-    return pl.pallas_call(
-        kernel_body,
-        out_shape=[pltpu.VMEM((rows, columns), jnp.bfloat16)] * 2,
+        squared = ahead_ref[...]
+        for tile in range(tiles):
+            if tile + 1 < tiles:
+                ahead = squares(step, tile + 1)
+            else:
+                ahead = squares(jnp.minimum(step + 1, steps - 1), 0)
+            rows, columns = place(step, tile)
+            value = value_of(squared)
+            high = value.astype(jnp.bfloat16)
+            low = (value - high.astype(jnp.float32)).astype(jnp.bfloat16)
+            high_ref[rows, columns] = high
+            low_ref[rows, columns] = low
+            vv = vv_ref[:, rows]
+            acc_ref[:, columns] += jnp.dot(
+                vv, high, preferred_element_type=jnp.float32
+            ) + jnp.dot(vv, low, preferred_element_type=jnp.float32)
+            squared = ahead
+        ahead_ref[...] = squared
+
+    for c in range(out_ref.shape[0]):
+        columns = slice(c * width, (c + 1) * width)
+        out_ref[c] = FACTOR * (acc_ref[:members, columns] + acc_ref[members:, columns])
+
+
+def build_and_product(zv, zi):
+    feats, width = zi.shape[1], zi.shape[2]
+    members = zv.shape[1] - feats
+    rows, columns = zv.shape[0] * width, zi.shape[0] * width
+    return pl.pallas_call(
+        build_body,
+        out_shape=[pltpu.VMEM((rows, columns), jnp.bfloat16)] * 2
+        + [jax.ShapeDtypeStruct((zi.shape[0], members, width), jnp.float32)],
         in_specs=[pl.BlockSpec(memory_space=VMEM)] * 2,
-        out_specs=[pl.BlockSpec(memory_space=VMEM)] * 2,
+        out_specs=[pl.BlockSpec(memory_space=VMEM)] * 3,
         scratch_shapes=[
             pltpu.VMEM((rows, 128), jnp.bfloat16),
             pltpu.VMEM((128, columns), jnp.bfloat16),
+            pltpu.VMEM((2 * members, rows), jnp.bfloat16),
+            pltpu.VMEM((2 * members, columns), jnp.float32),
+            pltpu.VMEM((width, TILE), jnp.float32),
         ],
         compiler_params=pltpu.CompilerParams(vmem_limit_bytes=12 * MIB),
         cost_estimate=pl.CostEstimate(
             flops=40 * rows * columns, bytes_accessed=4 * rows * columns, transcendentals=0
         ),
-        name="matern",
-    )(zj, zi)
+        name="build",
+    )(zv, zi)
 
 
 def product_body(v_ref, high_ref, low_ref, out_ref, vv_ref):
     count, members, width = v_ref.shape
-    for r in range(count):
-        high, low = halves(v_ref[r])
-        columns = slice(r * width, (r + 1) * width)
-        vv_ref[:members, columns] = high.astype(jnp.bfloat16)
-        vv_ref[members:, columns] = low.astype(jnp.bfloat16)
+    split_vector(v_ref, 0, vv_ref)
     wide = 2 * width
 
     @pl.loop(0, high_ref.shape[1] // wide)
@@ -136,6 +182,121 @@
         ),
         name="product",
     )(v, high, low)
+
+
+def to_column(row, size):
+    shape = (size, row.shape[1])
+    same = lax.broadcasted_iota(jnp.int32, shape, 0) == lax.broadcasted_iota(jnp.int32, shape, 1)
+    return jnp.sum(jnp.where(same, jnp.broadcast_to(row, shape), 0.0), axis=1, keepdims=True)
+
+
+def terms_body(capacity, values_ref, weights_ref, index_ref, count_ref, owner_ref, out_ref, t_ref):
+    slots, held = index_ref.shape
+    members = values_ref.shape[0] // held
+    lanes = slots * members
+    group = 2 * slots
+    lane = lax.broadcasted_iota(jnp.int32, (slots, lanes), 1)
+    own = lane // members == lax.broadcasted_iota(jnp.int32, (slots, lanes), 0)
+    for g in range(held // group):
+        weights = weights_ref[g * group * slots : (g + 1) * group * slots, :]
+        values = values_ref[g * group * members : (g + 1) * group * members, :]
+        every = lax.dot_general(
+            weights, values, (((1,), (1,)), ((), ())), preferred_element_type=jnp.float32
+        )
+        rows = []
+        for p in range(group):
+            part = every[p * slots : (p + 1) * slots, p // slots * lanes : (p // slots + 1) * lanes]
+            turn = (-(p % slots) * members) % lanes
+            part = pltpu.roll(part, turn, 1) if turn else part
+            part = pltpu.roll(part, 0, 1, stride=members, stride_axis=0)
+            rows.append(jnp.sum(jnp.where(own, part, 0.0), axis=0, keepdims=True))
+        t_ref[g * group : (g + 1) * group, :] = jnp.concatenate(rows, axis=0)
+    count = to_column(count_ref[...].astype(jnp.float32), held)
+    slot = (lax.broadcasted_iota(jnp.int32, (held, lanes), 1) // members).astype(jnp.float32)
+    terms = jnp.where(slot < count, t_ref[...], 0.0)
+    payload = jnp.concatenate(thirds(terms), axis=1).astype(jnp.bfloat16)
+
+    owner = owner_ref[...].astype(jnp.float32)
+    square = (held, held)
+    before = lax.broadcasted_iota(jnp.int32, square, 0) < lax.broadcasted_iota(jnp.int32, square, 1)
+    shared = (to_column(owner, held) == owner) & before
+    rank = jnp.sum(jnp.where(shared, 1.0, 0.0), axis=0, keepdims=True)
+    devices = out_ref.shape[0]
+    device = lax.broadcasted_iota(jnp.int32, (devices, held), 0).astype(jnp.float32)
+    mine = jnp.where(device == owner, 1.0, 0.0)
+    index = index_ref[...].astype(jnp.float32)
+    indices = []
+    for k in range(capacity):
+        ranked = jnp.where(rank == k, 1.0, 0.0)
+        table = (mine * ranked).astype(jnp.bfloat16)
+        placed = jnp.dot(table, payload, preferred_element_type=jnp.float32)
+        out_ref[:, k * lanes : (k + 1) * lanes] = (
+            placed[:, :lanes] + placed[:, lanes : 2 * lanes]
+        ) + placed[:, 2 * lanes :]
+        indices.append(index * ranked)
+    indices.append(jnp.zeros((lanes - capacity * slots, held), jnp.float32))
+    out_ref[:, capacity * lanes :] = lax.dot_general(
+        mine.astype(jnp.bfloat16),
+        jnp.concatenate(indices, axis=0).astype(jnp.bfloat16),
+        (((1,), (1,)), ((), ())),
+        preferred_element_type=jnp.float32,
+    )
+
+
+def terms_of(values, weights, index, count, owner, devices, capacity):
+    slots, held = index.shape
+    lanes = slots * (values.shape[0] // held)
+    return pl.pallas_call(
+        functools.partial(terms_body, capacity),
+        out_shape=jax.ShapeDtypeStruct((devices, (capacity + 1) * lanes), jnp.float32),
+        in_specs=[pl.BlockSpec(memory_space=VMEM)] * 5,
+        out_specs=pl.BlockSpec(memory_space=VMEM),
+        scratch_shapes=[pltpu.VMEM((held, lanes), jnp.float32)],
+        compiler_params=pltpu.CompilerParams(vmem_limit_bytes=8 * MIB),
+        cost_estimate=pl.CostEstimate(flops=10**9, bytes_accessed=10**6, transcendentals=0),
+        name="terms",
+    )(values, weights, index, count, owner)
+
+
+def gather_body(capacity, slots, message_ref, z_ref, rhs_ref, copies_ref):
+    devices = message_ref.shape[0]
+    members, width = rhs_ref.shape
+    lanes = slots * members
+    index = jnp.transpose(message_ref[:, capacity * lanes :])
+    station = lax.broadcasted_iota(jnp.int32, (width, devices), 0).astype(jnp.float32)
+    total = jnp.zeros((3 * members, width), jnp.float32)
+    for k in range(capacity):
+        terms = jnp.transpose(message_ref[:, k * lanes : (k + 1) * lanes])
+        split = [part.astype(jnp.bfloat16) for part in thirds(terms)]
+        for s in range(slots):
+            at = k * slots + s
+            here = jnp.where(station == index[at : at + 1, :], 1.0, 0.0).astype(jnp.bfloat16)
+            left = jnp.concatenate([p[s * members : (s + 1) * members] for p in split], axis=0)
+            total += lax.dot_general(
+                left, here, (((1,), (1,)), ((), ())), preferred_element_type=jnp.float32
+            )
+    rhs = total[:members] + (total[members : 2 * members] + total[2 * members :])
+    rhs_ref[...] = rhs
+    z = z_ref[...]
+    for r in range(copies_ref.shape[0]):
+        copies_ref[r, : z.shape[0]] = z
+        copies_ref[r, z.shape[0] :] = rhs
+
+
+def gather_terms(message, z, members, copies, capacity, slots):
+    feats, width = z.shape
+    return pl.pallas_call(
+        functools.partial(gather_body, capacity, slots),
+        out_shape=[
+            jax.ShapeDtypeStruct((members, width), jnp.float32),
+            jax.ShapeDtypeStruct((copies, feats + members, width), jnp.float32),
+        ],
+        in_specs=[pl.BlockSpec(memory_space=VMEM)] * 2,
+        out_specs=[pl.BlockSpec(memory_space=VMEM)] * 2,
+        compiler_params=pltpu.CompilerParams(vmem_limit_bytes=8 * MIB),
+        cost_estimate=pl.CostEstimate(flops=10**9, bytes_accessed=10**6, transcendentals=0),
+        name="gather",
+    )(message, z)
 
 
 def total_body(shares_ref, v_ref, nugget_ref, out_ref, copies_ref):
@@ -271,46 +432,23 @@
     stations = nugget.shape[0]
     capacity = max(2, 2 * held // devices)
 
-    scaled_cov = covariates / lengthscale[:, None]
-    column_cov, row_cov = spread(scaled_cov, ROW), spread(scaled_cov, COL)
-
-    terms = jnp.einsum(
-        "psc,pmc->psm", patch_weights, patch_values, preferred_element_type=jnp.float32
+    z = covariates / lengthscale[:, None]
+    zi = spread(z, COL)
+    message = terms_of(
+        patch_values.reshape(held * members, cells),
+        patch_weights.reshape(held * slots, cells),
+        block_index.T,
+        slot_count[None, :],
+        owner.T,
+        devices,
+        capacity,
     )
-    live = (jnp.arange(slots)[None, :] < slot_count[:, None]).astype(jnp.float32)
-    terms = (terms * live[:, :, None]).reshape(held, slots * members)
-    target = owner[:, 0]
-    earlier = jnp.arange(held)[None, :] < jnp.arange(held)[:, None]
-    rank = jnp.sum(((target[:, None] == target[None, :]) & earlier).astype(jnp.int32), axis=1)
-    position = rank * devices + target
-    table = (position[None, :] == jnp.arange(devices * capacity)[:, None]).astype(jnp.float32)
-    payload = jnp.concatenate([terms, block_index.astype(jnp.float32)], axis=1)
-    placed = jnp.dot(table, payload, precision=HIGH, preferred_element_type=jnp.float32)
-    placed = placed.reshape(capacity, devices, payload.shape[1])
-    message = jnp.concatenate(
-        [placed[k, :, : slots * members] for k in range(capacity)]
-        + [placed[k, :, slots * members :] for k in range(capacity)],
-        axis=1,
-    )
-    message = lax.all_to_all(message, ALL, split_axis=0, concat_axis=0, tiled=True)
-
-    entries = capacity * slots
-    flat = message[:, : entries * members].reshape(devices, entries, members)
-    index = message[:, entries * members :].astype(jnp.int32)
-    onehot = (index.reshape(-1)[:, None] == jnp.arange(stations)[None, :]).astype(jnp.float32)
-    rhs = lax.dot_general(
-        flat.reshape(-1, members),
-        onehot,
-        (((0,), (0,)), ((), ())),
-        precision=HIGH,
-        preferred_element_type=jnp.float32,
-    )
-
-    gathered = spread(rhs, ROW)
-    gathered, column_cov, row_cov = lax.optimization_barrier((gathered, column_cov, row_cov))
-    high, low = build_kernel(column_cov, row_cov)
+    zi, message = lax.optimization_barrier((zi, message))
+    message = exchange(message, ALL)
+    rhs, copies = gather_terms(message, z, members, lax.axis_size(ROW), capacity, slots)
     nugget = nugget[None, :]
-    shares = exchange(kernel_product(gathered, high, low), COL)
+    high, low, partial_value = build_and_product(exchange(copies, ROW), zi)
+    shares = exchange(partial_value, COL)
     first, copies = total_of(shares, rhs, nugget, lax.axis_size(ROW))
     shares = exchange(kernel_product(exchange(copies, ROW), high, low), COL)
     second, sums = close(shares, rhs, first, nugget)

time: 142 us -> 125 us (0.88)
  blocking collectives: 54.7 us -> 75.3 us
  waiting for transfers between devices: 20.2 us -> 1.74 us
  starting transfers between devices: 18.8 us -> 8.59 us
  matrix products: 5.17 us -> 0 us
  Pallas kernels: 33.6 us -> 31.1 us
  other arithmetic: 3.2 us -> 0.79 us
    all_to_all x4 -> x6, blocking collectives: 45.4 us -> 75.3 us  [exchange(): return lax.all_to_all(pieces, axes, split_axis=0, concat_axis=0, tiled=True)]
    all_to_all x1 -> x0, waiting for transfers between devices: 12 us -> none  [local(): lax.all_to_all(message, ALL, split_axis=0, concat_axis=0, tiled=True)]
    all_to_all x1 -> x0, starting transfers between devices: 11.5 us -> none  [local(): lax.all_to_all(message, ALL, split_axis=0, concat_axis=0, tiled=True)]
    all_to_all x1 -> x0, blocking collectives: 9.35 us -> none  [spread(): return lax.all_to_all(copies, axes, split_axis=0, concat_axis=0, tiled=True)]
    all_to_all x2 -> x1, waiting for transfers between devices: 8.25 us -> 1.74 us  [spread(): return lax.all_to_all(copies, axes, split_axis=0, concat_axis=0, tiled=True)]
    pallas_call x2 -> x1, Pallas kernels: 12.5 us -> 6.24 us  [kernel_product(): pl.pallas_call(product_body, out_shape=jax.ShapeDtypeStruct((columns // w...]
    dot_general x3 -> x0, matrix products: 5.17 us -> none  [the longest x1 3.04 us: local(): lax.dot_general(flat.reshape(-1, members), onehot, (((0,), (0,)), ((), ()...]
    unnamed x15, local copies, waits for them, and re-layouts: 0.06 us -> 5.02 us
  transfers between devices with their start and end apart: 3 -> 1, of which waited for: 3 -> 1; matrix products, arithmetic and copies ran while one was open for 3% -> 0% of each run, Pallas kernels for 0% -> 1%
where the time goes in v3:
time: 125 us; the launch traced here: 124 us
  blocking collectives  75.3 us (60%)
  Pallas kernels  31.1 us (25%)
  starting transfers between devices  8.59 us (7%)
  local copies, waits for them, and re-layouts  6.13 us (5%)
  waiting for transfers between devices  1.74 us (1%)
    all_to_all x6, blocking collectives, exchange(): return lax.all_to_all(pieces, axes, split_axis=0, concat_axis=0, tiled=True)  75.3 us
    pallas_call x1, Pallas kernels, build_and_product(): pl.pallas_call(build_body, out_shape=[pltpu.VMEM((rows, columns), jnp.bfl...  21 us
    all_to_all x1, starting transfers between devices, spread(): return lax.all_to_all(copies, axes, split_axis=0, concat_axis=0, tiled=True)  8.59 us
    pallas_call x1, Pallas kernels, kernel_product(): pl.pallas_call(product_body, out_shape=jax.ShapeDtypeStruct((columns // w...  6.24 us
    unnamed x15, local copies, waits for them, and re-layouts  5.02 us
  transfers between devices with their start and end apart: 1, of which 1 were waited for; matrix products, arithmetic and copies ran while one was open for 0% of the time, Pallas kernels for 1%

profile of v3, /device:TPU:1, one launch (start us, length us, event | category | flops | bytes accessed | tf_op | source)
XLA Modules:
  0.0 124.4 jit_solution(14814708278141190580)
XLA Ops:
  0.6 0.8 broadcast_divide_fusion.z_ref
  1.4 0.7 broadcast_in_dim.10
  2.2 8.6 %all-to-all-start = ((f32[16,16,256]{2,1,0:T(8,128)}), f32[16,16,256]{2,1,0:T(8,128)S(1)}, u32[]{:S(2)}, u32[]{:S(2)}) async-start(f32[16,16,256]{2,1,0:T(8,128)} %broadcast_in_dim.10), calls=%async_computation | async-start | bytes 524288 | tf_op jit(solution)/shard_map/all_to_all | solution.py:29
  10.8 0.0 copy-start.2
  10.8 1.2 copy-done.2
  12.0 0.0 copy-start.3
  12.0 1.0 copy-done.3
  13.0 0.0 copy-start.4
  13.0 0.7 copy-done.4
  13.7 0.0 copy-start.5
  13.7 0.7 copy-done.5
  14.4 0.0 copy-start.6
  14.4 0.7 copy-done.6
  15.1 1.5 %terms.1 = f32[128,640]{1,0:T(8,128)S(1)} custom-call(bf16[4096,128]{1,0:T(8,128)(2,1)S(1)} %bitcast.18, bf16[2048,128]{1,0:T(8,128)(2,1)S(1)} %bitcast.19, s32[8,256]{1,0:T(8,128)S(1)} %bitcast.20, s32[1,256]{1,0:T(1,128)S(1)} %bitcast.21, s32[1,256]{1,0:T(1,128)S(1)} %bitcast.22), custom_call_target="tpu_custom_call" | custom-call | flops 1000000000 | bytes 1000000 | tf_op jit(solution)/shard_map/terms/pallas_call | solution.py:249
  16.6 1.7 %all-to-all-done.zi_ref = f32[16,16,256]{2,1,0:T(8,128)S(1)} async-done(((f32[16,16,256]{2,1,0:T(8,128)}), f32[16,16,256]{2,1,0:T(8,128)S(1)}, u32[]{:S(2)}, u32[]{:S(2)}) %all-to-all-start) | async-done | bytes 262176 | tf_op jit(solution)/shard_map/all_to_all | solution.py:29
  18.3 0.3 copy.10
  18.6 20.3 %all_to_all.41 = f32[128,1,640]{2,1,0:T(1,128)S(1)} all-to-all(f32[128,1,640]{2,1,0:T(1,128)S(1)} %copy.10), channel_id=1, replica_groups=mesh['row_0'=4,'row_1'=2,'col_0'=4,'col_1'=4] {'row_0','row_1','col_0','..., dimensions={0} | all-to-all | bytes 655360 | tf_op jit(solution)/shard_map/all_to_all | solution.py:423
  38.9 0.8 gather.1
  39.8 9.4 %all_to_all.42.zv_ref = f32[8,32,256]{2,1,0:T(8,128)S(1)} all-to-all(f32[8,32,256]{2,1,0:T(8,128)S(1)} %get-tuple-element.14), channel_id=1, replica_groups=mesh['row_0'=4,'row_1'=2,'col_0'=4,'col_1'=4] {'row_0','row_1'}, dimensions={0} | all-to-all | bytes 524288 | tf_op jit(solution)/shard_map/all_to_all | solution.py:423
  49.2 21.0 %build.1 = (bf16[2048,4096]{1,0:T(8,128)(2,1)S(1)}, bf16[2048,4096]{1,0:T(8,128)(2,1)S(1)}, f32[16,16,256]{2,1,0:T(8,128)S(1)}) custom-call(f32[8,32,256]{2,1,0:T(8,128)S(1)} %all_to_all.42.zv_ref, f32[16,16,256]{2,1,0:T(8,128)S(1)} %all-to-all-done.zi_ref), custom_call_target="tpu_custom_call" | custom-call | flops 335544320 | bytes 33554432 | tf_op jit(solution)/shard_map/build/pallas_call | solution.py:133
  70.1 10.4 %all_to_all.43.shares_ref = f32[16,16,256]{2,1,0:T(8,128)S(1)} all-to-all(f32[16,16,256]{2,1,0:T(8,128)S(1)} %get-tuple-element.16), channel_id=1, replica_groups=mesh['row_0'=4,'row_1'=2,'col_0'=4,'col_1'=4] {'col_0','col_1'}, dimensions={0} | all-to-all | bytes 524288 | tf_op jit(solution)/shard_map/all_to_all | solution.py:423
  80.6 0.0 copy-start
  80.6 0.7 copy-done
  81.3 9.9 %all_to_all.44.v_ref = f32[8,16,256]{2,1,0:T(8,128)S(1)} all-to-all(f32[8,16,256]{2,1,0:T(8,128)S(1)} %get-tuple-element.18), channel_id=1, replica_groups=mesh['row_0'=4,'row_1'=2,'col_0'=4,'col_1'=4] {'row_0','row_1'}, dimensions={0} | all-to-all | bytes 262144 | tf_op jit(solution)/shard_map/all_to_all | solution.py:423
  91.2 0.0 copy-start.1
  91.2 6.2 %product.1 = f32[16,16,256]{2,1,0:T(8,128)S(1)} custom-call(f32[8,16,256]{2,1,0:T(8,128)S(1)} %all_to_all.44.v_ref, bf16[2048,4096]{1,0:T(8,128)(2,1)S(1)} %get-tuple-element.19.high_ref, bf16[2048,4096]{1,0:T(8,128)(2,1)S(1)} %get-tuple-element.20.low_ref), custom_call_target="tpu_custom_call" | custom-call | flops 1073741824 | bytes 33554432 | tf_op jit(solution)/shard_map/product/pallas_call | solution.py:173
  97.5 10.2 %all_to_all.45.shares_ref = f32[16,16,256]{2,1,0:T(8,128)S(1)} all-to-all(f32[16,16,256]{2,1,0:T(8,128)S(1)} %product.1), channel_id=1, replica_groups=mesh['row_0'=4,'row_1'=2,'col_0'=4,'col_1'=4] {'col_0','col_1'}, dimensions={0} | all-to-all | bytes 524288 | tf_op jit(solution)/shard_map/all_to_all | solution.py:423
  107.7 0.0 copy-done.1
  107.7 0.2 close.1
  107.9 15.1 %all_to_all.46 = f32[128,1,128]{2,1,0:T(1,128)S(1)} all-to-all(f32[128,1,128]{2,1,0:T(1,128)S(1)} %broadcast_in_dim.25), channel_id=1, replica_groups=mesh['row_0'=4,'row_1'=2,'col_0'=4,'col_1'=4] {'row_0','row_1','col_0','..., dimensions={0} | all-to-all | bytes 131072 | tf_op jit(solution)/shard_map/all_to_all | solution.py:423
  123.0 1.4 %finish.1 = (f32[16,256]{1,0:T(8,128)}, f32[16,256]{1,0:T(8,128)}) custom-call(f32[128,128]{1,0:T(8,128)S(1)} %bitcast.14, f32[16,256]{1,0:T(8,128)S(1)} %get-tuple-element.17.v_ref.rhs_ref, f32[16,256]{1,0:T(8,128)S(1)} %get-tuple-element.21.first_ref, f32[16,256]{1,0:T(8,128)S(1)} %get-tuple-element.23.second_ref), custom_call_target="tpu_custom_call" | custom-call | tf_op jit(solution)/shard_map/finish/pallas_call | solution.py:412
  (3 shorter events, 0.1 us)
Async XLA Ops:
  2.2 16.1 %all-to-all-start = ((f32[16,16,256]{2,1,0:T(8,128)}), f32[16,16,256]{2,1,0:T(8,128)S(1)}, u32[]{:S(2)}, u32[]{:S(2)}) async-start(f32[16,16,256]{2,1,0:T(8,128)} %broadcast_in_dim.10), calls=%async_computation | async-start | bytes 524288 | tf_op jit(solution)/shard_map/all_to_all | solution.py:29
  10.8 1.2 copy-start.2
  12.0 1.0 copy-start.3
  13.0 0.7 copy-start.4
  13.7 0.7 copy-start.5
  14.4 0.7 copy-start.6
  80.6 0.7 copy-start
  91.2 16.4 %copy-start.1 = (f32[256]{0:T(256)S(1)}, f32[256]{0:T(256)}, u32[]{:S(2)}) copy-start(f32[256]{0:T(256)} %param.10) | copy-start | bytes 3076

commit v4 on v3

--- a/solution.py
+++ b/solution.py
@@ -19,14 +19,19 @@
 LINEAR = 3.0 / LN2
 CONST = 3.0 / (LN2 * LN2)
 TINY = 1e-30
-TILE, TILES = 512, 4
+TALL, WIDE = 512, 256
 VMEM = pltpu.MemorySpace.VMEM
+HBM = pltpu.MemorySpace.HBM
 MIB = 1 << 20
 
 
-def spread(shard, axes):
-    copies = jnp.broadcast_to(shard[None], (lax.axis_size(axes),) + shard.shape)
-    return lax.all_to_all(copies, axes, split_axis=0, concat_axis=0, tiled=True)
+def rotate(x, axis, by):
+    size = lax.axis_size(axis)
+    return lax.ppermute(x, axis, [(i, (i + by) % size) for i in range(size)])
+
+
+def ring(x, axis):
+    return [rotate(x, axis, by) for by in range(1, lax.axis_size(axis))]
 
 
 def halves(x):
@@ -74,25 +79,21 @@
 
 
 def build_body(
-    zv_ref, zi_ref, high_ref, low_ref, out_ref, fj_ref, fi_ref, vv_ref, acc_ref, ahead_ref
+    zv_ref, fi_ref, high_ref, low_ref, out_ref, fj_ref, vv_ref, acc_ref, ahead_ref
 ):
-    feats, members, width = zi_ref.shape[1], vv_ref.shape[0] // 2, zi_ref.shape[2]
+    members, width = out_ref.shape[1:]
+    feats = zv_ref.shape[1] - members
     for r in range(zv_ref.shape[0]):
         block = features(zv_ref[r, :feats] * SCALE, True)
         fj_ref[r * width : (r + 1) * width, :] = jnp.transpose(block.astype(jnp.bfloat16))
-    for c in range(zi_ref.shape[0]):
-        block = features(zi_ref[c] * SCALE, False)
-        fi_ref[:, c * width : (c + 1) * width] = block.astype(jnp.bfloat16)
     split_vector(zv_ref, feats, vv_ref)
     acc_ref[...] = jnp.zeros_like(acc_ref)
-    tall, wide, tiles = width, TILE, TILES
-    across = fi_ref.shape[1] // (wide * tiles)
-    steps = across * (fj_ref.shape[0] // tall)
+    tall, wide = TALL, WIDE
+    tiles, steps = fi_ref.shape[1] // wide, fj_ref.shape[0] // tall
 
     def place(step, tile):
-        rows = pl.ds(pl.multiple_of((step // across) * tall, tall), tall)
-        columns = ((step % across) * tiles + tile) * wide
-        return rows, pl.ds(pl.multiple_of(columns, wide), wide)
+        rows = pl.ds(pl.multiple_of(step * tall, tall), tall)
+        return rows, slice(tile * wide, (tile + 1) * wide)
 
     def squares(step, tile):
         rows, columns = place(step, tile)
@@ -126,49 +127,42 @@
         out_ref[c] = FACTOR * (acc_ref[:members, columns] + acc_ref[members:, columns])
 
 
-def build_and_product(zv, zi):
-    feats, width = zi.shape[1], zi.shape[2]
-    members = zv.shape[1] - feats
-    rows, columns = zv.shape[0] * width, zi.shape[0] * width
+def build_and_product(zv, fi, members):
+    width = zv.shape[2]
+    rows, columns = zv.shape[0] * width, fi.shape[1]
     return pl.pallas_call(
         build_body,
         out_shape=[pltpu.VMEM((rows, columns), jnp.bfloat16)] * 2
-        + [jax.ShapeDtypeStruct((zi.shape[0], members, width), jnp.float32)],
+        + [jax.ShapeDtypeStruct((columns // width, members, width), jnp.float32)],
         in_specs=[pl.BlockSpec(memory_space=VMEM)] * 2,
         out_specs=[pl.BlockSpec(memory_space=VMEM)] * 3,
         scratch_shapes=[
-            pltpu.VMEM((rows, 128), jnp.bfloat16),
-            pltpu.VMEM((128, columns), jnp.bfloat16),
+            pltpu.VMEM((rows, fi.shape[0]), jnp.bfloat16),
             pltpu.VMEM((2 * members, rows), jnp.bfloat16),
             pltpu.VMEM((2 * members, columns), jnp.float32),
-            pltpu.VMEM((width, TILE), jnp.float32),
+            pltpu.VMEM((TALL, WIDE), jnp.float32),
         ],
         compiler_params=pltpu.CompilerParams(vmem_limit_bytes=12 * MIB),
         cost_estimate=pl.CostEstimate(
             flops=40 * rows * columns, bytes_accessed=4 * rows * columns, transcendentals=0
         ),
         name="build",
-    )(zv, zi)
+    )(zv, fi)
 
 
 def product_body(v_ref, high_ref, low_ref, out_ref, vv_ref):
-    count, members, width = v_ref.shape
+    _, members, width = v_ref.shape
     split_vector(v_ref, 0, vv_ref)
-    wide = 2 * width
-
-    @pl.loop(0, high_ref.shape[1] // wide)
-    def _(step):
-        columns = pl.ds(pl.multiple_of(step * wide, wide), wide)
-        vv = vv_ref[...]
-        both = jnp.dot(vv, high_ref[:, columns], preferred_element_type=jnp.float32)
-        both += jnp.dot(vv, low_ref[:, columns], preferred_element_type=jnp.float32)
-        total = FACTOR * (both[:members] + both[members:])
-        for t in range(2):
-            out_ref[step * 2 + t] = total[:, t * width : (t + 1) * width]
+    vv = vv_ref[...]
+    both = jnp.dot(vv, high_ref[...], preferred_element_type=jnp.float32)
+    both += jnp.dot(vv, low_ref[...], preferred_element_type=jnp.float32)
+    total = FACTOR * (both[:members] + both[members:])
+    for c in range(out_ref.shape[0]):
+        out_ref[c] = total[:, c * width : (c + 1) * width]
 
 
 def kernel_product(v, high, low):
-    count, members, width = v.shape
+    _, members, width = v.shape
     rows, columns = high.shape
     return pl.pallas_call(
         product_body,
@@ -190,11 +184,47 @@
     return jnp.sum(jnp.where(same, jnp.broadcast_to(row, shape), 0.0), axis=1, keepdims=True)
 
 
-def terms_body(capacity, values_ref, weights_ref, index_ref, count_ref, owner_ref, out_ref, t_ref):
+def terms_body(capacity, *refs):
+    sources, (out_ref, z_ref, nugget_out_ref) = refs[:8], refs[8:11]
+    t_ref, held_refs, sems = refs[11], refs[12:20], refs[20]
+    copies = [
+        pltpu.make_async_copy(source, held_ref, sems.at[i])
+        for i, (source, held_ref) in enumerate(zip(sources, held_refs))
+    ]
+    for copy in copies:
+        copy.start()
+    values_ref, weights_ref, index_ref, count_ref, owner_ref, cov_ref, scale_ref, nugget_ref = held_refs
     slots, held = index_ref.shape
     members = values_ref.shape[0] // held
     lanes = slots * members
     group = 2 * slots
+
+    for copy in copies[2:]:
+        copy.wait()
+    z_ref[...] = cov_ref[...] / to_column(scale_ref[...], cov_ref.shape[0])
+    nugget_out_ref[...] = nugget_ref[...]
+    owner = owner_ref[...].astype(jnp.float32)
+    square = (held, held)
+    before = lax.broadcasted_iota(jnp.int32, square, 0) < lax.broadcasted_iota(jnp.int32, square, 1)
+    shared = (to_column(owner, held) == owner) & before
+    rank = jnp.sum(jnp.where(shared, 1.0, 0.0), axis=0, keepdims=True)
+    devices = out_ref.shape[0]
+    device = lax.broadcasted_iota(jnp.int32, (devices, held), 0).astype(jnp.float32)
+    mine = jnp.where(device == owner, 1.0, 0.0)
+    count = to_column(count_ref[...].astype(jnp.float32), held)
+    index = index_ref[...].astype(jnp.float32)
+    ranked = [jnp.where(rank == k, 1.0, 0.0) for k in range(capacity)]
+    indices = [index * r for r in ranked]
+    indices.append(jnp.zeros((lanes - capacity * slots, held), jnp.float32))
+    out_ref[:, capacity * lanes :] = lax.dot_general(
+        mine.astype(jnp.bfloat16),
+        jnp.concatenate(indices, axis=0).astype(jnp.bfloat16),
+        (((1,), (1,)), ((), ())),
+        preferred_element_type=jnp.float32,
+    )
+
+    for copy in copies[:2]:
+        copy.wait()
     lane = lax.broadcasted_iota(jnp.int32, (slots, lanes), 1)
     own = lane // members == lax.broadcasted_iota(jnp.int32, (slots, lanes), 0)
     for g in range(held // group):
@@ -211,51 +241,67 @@
             part = pltpu.roll(part, 0, 1, stride=members, stride_axis=0)
             rows.append(jnp.sum(jnp.where(own, part, 0.0), axis=0, keepdims=True))
         t_ref[g * group : (g + 1) * group, :] = jnp.concatenate(rows, axis=0)
-    count = to_column(count_ref[...].astype(jnp.float32), held)
     slot = (lax.broadcasted_iota(jnp.int32, (held, lanes), 1) // members).astype(jnp.float32)
     terms = jnp.where(slot < count, t_ref[...], 0.0)
     payload = jnp.concatenate(thirds(terms), axis=1).astype(jnp.bfloat16)
-
-    owner = owner_ref[...].astype(jnp.float32)
-    square = (held, held)
-    before = lax.broadcasted_iota(jnp.int32, square, 0) < lax.broadcasted_iota(jnp.int32, square, 1)
-    shared = (to_column(owner, held) == owner) & before
-    rank = jnp.sum(jnp.where(shared, 1.0, 0.0), axis=0, keepdims=True)
-    devices = out_ref.shape[0]
-    device = lax.broadcasted_iota(jnp.int32, (devices, held), 0).astype(jnp.float32)
-    mine = jnp.where(device == owner, 1.0, 0.0)
-    index = index_ref[...].astype(jnp.float32)
-    indices = []
     for k in range(capacity):
-        ranked = jnp.where(rank == k, 1.0, 0.0)
-        table = (mine * ranked).astype(jnp.bfloat16)
+        table = (mine * ranked[k]).astype(jnp.bfloat16)
         placed = jnp.dot(table, payload, preferred_element_type=jnp.float32)
         out_ref[:, k * lanes : (k + 1) * lanes] = (
             placed[:, :lanes] + placed[:, lanes : 2 * lanes]
         ) + placed[:, 2 * lanes :]
-        indices.append(index * ranked)
-    indices.append(jnp.zeros((lanes - capacity * slots, held), jnp.float32))
-    out_ref[:, capacity * lanes :] = lax.dot_general(
-        mine.astype(jnp.bfloat16),
-        jnp.concatenate(indices, axis=0).astype(jnp.bfloat16),
-        (((1,), (1,)), ((), ())),
-        preferred_element_type=jnp.float32,
-    )
-
-
-def terms_of(values, weights, index, count, owner, devices, capacity):
+
+
+def terms_of(args, devices, capacity):
+    values, _, index, _, _, covariates, _, nugget = args
     slots, held = index.shape
     lanes = slots * (values.shape[0] // held)
     return pl.pallas_call(
         functools.partial(terms_body, capacity),
-        out_shape=jax.ShapeDtypeStruct((devices, (capacity + 1) * lanes), jnp.float32),
-        in_specs=[pl.BlockSpec(memory_space=VMEM)] * 5,
-        out_specs=pl.BlockSpec(memory_space=VMEM),
-        scratch_shapes=[pltpu.VMEM((held, lanes), jnp.float32)],
+        out_shape=[
+            jax.ShapeDtypeStruct((devices, (capacity + 1) * lanes), jnp.float32),
+            jax.ShapeDtypeStruct(covariates.shape, jnp.float32),
+            jax.ShapeDtypeStruct(nugget.shape, jnp.float32),
+        ],
+        in_specs=[pl.BlockSpec(memory_space=HBM)] * len(args),
+        out_specs=[pl.BlockSpec(memory_space=VMEM)] * 3,
+        scratch_shapes=[pltpu.VMEM((held, lanes), jnp.float32)]
+        + [pltpu.VMEM(x.shape, x.dtype) for x in args]
+        + [pltpu.SemaphoreType.DMA((len(args),))],
         compiler_params=pltpu.CompilerParams(vmem_limit_bytes=8 * MIB),
         cost_estimate=pl.CostEstimate(flops=10**9, bytes_accessed=10**6, transcendentals=0),
         name="terms",
-    )(values, weights, index, count, owner)
+    )(*(pltpu.with_memory_space_constraint(x, HBM) for x in args))
+
+
+def place_body(*refs):
+    pieces, fi_ref = refs[:-1], refs[-1]
+    width = pieces[0].shape[2]
+    outer, inner = lax.axis_index(COL[0]), lax.axis_index(COL[1])
+    sides = [lax.axis_size(name) for name in COL]
+    at = 0
+    for ref in pieces:
+        for n in range(ref.shape[0]):
+            by_inner, by_outer = at // sides[0], at % sides[0]
+            source = (outer - by_outer + sides[0]) % sides[0] * sides[1]
+            source += (inner - by_inner + sides[1]) % sides[1]
+            columns = pl.ds(pl.multiple_of(source * width, width), width)
+            fi_ref[:, columns] = features(ref[n] * SCALE, False).astype(jnp.bfloat16)
+            at += 1
+
+
+def place(pieces):
+    width = pieces[0].shape[2]
+    blocks = sum(piece.shape[0] for piece in pieces)
+    return pl.pallas_call(
+        place_body,
+        out_shape=jax.ShapeDtypeStruct((128, blocks * width), jnp.bfloat16),
+        in_specs=[pl.BlockSpec(memory_space=VMEM)] * len(pieces),
+        out_specs=pl.BlockSpec(memory_space=VMEM),
+        compiler_params=pltpu.CompilerParams(vmem_limit_bytes=4 * MIB),
+        cost_estimate=pl.CostEstimate(flops=10**9, bytes_accessed=10**6, transcendentals=0),
+        name="place",
+    )(*pieces)
 
 
 def gather_body(capacity, slots, message_ref, z_ref, rhs_ref, copies_ref):
@@ -429,25 +475,28 @@
     devices = lax.axis_size(ALL)
     held, members, cells = patch_values.shape
     slots = patch_weights.shape[1]
-    stations = nugget.shape[0]
     capacity = max(2, 2 * held // devices)
 
-    z = covariates / lengthscale[:, None]
-    zi = spread(z, COL)
-    message = terms_of(
-        patch_values.reshape(held * members, cells),
-        patch_weights.reshape(held * slots, cells),
-        block_index.T,
-        slot_count[None, :],
-        owner.T,
+    message, z, nugget = terms_of(
+        (
+            patch_values.reshape(held * members, cells),
+            patch_weights.reshape(held * slots, cells),
+            block_index.T,
+            slot_count[None, :],
+            owner.T,
+            covariates,
+            lengthscale[None, :],
+            nugget[None, :],
+        ),
         devices,
         capacity,
     )
-    zi, message = lax.optimization_barrier((zi, message))
+    near = [z[None]] + ring(z[None], COL[0])
+    far = ring(jnp.concatenate(near), COL[1])
+    row_features = place(near + far)
     message = exchange(message, ALL)
     rhs, copies = gather_terms(message, z, members, lax.axis_size(ROW), capacity, slots)
-    nugget = nugget[None, :]
-    high, low, partial_value = build_and_product(exchange(copies, ROW), zi)
+    high, low, partial_value = build_and_product(exchange(copies, ROW), row_features, members)
     shares = exchange(partial_value, COL)
     first, copies = total_of(shares, rhs, nugget, lax.axis_size(ROW))
     shares = exchange(kernel_product(exchange(copies, ROW), high, low), COL)

time: 125 us -> 112 us (0.90)
  blocking collectives: 75.3 us -> 47.3 us
  starting transfers between devices: 8.59 us -> 21.7 us
  waiting for transfers between devices: 1.74 us -> 13.1 us
  local copies, waits for them, and re-layouts: 6.13 us -> 1.12 us
  Pallas kernels: 31.1 us -> 27.7 us
    all_to_all x6 -> x4, blocking collectives: 75.3 us -> 47.3 us  [exchange(): return lax.all_to_all(pieces, axes, split_axis=0, concat_axis=0, tiled=True)]
    all_to_all x1 -> x2, starting transfers between devices: 8.59 us -> 15.3 us  [exchange(): return lax.all_to_all(pieces, axes, split_axis=0, concat_axis=0, tiled=True)]
    ppermute x0 -> x6, starting transfers between devices: none -> 6.39 us  [rotate(): return lax.ppermute(x, axis, [(i, (i + by) % size) for i in range(size)])]
    all_to_all x1 -> x2, waiting for transfers between devices: 1.74 us -> 7.89 us  [exchange(): return lax.all_to_all(pieces, axes, split_axis=0, concat_axis=0, tiled=True)]
    ppermute x0 -> x6, waiting for transfers between devices: none -> 5.21 us  [rotate(): return lax.ppermute(x, axis, [(i, (i + by) % size) for i in range(size)])]
    unnamed x15 -> x1, local copies, waits for them, and re-layouts: 5.02 us -> 0.02 us
    pallas_call x1, Pallas kernels: 21 us -> 16.3 us  [build_and_product(): pl.pallas_call(build_body, out_shape=[pltpu.VMEM((rows, columns), jnp.bfl...]
    pallas_call x1 -> x2, Pallas kernels: 1.47 us -> 2.97 us  [the longest x1 2.73 us: terms_of(): pl.pallas_call(functools.partial(terms_body, capacity), out_shape=[jax.Sh...]
  transfers between devices with their start and end apart: 1 -> 8, of which waited for: 1 -> 4; matrix products, arithmetic and copies ran while one was open for 0% -> 0% of each run, Pallas kernels for 1% -> 2%
where the time goes in v4:
time: 112 us
  blocking collectives  47.3 us (42%)
  Pallas kernels  27.7 us (25%)
  starting transfers between devices  21.7 us (19%)
  waiting for transfers between devices  13.1 us (12%)
  local copies, waits for them, and re-layouts  1.12 us (1%)
    all_to_all x4, blocking collectives, exchange(): return lax.all_to_all(pieces, axes, split_axis=0, concat_axis=0, tiled=True)  47.3 us
    pallas_call x1, Pallas kernels, build_and_product(): pl.pallas_call(build_body, out_shape=[pltpu.VMEM((rows, columns), jnp.bfl...  16.3 us
    all_to_all x2, starting transfers between devices, exchange(): return lax.all_to_all(pieces, axes, split_axis=0, concat_axis=0, tiled=True)  15.3 us
    all_to_all x2, waiting for transfers between devices, exchange(): return lax.all_to_all(pieces, axes, split_axis=0, concat_axis=0, tiled=True)  7.89 us
    ppermute x6, starting transfers between devices, rotate(): return lax.ppermute(x, axis, [(i, (i + by) % size) for i in range(size)])  6.39 us
    pallas_call x1, Pallas kernels, kernel_product(): pl.pallas_call(product_body, out_shape=jax.ShapeDtypeStruct((columns // w...  5.34 us
    ppermute x6, waiting for transfers between devices, rotate(): return lax.ppermute(x, axis, [(i, (i + by) % size) for i in range(size)])  5.21 us
    pallas_call x1, Pallas kernels, terms_of(): pl.pallas_call(functools.partial(terms_body, capacity), out_shape=[jax.Sh...  2.73 us
  transfers between devices with their start and end apart: 8, of which 4 were waited for; matrix products, arithmetic and copies ran while one was open for 0% of the time, Pallas kernels for 2%

profile of v4, /device:TPU:1, one launch (start us, length us, event | category | flops | bytes accessed | tf_op | source)
XLA Modules:
  0.0 111.7 jit_solution(5786763194996733020)
XLA Ops:
  0.6 2.7 %terms.1 = (f32[128,640]{1,0:T(8,128)S(1)}, f32[16,256]{1,0:T(8,128)S(1)}, f32[1,256]{1,0:T(1,128)S(1)}) custom-call(bf16[4096,128]{1,0:T(8,128)(2,1)} %bitcast.23, bf16[2048,128]{1,0:T(8,128)(2,1)} %bitcast.24, s32[8,256]{1,0:T(8,128)} %bitcast.25, s32[1,256]{1,0:T(1,128)} %bitcast.26, s32[1,256]{1,0:T(1,128)} %bitcast.27, f32[16,256]{1,0:T(8,128)} %refs_5_.1, ...), custom_call_target="tpu_custom_call" | custom-call | flops 1000000000 | bytes 1000000 | tf_op jit(solution)/shard_map/terms/pallas_call | solution.py:259
  3.4 1.1 copy.10
  4.4 11.5 %all-to-all-start = ((f32[128,1,640]{2,1,0:T(1,128)}), f32[128,1,640]{2,1,0:T(1,128)S(1)}, u32[]{:S(2)}, u32[]{:S(2)}) async-start(f32[128,1,640]{2,1,0:T(1,128)} %copy.10), calls=%async_computation | async-start | bytes 655360 | tf_op jit(solution)/shard_map/all_to_all | solution.py:469
  15.9 3.3 %collective-permute-start.2 = (f32[1,16,256]{2,1,0:T(8,128)S(1)}, f32[1,16,256]{2,1,0:T(8,128)S(1)}, u32[]{:S(2)}, u32[]{:S(2)}) collective-permute-start(f32[1,16,256]{2,1,0:T(8,128)S(1)} %bitcast.17), channel_id=1, source_target_pairs={{0,12},{4,0},{8,4},{12,8},{1,13},{5,1},{9,5},{13,9},{2,14},{6,2},{... | collective-permute-start | bytes 49160 | tf_op jit(solution)/shard_map/ppermute | solution.py:30
  19.2 0.1 collective-permute-start.1
  19.3 0.8 collective-permute-start
  20.1 7.9 %all-to-all-done = f32[128,1,640]{2,1,0:T(1,128)S(1)} async-done(((f32[128,1,640]{2,1,0:T(1,128)}), f32[128,1,640]{2,1,0:T(1,128)S(1)}, u32[]{:S(2)}, u32[]{:S(2)}) %all-to-all-start) | async-done | bytes 327712 | tf_op jit(solution)/shard_map/all_to_all | solution.py:469
  28.0 1.5 %gather.1 = (f32[16,256]{1,0:T(8,128)S(1)}, f32[8,32,256]{2,1,0:T(8,128)}) custom-call(f32[128,640]{1,0:T(8,128)S(1)} %bitcast.15, f32[16,256]{1,0:T(8,128)S(1)} %get-tuple-element.15.z_ref), custom_call_target="tpu_custom_call" | custom-call | flops 1000000000 | bytes 1000000 | tf_op jit(solution)/shard_map/gather/pallas_call | solution.py:334
  29.6 3.8 %all-to-all-start.1 = ((f32[8,32,256]{2,1,0:T(8,128)}), f32[8,32,256]{2,1,0:T(8,128)S(1)}, u32[]{:S(2)}, u32[]{:S(2)}) async-start(f32[8,32,256]{2,1,0:T(8,128)} %get-tuple-element.16), calls=%async_computation.1 | async-start | bytes 524288 | tf_op jit(solution)/shard_map/all_to_all | solution.py:469
  33.4 0.0 collective-permute-done.2.refs_3_
  33.4 0.0 collective-permute-done.1.refs_2_
  33.4 0.0 collective-permute-done.refs_1_
  33.4 0.9 collective-permute-start.5
  34.3 1.3 %collective-permute-start.4 = (f32[4,16,256]{2,1,0:T(8,128)S(1)}, f32[4,16,256]{2,1,0:T(8,128)S(1)}, u32[]{:S(2)}, u32[]{:S(2)}) collective-permute-start(f32[4,16,256]{2,1,0:T(8,128)S(1)} %pad_maximum_fusion), channel_id=1, source_target_pairs={{0,2},{1,3},{2,0},{3,1},{4,6},{5,7},{6,4},{7,5},{8,10},{9,11},{10,... | collective-permute-start | bytes 196616 | tf_op jit(solution)/shard_map/ppermute | solution.py:30
  35.6 0.0 collective-permute-start.3
  35.6 1.4 %collective-permute-done.5.refs_6_ = f32[4,16,256]{2,1,0:T(8,128)S(1)} collective-permute-done((f32[4,16,256]{2,1,0:T(8,128)S(1)}, f32[4,16,256]{2,1,0:T(8,128)S(1)}, u32[]{:S(2)}, u32[]{:S(2)}) %collective-permute-start.5) | collective-permute-done | bytes 65568 | tf_op jit(solution)/shard_map/ppermute | solution.py:30
  37.0 1.9 %collective-permute-done.4.refs_5_ = f32[4,16,256]{2,1,0:T(8,128)S(1)} collective-permute-done((f32[4,16,256]{2,1,0:T(8,128)S(1)}, f32[4,16,256]{2,1,0:T(8,128)S(1)}, u32[]{:S(2)}, u32[]{:S(2)}) %collective-permute-start.4) | collective-permute-done | bytes 65568 | tf_op jit(solution)/shard_map/ppermute | solution.py:30
  38.9 1.9 %collective-permute-done.3.refs_4_ = f32[4,16,256]{2,1,0:T(8,128)S(1)} collective-permute-done((f32[4,16,256]{2,1,0:T(8,128)S(1)}, f32[4,16,256]{2,1,0:T(8,128)S(1)}, u32[]{:S(2)}, u32[]{:S(2)}) %collective-permute-start.3) | collective-permute-done | bytes 65568 | tf_op jit(solution)/shard_map/ppermute | solution.py:30
  40.8 0.2 place.1.fi_ref
  41.1 0.0 all-to-all-done.1.zv_ref
  41.1 16.3 %build.1 = (bf16[2048,4096]{1,0:T(8,128)(2,1)S(1)}, bf16[2048,4096]{1,0:T(8,128)(2,1)S(1)}, f32[16,16,256]{2,1,0:T(8,128)S(1)}) custom-call(f32[8,32,256]{2,1,0:T(8,128)S(1)} %all-to-all-done.1.zv_ref, bf16[128,4096]{1,0:T(8,128)(2,1)S(1)} %place.1.fi_ref), custom_call_target="tpu_custom_call" | custom-call | flops 335544320 | bytes 33554432 | tf_op jit(solution)/shard_map/build/pallas_call | solution.py:133
  57.4 10.4 %all_to_all.36.shares_ref = f32[16,16,256]{2,1,0:T(8,128)S(1)} all-to-all(f32[16,16,256]{2,1,0:T(8,128)S(1)} %get-tuple-element.17), channel_id=1, replica_groups=mesh['row_0'=4,'row_1'=2,'col_0'=4,'col_1'=4] {'col_0','col_1'}, dimensions={0} | all-to-all | bytes 524288 | tf_op jit(solution)/shard_map/all_to_all | solution.py:469
  67.8 11.7 %all_to_all.37.v_ref = f32[8,16,256]{2,1,0:T(8,128)S(1)} all-to-all(f32[8,16,256]{2,1,0:T(8,128)S(1)} %get-tuple-element.20), channel_id=1, replica_groups=mesh['row_0'=4,'row_1'=2,'col_0'=4,'col_1'=4] {'row_0','row_1'}, dimensions={0} | all-to-all | bytes 262144 | tf_op jit(solution)/shard_map/all_to_all | solution.py:469
  79.4 5.3 %product.1 = f32[16,16,256]{2,1,0:T(8,128)S(1)} custom-call(f32[8,16,256]{2,1,0:T(8,128)S(1)} %all_to_all.37.v_ref, bf16[2048,4096]{1,0:T(8,128)(2,1)S(1)} %get-tuple-element.21.high_ref, bf16[2048,4096]{1,0:T(8,128)(2,1)S(1)} %get-tuple-element.22.low_ref), custom_call_target="tpu_custom_call" | custom-call | flops 1073741824 | bytes 33554432 | tf_op jit(solution)/shard_map/product/pallas_call | solution.py:167
  84.8 10.2 %all_to_all.38.shares_ref = f32[16,16,256]{2,1,0:T(8,128)S(1)} all-to-all(f32[16,16,256]{2,1,0:T(8,128)S(1)} %product.1), channel_id=1, replica_groups=mesh['row_0'=4,'row_1'=2,'col_0'=4,'col_1'=4] {'col_0','col_1'}, dimensions={0} | all-to-all | bytes 524288 | tf_op jit(solution)/shard_map/all_to_all | solution.py:469
  95.0 0.2 close.1
  95.2 15.1 %all_to_all.39 = f32[128,1,128]{2,1,0:T(1,128)S(1)} all-to-all(f32[128,1,128]{2,1,0:T(1,128)S(1)} %broadcast_in_dim.26), channel_id=1, replica_groups=mesh['row_0'=4,'row_1'=2,'col_0'=4,'col_1'=4] {'row_0','row_1','col_0','..., dimensions={0} | all-to-all | bytes 131072 | tf_op jit(solution)/shard_map/all_to_all | solution.py:469
  110.3 1.4 %finish.1 = (f32[16,256]{1,0:T(8,128)}, f32[16,256]{1,0:T(8,128)}) custom-call(f32[128,128]{1,0:T(8,128)S(1)} %bitcast.16, f32[16,256]{1,0:T(8,128)S(1)} %get-tuple-element.18.v_ref.rhs_ref, f32[16,256]{1,0:T(8,128)S(1)} %get-tuple-element.23.first_ref, f32[16,256]{1,0:T(8,128)S(1)} %get-tuple-element.25.second_ref), custom_call_target="tpu_custom_call" | custom-call | tf_op jit(solution)/shard_map/finish/pallas_call | solution.py:458
  (4 shorter events, 0.1 us)
Async XLA Ops:
  4.4 23.6 %all-to-all-start = ((f32[128,1,640]{2,1,0:T(1,128)}), f32[128,1,640]{2,1,0:T(1,128)S(1)}, u32[]{:S(2)}, u32[]{:S(2)}) async-start(f32[128,1,640]{2,1,0:T(1,128)} %copy.10), calls=%async_computation | async-start | bytes 655360 | tf_op jit(solution)/shard_map/all_to_all | solution.py:469
  15.9 17.5 %collective-permute-start.2 = (f32[1,16,256]{2,1,0:T(8,128)S(1)}, f32[1,16,256]{2,1,0:T(8,128)S(1)}, u32[]{:S(2)}, u32[]{:S(2)}) collective-permute-start(f32[1,16,256]{2,1,0:T(8,128)S(1)} %bitcast.17), channel_id=1, source_target_pairs={{0,12},{4,0},{8,4},{12,8},{1,13},{5,1},{9,5},{13,9},{2,14},{6,2},{... | collective-permute-start | bytes 49160 | tf_op jit(solution)/shard_map/ppermute | solution.py:30
  19.2 14.2 %collective-permute-start.1 = (f32[1,16,256]{2,1,0:T(8,128)S(1)}, f32[1,16,256]{2,1,0:T(8,128)S(1)}, u32[]{:S(2)}, u32[]{:S(2)}) collective-permute-start(f32[1,16,256]{2,1,0:T(8,128)S(1)} %bitcast.18), channel_id=1, source_target_pairs={{0,8},{4,12},{8,0},{12,4},{1,9},{5,13},{9,1},{13,5},{2,10},{6,14},... | collective-permute-start | bytes 49160 | tf_op jit(solution)/shard_map/ppermute | solution.py:30
  19.3 14.1 %collective-permute-start = (f32[1,16,256]{2,1,0:T(8,128)S(1)}, f32[1,16,256]{2,1,0:T(8,128)S(1)}, u32[]{:S(2)}, u32[]{:S(2)}) collective-permute-start(f32[1,16,256]{2,1,0:T(8,128)S(1)} %bitcast.19), channel_id=1, source_target_pairs={{0,4},{4,8},{8,12},{12,0},{1,5},{5,9},{9,13},{13,1},{2,6},{6,10},{... | collective-permute-start | bytes 49160 | tf_op jit(solution)/shard_map/ppermute | solution.py:30
  29.6 11.5 %all-to-all-start.1 = ((f32[8,32,256]{2,1,0:T(8,128)}), f32[8,32,256]{2,1,0:T(8,128)S(1)}, u32[]{:S(2)}, u32[]{:S(2)}) async-start(f32[8,32,256]{2,1,0:T(8,128)} %get-tuple-element.16), calls=%async_computation.1 | async-start | bytes 524288 | tf_op jit(solution)/shard_map/all_to_all | solution.py:469
  33.4 3.6 %collective-permute-start.5 = (f32[4,16,256]{2,1,0:T(8,128)S(1)}, f32[4,16,256]{2,1,0:T(8,128)S(1)}, u32[]{:S(2)}, u32[]{:S(2)}) collective-permute-start(f32[4,16,256]{2,1,0:T(8,128)S(1)} %pad_maximum_fusion), channel_id=1, source_target_pairs={{0,3},{1,0},{2,1},{3,2},{4,7},{5,4},{6,5},{7,6},{8,11},{9,8},{10,9... | collective-permute-start | bytes 196616 | tf_op jit(solution)/shard_map/ppermute | solution.py:30
  34.3 4.6 %collective-permute-start.4 = (f32[4,16,256]{2,1,0:T(8,128)S(1)}, f32[4,16,256]{2,1,0:T(8,128)S(1)}, u32[]{:S(2)}, u32[]{:S(2)}) collective-permute-start(f32[4,16,256]{2,1,0:T(8,128)S(1)} %pad_maximum_fusion), channel_id=1, source_target_pairs={{0,2},{1,3},{2,0},{3,1},{4,6},{5,7},{6,4},{7,5},{8,10},{9,11},{10,... | collective-permute-start | bytes 196616 | tf_op jit(solution)/shard_map/ppermute | solution.py:30
  35.6 5.2 %collective-permute-start.3 = (f32[4,16,256]{2,1,0:T(8,128)S(1)}, f32[4,16,256]{2,1,0:T(8,128)S(1)}, u32[]{:S(2)}, u32[]{:S(2)}) collective-permute-start(f32[4,16,256]{2,1,0:T(8,128)S(1)} %pad_maximum_fusion), channel_id=1, source_target_pairs={{0,1},{1,2},{2,3},{3,0},{4,5},{5,6},{6,7},{7,4},{8,9},{9,10},{10,1... | collective-permute-start | bytes 196616 | tf_op jit(solution)/shard_map/ppermute | solution.py:30

commit v5 on v4

--- a/solution.py
+++ b/solution.py
@@ -68,25 +68,19 @@
     return (squared + (LINEAR * root + CONST)) * jnp.exp2(-root)
 
 
-def split_vector(v_ref, first, vv_ref):
+def split_vector(v_ref, vv_ref):
     width = v_ref.shape[2]
     members = vv_ref.shape[0] // 2
     for r in range(v_ref.shape[0]):
-        high, low = halves(v_ref[r, first : first + members])
+        high, low = halves(v_ref[r])
         columns = slice(r * width, (r + 1) * width)
         vv_ref[:members, columns] = high.astype(jnp.bfloat16)
         vv_ref[members:, columns] = low.astype(jnp.bfloat16)
 
 
-def build_body(
-    zv_ref, fi_ref, high_ref, low_ref, out_ref, fj_ref, vv_ref, acc_ref, ahead_ref
-):
+def build_body(v_ref, fi_ref, fj_ref, high_ref, low_ref, out_ref, vv_ref, acc_ref, ahead_ref):
     members, width = out_ref.shape[1:]
-    feats = zv_ref.shape[1] - members
-    for r in range(zv_ref.shape[0]):
-        block = features(zv_ref[r, :feats] * SCALE, True)
-        fj_ref[r * width : (r + 1) * width, :] = jnp.transpose(block.astype(jnp.bfloat16))
-    split_vector(zv_ref, feats, vv_ref)
+    split_vector(v_ref, vv_ref)
     acc_ref[...] = jnp.zeros_like(acc_ref)
     tall, wide = TALL, WIDE
     tiles, steps = fi_ref.shape[1] // wide, fj_ref.shape[0] // tall
@@ -127,17 +121,16 @@
         out_ref[c] = FACTOR * (acc_ref[:members, columns] + acc_ref[members:, columns])
 
 
-def build_and_product(zv, fi, members):
-    width = zv.shape[2]
-    rows, columns = zv.shape[0] * width, fi.shape[1]
+def build_and_product(v, fi, fj):
+    members, width = v.shape[1:]
+    rows, columns = fj.shape[0], fi.shape[1]
     return pl.pallas_call(
         build_body,
         out_shape=[pltpu.VMEM((rows, columns), jnp.bfloat16)] * 2
         + [jax.ShapeDtypeStruct((columns // width, members, width), jnp.float32)],
-        in_specs=[pl.BlockSpec(memory_space=VMEM)] * 2,
+        in_specs=[pl.BlockSpec(memory_space=VMEM)] * 3,
         out_specs=[pl.BlockSpec(memory_space=VMEM)] * 3,
         scratch_shapes=[
-            pltpu.VMEM((rows, fi.shape[0]), jnp.bfloat16),
             pltpu.VMEM((2 * members, rows), jnp.bfloat16),
             pltpu.VMEM((2 * members, columns), jnp.float32),
             pltpu.VMEM((TALL, WIDE), jnp.float32),
@@ -147,12 +140,12 @@
             flops=40 * rows * columns, bytes_accessed=4 * rows * columns, transcendentals=0
         ),
         name="build",
-    )(zv, fi)
+    )(v, fi, fj)
 
 
 def product_body(v_ref, high_ref, low_ref, out_ref, vv_ref):
     _, members, width = v_ref.shape
-    split_vector(v_ref, 0, vv_ref)
+    split_vector(v_ref, vv_ref)
     vv = vv_ref[...]
     both = jnp.dot(vv, high_ref[...], preferred_element_type=jnp.float32)
     both += jnp.dot(vv, low_ref[...], preferred_element_type=jnp.float32)
@@ -274,37 +267,51 @@
     )(*(pltpu.with_memory_space_constraint(x, HBM) for x in args))
 
 
-def place_body(*refs):
-    pieces, fi_ref = refs[:-1], refs[-1]
+def sources(axes, order):
+    outer, inner = (lax.axis_index(name) for name in axes)
+    sides = [lax.axis_size(name) for name in axes]
+    for by_outer, by_inner in order:
+        source = (outer - by_outer + sides[0]) % sides[0] * sides[1]
+        yield source + (inner - by_inner + sides[1]) % sides[1]
+
+
+def place_body(count, *refs):
+    pieces, (fi_ref, fj_ref) = refs[:-2], refs[-2:]
     width = pieces[0].shape[2]
-    outer, inner = lax.axis_index(COL[0]), lax.axis_index(COL[1])
+    blocks = [(ref, n) for ref in pieces[:count] for n in range(ref.shape[0])]
     sides = [lax.axis_size(name) for name in COL]
-    at = 0
-    for ref in pieces:
-        for n in range(ref.shape[0]):
-            by_inner, by_outer = at // sides[0], at % sides[0]
-            source = (outer - by_outer + sides[0]) % sides[0] * sides[1]
-            source += (inner - by_inner + sides[1]) % sides[1]
-            columns = pl.ds(pl.multiple_of(source * width, width), width)
-            fi_ref[:, columns] = features(ref[n] * SCALE, False).astype(jnp.bfloat16)
-            at += 1
-
-
-def place(pieces):
-    width = pieces[0].shape[2]
-    blocks = sum(piece.shape[0] for piece in pieces)
-    return pl.pallas_call(
-        place_body,
-        out_shape=jax.ShapeDtypeStruct((128, blocks * width), jnp.bfloat16),
-        in_specs=[pl.BlockSpec(memory_space=VMEM)] * len(pieces),
-        out_specs=pl.BlockSpec(memory_space=VMEM),
+    order = [(at % sides[0], at // sides[0]) for at in range(len(blocks))]
+    for (ref, n), source in zip(blocks, sources(COL, order)):
+        columns = pl.ds(pl.multiple_of(source * width, width), width)
+        fi_ref[:, columns] = features(ref[n] * SCALE, False).astype(jnp.bfloat16)
+    blocks = [(ref, n) for ref in pieces[count:] for n in range(ref.shape[0])]
+    sides = [lax.axis_size(name) for name in ROW]
+    order = [(at // sides[1], at % sides[1]) for at in range(len(blocks))]
+    for (ref, n), source in zip(blocks, sources(ROW, order)):
+        rows = pl.ds(pl.multiple_of(source * width, width), width)
+        block = features(ref[n] * SCALE, True)
+        fj_ref[rows, :] = jnp.transpose(block.astype(jnp.bfloat16))
+
+
+def place(row_pieces, column_pieces):
+    width = row_pieces[0].shape[2]
+    rows = sum(piece.shape[0] for piece in row_pieces) * width
+    columns = sum(piece.shape[0] for piece in column_pieces) * width
+    return pl.pallas_call(
+        functools.partial(place_body, len(row_pieces)),
+        out_shape=[
+            jax.ShapeDtypeStruct((128, rows), jnp.bfloat16),
+            jax.ShapeDtypeStruct((columns, 128), jnp.bfloat16),
+        ],
+        in_specs=[pl.BlockSpec(memory_space=VMEM)] * len(row_pieces + column_pieces),
+        out_specs=[pl.BlockSpec(memory_space=VMEM)] * 2,
         compiler_params=pltpu.CompilerParams(vmem_limit_bytes=4 * MIB),
         cost_estimate=pl.CostEstimate(flops=10**9, bytes_accessed=10**6, transcendentals=0),
         name="place",
-    )(*pieces)
-
-
-def gather_body(capacity, slots, message_ref, z_ref, rhs_ref, copies_ref):
+    )(*row_pieces, *column_pieces)
+
+
+def gather_body(capacity, slots, message_ref, rhs_ref, copies_ref):
     devices = message_ref.shape[0]
     members, width = rhs_ref.shape
     lanes = slots * members
@@ -323,26 +330,23 @@
             )
     rhs = total[:members] + (total[members : 2 * members] + total[2 * members :])
     rhs_ref[...] = rhs
-    z = z_ref[...]
     for r in range(copies_ref.shape[0]):
-        copies_ref[r, : z.shape[0]] = z
-        copies_ref[r, z.shape[0] :] = rhs
-
-
-def gather_terms(message, z, members, copies, capacity, slots):
-    feats, width = z.shape
+        copies_ref[r] = rhs
+
+
+def gather_terms(message, shape, copies, capacity, slots):
     return pl.pallas_call(
         functools.partial(gather_body, capacity, slots),
         out_shape=[
-            jax.ShapeDtypeStruct((members, width), jnp.float32),
-            jax.ShapeDtypeStruct((copies, feats + members, width), jnp.float32),
+            jax.ShapeDtypeStruct(shape, jnp.float32),
+            jax.ShapeDtypeStruct((copies,) + shape, jnp.float32),
         ],
-        in_specs=[pl.BlockSpec(memory_space=VMEM)] * 2,
+        in_specs=[pl.BlockSpec(memory_space=VMEM)],
         out_specs=[pl.BlockSpec(memory_space=VMEM)] * 2,
         compiler_params=pltpu.CompilerParams(vmem_limit_bytes=8 * MIB),
         cost_estimate=pl.CostEstimate(flops=10**9, bytes_accessed=10**6, transcendentals=0),
         name="gather",
-    )(message, z)
+    )(message)
 
 
 def total_body(shares_ref, v_ref, nugget_ref, out_ref, copies_ref):
@@ -475,6 +479,7 @@
     devices = lax.axis_size(ALL)
     held, members, cells = patch_values.shape
     slots = patch_weights.shape[1]
+    stations = nugget.shape[0]
     capacity = max(2, 2 * held // devices)
 
     message, z, nugget = terms_of(
@@ -491,12 +496,18 @@
         devices,
         capacity,
     )
-    near = [z[None]] + ring(z[None], COL[0])
-    far = ring(jnp.concatenate(near), COL[1])
-    row_features = place(near + far)
+    own = z[None]
+    row_near = [own] + ring(own, COL[0])
+    row_joined = jnp.concatenate(row_near)
+    column_near = [own] + ring(own, ROW[1])
+    column_joined = jnp.concatenate(column_near)
+    row_far = ring(row_joined, COL[1])
+    column_far = ring(column_joined, ROW[0])
+    fi, fj = place(row_near + row_far, column_near + column_far)
     message = exchange(message, ALL)
-    rhs, copies = gather_terms(message, z, members, lax.axis_size(ROW), capacity, slots)
-    high, low, partial_value = build_and_product(exchange(copies, ROW), row_features, members)
+    rhs, copies = gather_terms(message, (members, stations), lax.axis_size(ROW), capacity, slots)
+    gathered = exchange(copies, ROW)
+    high, low, partial_value = build_and_product(gathered, fi, fj)
     shares = exchange(partial_value, COL)
     first, copies = total_of(shares, rhs, nugget, lax.axis_size(ROW))
     shares = exchange(kernel_product(exchange(copies, ROW), high, low), COL)

time: 112 us -> 112 us (level)
  waiting for transfers between devices: 13.1 us -> 5.14 us
  starting transfers between devices: 21.7 us -> 29.4 us
    ppermute x6 -> x10, starting transfers between devices: 6.39 us -> 12.6 us  [rotate(): return lax.ppermute(x, axis, [(i, (i + by) % size) for i in range(size)])]
    ppermute x6 -> x10, waiting for transfers between devices: 5.21 us -> 0.44 us  [rotate(): return lax.ppermute(x, axis, [(i, (i + by) % size) for i in range(size)])]
    all_to_all x2, waiting for transfers between devices: 7.89 us -> 4.71 us  [exchange(): return lax.all_to_all(pieces, axes, split_axis=0, concat_axis=0, tiled=True)]
    all_to_all x2, starting transfers between devices: 15.3 us -> 16.8 us  [exchange(): return lax.all_to_all(pieces, axes, split_axis=0, concat_axis=0, tiled=True)]
  transfers between devices with their start and end apart: 8 -> 12, of which waited for: 4 -> 3; matrix products, arithmetic and copies ran while one was open for 0% -> 0% of each run, Pallas kernels for 2% -> 2%
where the time goes in v5:
time: 112 us
  blocking collectives  47.4 us (42%)
  starting transfers between devices  29.4 us (26%)
  Pallas kernels  27.9 us (25%)
  waiting for transfers between devices  5.14 us (5%)
  local copies, waits for them, and re-layouts  1.12 us (1%)
    all_to_all x4, blocking collectives, exchange(): return lax.all_to_all(pieces, axes, split_axis=0, concat_axis=0, tiled=True)  47.4 us
    all_to_all x2, starting transfers between devices, exchange(): return lax.all_to_all(pieces, axes, split_axis=0, concat_axis=0, tiled=True)  16.8 us
    pallas_call x1, Pallas kernels, build_and_product(): pl.pallas_call(build_body, out_shape=[pltpu.VMEM((rows, columns), jnp.bfl...  16.2 us
    ppermute x10, starting transfers between devices, rotate(): return lax.ppermute(x, axis, [(i, (i + by) % size) for i in range(size)])  12.6 us
    pallas_call x1, Pallas kernels, kernel_product(): pl.pallas_call(product_body, out_shape=jax.ShapeDtypeStruct((columns // w...  5.34 us
    all_to_all x2, waiting for transfers between devices, exchange(): return lax.all_to_all(pieces, axes, split_axis=0, concat_axis=0, tiled=True)  4.71 us
    pallas_call x1, Pallas kernels, terms_of(): pl.pallas_call(functools.partial(terms_body, capacity), out_shape=[jax.Sh...  2.73 us
  transfers between devices with their start and end apart: 12, of which 3 were waited for; matrix products, arithmetic and copies ran while one was open for 0% of the time, Pallas kernels for 2%

profile of v5, /device:TPU:1, one launch (start us, length us, event | category | flops | bytes accessed | tf_op | source)
XLA Modules:
  0.0 111.8 jit_solution(12572275535141032213)
XLA Ops:
  0.6 2.7 %terms.1 = (f32[128,640]{1,0:T(8,128)S(1)}, f32[16,256]{1,0:T(8,128)S(1)}, f32[1,256]{1,0:T(1,128)S(1)}) custom-call(bf16[4096,128]{1,0:T(8,128)(2,1)} %bitcast.26, bf16[2048,128]{1,0:T(8,128)(2,1)} %bitcast.27, s32[8,256]{1,0:T(8,128)} %bitcast.28, s32[1,256]{1,0:T(1,128)} %bitcast.29, s32[1,256]{1,0:T(1,128)} %bitcast.30, f32[16,256]{1,0:T(8,128)} %refs_5_.1, ...), custom_call_target="tpu_custom_call" | custom-call | flops 1000000000 | bytes 1000000 | tf_op jit(solution)/shard_map/terms/pallas_call | solution.py:252
  3.4 1.1 copy.10
  4.4 11.5 %all-to-all-start = ((f32[128,1,640]{2,1,0:T(1,128)}), f32[128,1,640]{2,1,0:T(1,128)S(1)}, u32[]{:S(2)}, u32[]{:S(2)}) async-start(f32[128,1,640]{2,1,0:T(1,128)} %copy.10), calls=%async_computation | async-start | bytes 655360 | tf_op jit(solution)/shard_map/all_to_all | solution.py:473
  15.9 1.1 %collective-permute-start.6 = (f32[1,16,256]{2,1,0:T(8,128)S(1)}, f32[1,16,256]{2,1,0:T(8,128)S(1)}, u32[]{:S(2)}, u32[]{:S(2)}) collective-permute-start(f32[1,16,256]{2,1,0:T(8,128)S(1)} %bitcast.17), channel_id=1, source_target_pairs={{0,16},{16,0},{1,17},{17,1},{2,18},{18,2},{3,19},{19,3},{4,20},{20... | collective-permute-start | bytes 49160 | tf_op jit(solution)/shard_map/ppermute | solution.py:30
  17.1 2.5 %collective-permute-start.2 = (f32[1,16,256]{2,1,0:T(8,128)S(1)}, f32[1,16,256]{2,1,0:T(8,128)S(1)}, u32[]{:S(2)}, u32[]{:S(2)}) collective-permute-start(f32[1,16,256]{2,1,0:T(8,128)S(1)} %bitcast.18), channel_id=1, source_target_pairs={{0,12},{4,0},{8,4},{12,8},{1,13},{5,1},{9,5},{13,9},{2,14},{6,2},{... | collective-permute-start | bytes 49160 | tf_op jit(solution)/shard_map/ppermute | solution.py:30
  19.6 0.0 collective-permute-start.1
  19.7 0.8 collective-permute-start
  20.5 2.4 %collective-permute-start.9 = (f32[2,16,256]{2,1,0:T(8,128)S(1)}, f32[2,16,256]{2,1,0:T(8,128)S(1)}, u32[]{:S(2)}, u32[]{:S(2)}) collective-permute-start(f32[2,16,256]{2,1,0:T(8,128)S(1)} %pad_maximum_fusion.1), channel_id=1, source_target_pairs={{0,96},{32,0},{64,32},{96,64},{1,97},{33,1},{65,33},{97,65},{2,98}... | collective-permute-start | bytes 98312 | tf_op jit(solution)/shard_map/ppermute | solution.py:30
  23.0 0.5 collective-permute-start.8
  23.5 0.0 collective-permute-done.2.refs_3_
  23.5 0.6 collective-permute-start.7
  24.1 0.2 collective-permute-done.1.refs_2_
  24.3 0.2 collective-permute-done.refs_1_
  24.5 3.2 %collective-permute-start.5 = (f32[4,16,256]{2,1,0:T(8,128)S(1)}, f32[4,16,256]{2,1,0:T(8,128)S(1)}, u32[]{:S(2)}, u32[]{:S(2)}) collective-permute-start(f32[4,16,256]{2,1,0:T(8,128)S(1)} %pad_maximum_fusion), channel_id=1, source_target_pairs={{0,3},{1,0},{2,1},{3,2},{4,7},{5,4},{6,5},{7,6},{8,11},{9,8},{10,9... | collective-permute-start | bytes 196616 | tf_op jit(solution)/shard_map/ppermute | solution.py:30
  27.7 0.4 collective-permute-start.4
  28.2 0.0 all-to-all-done
  28.2 0.0 collective-permute-done.9.refs_11_
  28.2 0.8 collective-permute-start.3
  29.0 1.5 %gather.1 = (f32[16,256]{1,0:T(8,128)S(1)}, f32[8,16,256]{2,1,0:T(8,128)}) custom-call(f32[128,640]{1,0:T(8,128)S(1)} %bitcast.14), custom_call_target="tpu_custom_call" | custom-call | flops 1000000000 | bytes 1000000 | tf_op jit(solution)/shard_map/gather/pallas_call | solution.py:338
  30.5 5.3 %all-to-all-start.1 = ((f32[8,16,256]{2,1,0:T(8,128)}), f32[8,16,256]{2,1,0:T(8,128)S(1)}, u32[]{:S(2)}, u32[]{:S(2)}) async-start(f32[8,16,256]{2,1,0:T(8,128)} %get-tuple-element.17), calls=%async_computation.1 | async-start | bytes 262144 | tf_op jit(solution)/shard_map/all_to_all | solution.py:473
  35.8 0.0 collective-permute-done.5.refs_6_
  35.9 0.0 collective-permute-done.4.refs_5_
  35.9 0.5 place.1
  36.4 4.7 %all-to-all-done.1.v_ref = f32[8,16,256]{2,1,0:T(8,128)S(1)} async-done(((f32[8,16,256]{2,1,0:T(8,128)}), f32[8,16,256]{2,1,0:T(8,128)S(1)}, u32[]{:S(2)}, u32[]{:S(2)}) %all-to-all-start.1) | async-done | bytes 131104 | tf_op jit(solution)/shard_map/all_to_all | solution.py:473
  41.1 16.2 %build.1 = (bf16[2048,4096]{1,0:T(8,128)(2,1)S(1)}, bf16[2048,4096]{1,0:T(8,128)(2,1)S(1)}, f32[16,16,256]{2,1,0:T(8,128)S(1)}) custom-call(f32[8,16,256]{2,1,0:T(8,128)S(1)} %all-to-all-done.1.v_ref, bf16[128,4096]{1,0:T(8,128)(2,1)S(1)} %get-tuple-element.19.fi_ref, bf16[2048,128]{1,0:T(8,128)(2,1)S(1)} %get-tuple-element.20.fj_ref), custom_call_target="tpu_custom_call" | custom-call | flops 335544320 | bytes 33554432 | tf_op jit(solution)/shard_map/build/pallas_call | solution.py:127
  57.3 12.3 %all_to_all.36.shares_ref = f32[16,16,256]{2,1,0:T(8,128)S(1)} all-to-all(f32[16,16,256]{2,1,0:T(8,128)S(1)} %get-tuple-element.21), channel_id=1, replica_groups=mesh['row_0'=4,'row_1'=2,'col_0'=4,'col_1'=4] {'col_0','col_1'}, dimensions={0} | all-to-all | bytes 524288 | tf_op jit(solution)/shard_map/all_to_all | solution.py:473
  69.6 9.9 %all_to_all.37.v_ref = f32[8,16,256]{2,1,0:T(8,128)S(1)} all-to-all(f32[8,16,256]{2,1,0:T(8,128)S(1)} %get-tuple-element.24), channel_id=1, replica_groups=mesh['row_0'=4,'row_1'=2,'col_0'=4,'col_1'=4] {'row_0','row_1'}, dimensions={0} | all-to-all | bytes 262144 | tf_op jit(solution)/shard_map/all_to_all | solution.py:473
  79.5 5.3 %product.1 = f32[16,16,256]{2,1,0:T(8,128)S(1)} custom-call(f32[8,16,256]{2,1,0:T(8,128)S(1)} %all_to_all.37.v_ref, bf16[2048,4096]{1,0:T(8,128)(2,1)S(1)} %get-tuple-element.25.high_ref, bf16[2048,4096]{1,0:T(8,128)(2,1)S(1)} %get-tuple-element.26.low_ref), custom_call_target="tpu_custom_call" | custom-call | flops 1073741824 | bytes 33554432 | tf_op jit(solution)/shard_map/product/pallas_call | solution.py:160
  84.8 10.2 %all_to_all.38.shares_ref = f32[16,16,256]{2,1,0:T(8,128)S(1)} all-to-all(f32[16,16,256]{2,1,0:T(8,128)S(1)} %product.1), channel_id=1, replica_groups=mesh['row_0'=4,'row_1'=2,'col_0'=4,'col_1'=4] {'col_0','col_1'}, dimensions={0} | all-to-all | bytes 524288 | tf_op jit(solution)/shard_map/all_to_all | solution.py:473
  95.0 0.2 close.1
  95.3 15.1 %all_to_all.39 = f32[128,1,128]{2,1,0:T(1,128)S(1)} all-to-all(f32[128,1,128]{2,1,0:T(1,128)S(1)} %broadcast_in_dim.25), channel_id=1, replica_groups=mesh['row_0'=4,'row_1'=2,'col_0'=4,'col_1'=4] {'row_0','row_1','col_0','..., dimensions={0} | all-to-all | bytes 131072 | tf_op jit(solution)/shard_map/all_to_all | solution.py:473
  110.3 1.4 %finish.1 = (f32[16,256]{1,0:T(8,128)}, f32[16,256]{1,0:T(8,128)}) custom-call(f32[128,128]{1,0:T(8,128)S(1)} %bitcast.16, f32[16,256]{1,0:T(8,128)S(1)} %get-tuple-element.22.v_ref.rhs_ref, f32[16,256]{1,0:T(8,128)S(1)} %get-tuple-element.27.first_ref, f32[16,256]{1,0:T(8,128)S(1)} %get-tuple-element.29.second_ref), custom_call_target="tpu_custom_call" | custom-call | tf_op jit(solution)/shard_map/finish/pallas_call | solution.py:462
  (9 shorter events, 0.1 us)
Async XLA Ops:
  4.4 23.7 %all-to-all-start = ((f32[128,1,640]{2,1,0:T(1,128)}), f32[128,1,640]{2,1,0:T(1,128)S(1)}, u32[]{:S(2)}, u32[]{:S(2)}) async-start(f32[128,1,640]{2,1,0:T(1,128)} %copy.10), calls=%async_computation | async-start | bytes 655360 | tf_op jit(solution)/shard_map/all_to_all | solution.py:473
  15.9 4.6 %collective-permute-start.6 = (f32[1,16,256]{2,1,0:T(8,128)S(1)}, f32[1,16,256]{2,1,0:T(8,128)S(1)}, u32[]{:S(2)}, u32[]{:S(2)}) collective-permute-start(f32[1,16,256]{2,1,0:T(8,128)S(1)} %bitcast.17), channel_id=1, source_target_pairs={{0,16},{16,0},{1,17},{17,1},{2,18},{18,2},{3,19},{19,3},{4,20},{20... | collective-permute-start | bytes 49160 | tf_op jit(solution)/shard_map/ppermute | solution.py:30
  17.1 6.4 %collective-permute-start.2 = (f32[1,16,256]{2,1,0:T(8,128)S(1)}, f32[1,16,256]{2,1,0:T(8,128)S(1)}, u32[]{:S(2)}, u32[]{:S(2)}) collective-permute-start(f32[1,16,256]{2,1,0:T(8,128)S(1)} %bitcast.18), channel_id=1, source_target_pairs={{0,12},{4,0},{8,4},{12,8},{1,13},{5,1},{9,5},{13,9},{2,14},{6,2},{... | collective-permute-start | bytes 49160 | tf_op jit(solution)/shard_map/ppermute | solution.py:30
  19.6 4.7 %collective-permute-start.1 = (f32[1,16,256]{2,1,0:T(8,128)S(1)}, f32[1,16,256]{2,1,0:T(8,128)S(1)}, u32[]{:S(2)}, u32[]{:S(2)}) collective-permute-start(f32[1,16,256]{2,1,0:T(8,128)S(1)} %bitcast.19), channel_id=1, source_target_pairs={{0,8},{4,12},{8,0},{12,4},{1,9},{5,13},{9,1},{13,5},{2,10},{6,14},... | collective-permute-start | bytes 49160 | tf_op jit(solution)/shard_map/ppermute | solution.py:30
  19.7 4.9 %collective-permute-start = (f32[1,16,256]{2,1,0:T(8,128)S(1)}, f32[1,16,256]{2,1,0:T(8,128)S(1)}, u32[]{:S(2)}, u32[]{:S(2)}) collective-permute-start(f32[1,16,256]{2,1,0:T(8,128)S(1)} %bitcast.20), channel_id=1, source_target_pairs={{0,4},{4,8},{8,12},{12,0},{1,5},{5,9},{9,13},{13,1},{2,6},{6,10},{... | collective-permute-start | bytes 49160 | tf_op jit(solution)/shard_map/ppermute | solution.py:30
  20.5 7.7 %collective-permute-start.9 = (f32[2,16,256]{2,1,0:T(8,128)S(1)}, f32[2,16,256]{2,1,0:T(8,128)S(1)}, u32[]{:S(2)}, u32[]{:S(2)}) collective-permute-start(f32[2,16,256]{2,1,0:T(8,128)S(1)} %pad_maximum_fusion.1), channel_id=1, source_target_pairs={{0,96},{32,0},{64,32},{96,64},{1,97},{33,1},{65,33},{97,65},{2,98}... | collective-permute-start | bytes 98312 | tf_op jit(solution)/shard_map/ppermute | solution.py:30
  23.0 12.9 %collective-permute-start.8 = (f32[2,16,256]{2,1,0:T(8,128)S(1)}, f32[2,16,256]{2,1,0:T(8,128)S(1)}, u32[]{:S(2)}, u32[]{:S(2)}) collective-permute-start(f32[2,16,256]{2,1,0:T(8,128)S(1)} %pad_maximum_fusion.1), channel_id=1, source_target_pairs={{0,64},{32,96},{64,0},{96,32},{1,65},{33,97},{65,1},{97,33},{2,66}... | collective-permute-start | bytes 98312 | tf_op jit(solution)/shard_map/ppermute | solution.py:30
  23.5 12.3 %collective-permute-start.7 = (f32[2,16,256]{2,1,0:T(8,128)S(1)}, f32[2,16,256]{2,1,0:T(8,128)S(1)}, u32[]{:S(2)}, u32[]{:S(2)}) collective-permute-start(f32[2,16,256]{2,1,0:T(8,128)S(1)} %pad_maximum_fusion.1), channel_id=1, source_target_pairs={{0,32},{32,64},{64,96},{96,0},{1,33},{33,65},{65,97},{97,1},{2,34}... | collective-permute-start | bytes 98312 | tf_op jit(solution)/shard_map/ppermute | solution.py:30
  24.5 11.3 %collective-permute-start.5 = (f32[4,16,256]{2,1,0:T(8,128)S(1)}, f32[4,16,256]{2,1,0:T(8,128)S(1)}, u32[]{:S(2)}, u32[]{:S(2)}) collective-permute-start(f32[4,16,256]{2,1,0:T(8,128)S(1)} %pad_maximum_fusion), channel_id=1, source_target_pairs={{0,3},{1,0},{2,1},{3,2},{4,7},{5,4},{6,5},{7,6},{8,11},{9,8},{10,9... | collective-permute-start | bytes 196616 | tf_op jit(solution)/shard_map/ppermute | solution.py:30
  27.7 8.1 %collective-permute-start.4 = (f32[4,16,256]{2,1,0:T(8,128)S(1)}, f32[4,16,256]{2,1,0:T(8,128)S(1)}, u32[]{:S(2)}, u32[]{:S(2)}) collective-permute-start(f32[4,16,256]{2,1,0:T(8,128)S(1)} %pad_maximum_fusion), channel_id=1, source_target_pairs={{0,2},{1,3},{2,0},{3,1},{4,6},{5,7},{6,4},{7,5},{8,10},{9,11},{10,... | collective-permute-start | bytes 196616 | tf_op jit(solution)/shard_map/ppermute | solution.py:30
  28.2 7.7 %collective-permute-start.3 = (f32[4,16,256]{2,1,0:T(8,128)S(1)}, f32[4,16,256]{2,1,0:T(8,128)S(1)}, u32[]{:S(2)}, u32[]{:S(2)}) collective-permute-start(f32[4,16,256]{2,1,0:T(8,128)S(1)} %pad_maximum_fusion), channel_id=1, source_target_pairs={{0,1},{1,2},{2,3},{3,0},{4,5},{5,6},{6,7},{7,4},{8,9},{9,10},{10,1... | collective-permute-start | bytes 196616 | tf_op jit(solution)/shard_map/ppermute | solution.py:30
  30.5 10.6 %all-to-all-start.1 = ((f32[8,16,256]{2,1,0:T(8,128)}), f32[8,16,256]{2,1,0:T(8,128)S(1)}, u32[]{:S(2)}, u32[]{:S(2)}) async-start(f32[8,16,256]{2,1,0:T(8,128)} %get-tuple-element.17), calls=%async_computation.1 | async-start | bytes 262144 | tf_op jit(solution)/shard_map/all_to_all | solution.py:473

commit v6 on v5

--- a/solution.py
+++ b/solution.py
@@ -19,7 +19,9 @@
 LINEAR = 3.0 / LN2
 CONST = 3.0 / (LN2 * LN2)
 TINY = 1e-30
-TALL, WIDE = 512, 256
+EARLY, TALL, WIDE = 256, 896, 256
+EARLY_COPIES = 4
+VALUE_COPIES = 4
 VMEM = pltpu.MemorySpace.VMEM
 HBM = pltpu.MemorySpace.HBM
 MIB = 1 << 20
@@ -78,12 +80,74 @@
         vv_ref[members:, columns] = low.astype(jnp.bfloat16)
 
 
-def build_body(v_ref, fi_ref, fj_ref, high_ref, low_ref, out_ref, vv_ref, acc_ref, ahead_ref):
+def split_value(squared):
+    value = value_of(squared)
+    high = value.astype(jnp.bfloat16)
+    return high, (value - high.astype(jnp.float32)).astype(jnp.bfloat16)
+
+
+def early_body(fi_ref, fj_ref, high_out_ref, low_out_ref, high_ref, low_ref, sems):
+    tall, columns = high_ref.shape
+    last = slice(fj_ref.shape[0] - tall, fj_ref.shape[0])
+    chunk = columns // EARLY_COPIES
+    copies = []
+    for part in range(EARLY_COPIES):
+        for tile in range(chunk // WIDE):
+            at = slice(part * chunk + tile * WIDE, part * chunk + (tile + 1) * WIDE)
+            squared = jnp.dot(
+                fj_ref[last, :], fi_ref[:, at], preferred_element_type=jnp.float32
+            )
+            high_ref[:, at], low_ref[:, at] = split_value(squared)
+        at = slice(part * chunk, (part + 1) * chunk)
+        for n, (source, target) in enumerate(((high_ref, high_out_ref), (low_ref, low_out_ref))):
+            copy = pltpu.make_async_copy(source.at[:, at], target.at[:, at], sems.at[2 * part + n])
+            copy.start()
+            copies.append(copy)
+    for copy in copies:
+        copy.wait()
+
+
+def build_early(fi, fj):
+    shape = (EARLY, fi.shape[1])
+    return pl.pallas_call(
+        early_body,
+        out_shape=[HBM(shape, jnp.bfloat16)] * 2,
+        in_specs=[pl.BlockSpec(memory_space=VMEM)] * 2,
+        out_specs=[pl.BlockSpec(memory_space=HBM)] * 2,
+        scratch_shapes=[pltpu.VMEM(shape, jnp.bfloat16)] * 2
+        + [pltpu.SemaphoreType.DMA((2 * EARLY_COPIES,))],
+        compiler_params=pltpu.CompilerParams(vmem_limit_bytes=20 * MIB),
+        cost_estimate=pl.CostEstimate(flops=10**9, bytes_accessed=10**6, transcendentals=0),
+        name="early",
+    )(fi, fj)
+
+
+def build_body(
+    v_ref,
+    fi_ref,
+    fj_ref,
+    high_in_ref,
+    low_in_ref,
+    high_ref,
+    low_ref,
+    out_ref,
+    vv_ref,
+    acc_ref,
+    ahead_ref,
+    sems,
+):
     members, width = out_ref.shape[1:]
+    tall, wide = TALL, WIDE
+    tiles, steps = fi_ref.shape[1] // wide, (fj_ref.shape[0] - EARLY) // tall
+    last = slice(fj_ref.shape[0] - EARLY, fj_ref.shape[0])
+    copies = [
+        pltpu.make_async_copy(source, target.at[last, :], sems.at[n])
+        for n, (source, target) in enumerate(((high_in_ref, high_ref), (low_in_ref, low_ref)))
+    ]
+    for copy in copies:
+        copy.start()
     split_vector(v_ref, vv_ref)
     acc_ref[...] = jnp.zeros_like(acc_ref)
-    tall, wide = TALL, WIDE
-    tiles, steps = fi_ref.shape[1] // wide, fj_ref.shape[0] // tall
 
     def place(step, tile):
         rows = pl.ds(pl.multiple_of(step * tall, tall), tall)
@@ -92,6 +156,11 @@
     def squares(step, tile):
         rows, columns = place(step, tile)
         return jnp.dot(fj_ref[rows, :], fi_ref[:, columns], preferred_element_type=jnp.float32)
+
+    def product(vv, high, low):
+        return jnp.dot(vv, high, preferred_element_type=jnp.float32) + jnp.dot(
+            vv, low, preferred_element_type=jnp.float32
+        )
 
     ahead_ref[...] = squares(0, 0)
 
@@ -104,43 +173,42 @@
             else:
                 ahead = squares(jnp.minimum(step + 1, steps - 1), 0)
             rows, columns = place(step, tile)
-            value = value_of(squared)
-            high = value.astype(jnp.bfloat16)
-            low = (value - high.astype(jnp.float32)).astype(jnp.bfloat16)
+            high, low = split_value(squared)
             high_ref[rows, columns] = high
             low_ref[rows, columns] = low
-            vv = vv_ref[:, rows]
-            acc_ref[:, columns] += jnp.dot(
-                vv, high, preferred_element_type=jnp.float32
-            ) + jnp.dot(vv, low, preferred_element_type=jnp.float32)
+            acc_ref[:, columns] += product(vv_ref[:, rows], high, low)
             squared = ahead
         ahead_ref[...] = squared
 
+    for copy in copies:
+        copy.wait()
+    acc = acc_ref[...] + product(vv_ref[:, last], high_ref[last, :], low_ref[last, :])
+    total = FACTOR * (acc[:members] + acc[members:])
     for c in range(out_ref.shape[0]):
-        columns = slice(c * width, (c + 1) * width)
-        out_ref[c] = FACTOR * (acc_ref[:members, columns] + acc_ref[members:, columns])
-
-
-def build_and_product(v, fi, fj):
+        out_ref[c] = total[:, c * width : (c + 1) * width]
+
+
+def build_and_product(v, fi, fj, high, low):
     members, width = v.shape[1:]
     rows, columns = fj.shape[0], fi.shape[1]
     return pl.pallas_call(
         build_body,
         out_shape=[pltpu.VMEM((rows, columns), jnp.bfloat16)] * 2
         + [jax.ShapeDtypeStruct((columns // width, members, width), jnp.float32)],
-        in_specs=[pl.BlockSpec(memory_space=VMEM)] * 3,
+        in_specs=[pl.BlockSpec(memory_space=VMEM)] * 3 + [pl.BlockSpec(memory_space=HBM)] * 2,
         out_specs=[pl.BlockSpec(memory_space=VMEM)] * 3,
         scratch_shapes=[
             pltpu.VMEM((2 * members, rows), jnp.bfloat16),
             pltpu.VMEM((2 * members, columns), jnp.float32),
             pltpu.VMEM((TALL, WIDE), jnp.float32),
+            pltpu.SemaphoreType.DMA((2,)),
         ],
         compiler_params=pltpu.CompilerParams(vmem_limit_bytes=12 * MIB),
         cost_estimate=pl.CostEstimate(
             flops=40 * rows * columns, bytes_accessed=4 * rows * columns, transcendentals=0
         ),
         name="build",
-    )(v, fi, fj)
+    )(v, fi, fj, *(pltpu.with_memory_space_constraint(x, HBM) for x in (high, low)))
 
 
 def product_body(v_ref, high_ref, low_ref, out_ref, vv_ref):
@@ -180,11 +248,12 @@
 def terms_body(capacity, *refs):
     sources, (out_ref, z_ref, nugget_out_ref) = refs[:8], refs[8:11]
     t_ref, held_refs, sems = refs[11], refs[12:20], refs[20]
-    copies = [
-        pltpu.make_async_copy(source, held_ref, sems.at[i])
-        for i, (source, held_ref) in enumerate(zip(sources, held_refs))
-    ]
-    for copy in copies:
+    chunk = sources[0].shape[0] // VALUE_COPIES
+    parts = [slice(i * chunk, (i + 1) * chunk) for i in range(VALUE_COPIES)]
+    pairs = [(sources[0].at[part], held_refs[0].at[part]) for part in parts]
+    pairs = list(zip(sources[1:], held_refs[1:])) + pairs
+    copies = [pltpu.make_async_copy(*pair, sems.at[i]) for i, pair in enumerate(pairs)]
+    for copy in copies[1:7] + copies[:1] + copies[7:]:
         copy.start()
     values_ref, weights_ref, index_ref, count_ref, owner_ref, cov_ref, scale_ref, nugget_ref = held_refs
     slots, held = index_ref.shape
@@ -192,7 +261,7 @@
     lanes = slots * members
     group = 2 * slots
 
-    for copy in copies[2:]:
+    for copy in copies[1:7]:
         copy.wait()
     z_ref[...] = cov_ref[...] / to_column(scale_ref[...], cov_ref.shape[0])
     nugget_out_ref[...] = nugget_ref[...]
@@ -209,18 +278,19 @@
     ranked = [jnp.where(rank == k, 1.0, 0.0) for k in range(capacity)]
     indices = [index * r for r in ranked]
     indices.append(jnp.zeros((lanes - capacity * slots, held), jnp.float32))
-    out_ref[:, capacity * lanes :] = lax.dot_general(
+    out_ref[:, 0, capacity * lanes :] = lax.dot_general(
         mine.astype(jnp.bfloat16),
         jnp.concatenate(indices, axis=0).astype(jnp.bfloat16),
         (((1,), (1,)), ((), ())),
         preferred_element_type=jnp.float32,
     )
 
-    for copy in copies[:2]:
-        copy.wait()
+    copies[0].wait()
     lane = lax.broadcasted_iota(jnp.int32, (slots, lanes), 1)
     own = lane // members == lax.broadcasted_iota(jnp.int32, (slots, lanes), 0)
     for g in range(held // group):
+        if g * group * members % chunk == 0:
+            copies[7 + g * group * members // chunk].wait()
         weights = weights_ref[g * group * slots : (g + 1) * group * slots, :]
         values = values_ref[g * group * members : (g + 1) * group * members, :]
         every = lax.dot_general(
@@ -240,7 +310,7 @@
     for k in range(capacity):
         table = (mine * ranked[k]).astype(jnp.bfloat16)
         placed = jnp.dot(table, payload, preferred_element_type=jnp.float32)
-        out_ref[:, k * lanes : (k + 1) * lanes] = (
+        out_ref[:, 0, k * lanes : (k + 1) * lanes] = (
             placed[:, :lanes] + placed[:, lanes : 2 * lanes]
         ) + placed[:, 2 * lanes :]
 
@@ -252,7 +322,7 @@
     return pl.pallas_call(
         functools.partial(terms_body, capacity),
         out_shape=[
-            jax.ShapeDtypeStruct((devices, (capacity + 1) * lanes), jnp.float32),
+            jax.ShapeDtypeStruct((devices, 1, (capacity + 1) * lanes), jnp.float32),
             jax.ShapeDtypeStruct(covariates.shape, jnp.float32),
             jax.ShapeDtypeStruct(nugget.shape, jnp.float32),
         ],
@@ -260,7 +330,7 @@
         out_specs=[pl.BlockSpec(memory_space=VMEM)] * 3,
         scratch_shapes=[pltpu.VMEM((held, lanes), jnp.float32)]
         + [pltpu.VMEM(x.shape, x.dtype) for x in args]
-        + [pltpu.SemaphoreType.DMA((len(args),))],
+        + [pltpu.SemaphoreType.DMA((len(args) - 1 + VALUE_COPIES,))],
         compiler_params=pltpu.CompilerParams(vmem_limit_bytes=8 * MIB),
         cost_estimate=pl.CostEstimate(flops=10**9, bytes_accessed=10**6, transcendentals=0),
         name="terms",
@@ -315,11 +385,11 @@
     devices = message_ref.shape[0]
     members, width = rhs_ref.shape
     lanes = slots * members
-    index = jnp.transpose(message_ref[:, capacity * lanes :])
+    index = jnp.transpose(message_ref[:, 0, capacity * lanes :])
     station = lax.broadcasted_iota(jnp.int32, (width, devices), 0).astype(jnp.float32)
     total = jnp.zeros((3 * members, width), jnp.float32)
     for k in range(capacity):
-        terms = jnp.transpose(message_ref[:, k * lanes : (k + 1) * lanes])
+        terms = jnp.transpose(message_ref[:, 0, k * lanes : (k + 1) * lanes])
         split = [part.astype(jnp.bfloat16) for part in thirds(terms)]
         for s in range(slots):
             at = k * slots + s
@@ -504,10 +574,11 @@
     row_far = ring(row_joined, COL[1])
     column_far = ring(column_joined, ROW[0])
     fi, fj = place(row_near + row_far, column_near + column_far)
+    high, low = build_early(fi, fj)
     message = exchange(message, ALL)
     rhs, copies = gather_terms(message, (members, stations), lax.axis_size(ROW), capacity, slots)
     gathered = exchange(copies, ROW)
-    high, low, partial_value = build_and_product(gathered, fi, fj)
+    high, low, partial_value = build_and_product(gathered, fi, fj, high, low)
     shares = exchange(partial_value, COL)
     first, copies = total_of(shares, rhs, nugget, lax.axis_size(ROW))
     shares = exchange(kernel_product(exchange(copies, ROW), high, low), COL)

time: 112 us -> 111 us (level)
  waiting for transfers between devices: 5.14 us -> 2.1 us
  Pallas kernels: 27.9 us -> 30.5 us
    all_to_all x2, waiting for transfers between devices: 4.71 us -> 1.66 us  [exchange(): return lax.all_to_all(pieces, axes, split_axis=0, concat_axis=0, tiled=True)]
    pallas_call x0 -> x1, Pallas kernels: none -> 3.04 us  [build_early(): pl.pallas_call(early_body, out_shape=[HBM(shape, jnp.bfloat16)] * 2, in_s...]
    pallas_call x1, Pallas kernels: 16.2 us -> 14.6 us  [build_and_product(): pl.pallas_call(build_body, out_shape=[pltpu.VMEM((rows, columns), jnp.bfl...]
    pallas_call x1, Pallas kernels: 2.73 us -> 3.92 us  [terms_of(): pl.pallas_call(functools.partial(terms_body, capacity), out_shape=[jax.Sh...]
  transfers between devices with their start and end apart: 12 -> 12, of which waited for: 3 -> 3; matrix products, arithmetic and copies ran while one was open for 0% -> 0% of each run, Pallas kernels for 2% -> 5%
where the time goes in v6:
time: 111 us; the launch traced here: 110 us
  blocking collectives  47.4 us (43%)
  Pallas kernels  30.5 us (27%)
  starting transfers between devices  29.4 us (26%)
  waiting for transfers between devices  2.1 us (2%)
    all_to_all x4, blocking collectives, exchange(): return lax.all_to_all(pieces, axes, split_axis=0, concat_axis=0, tiled=True)  47.4 us
    all_to_all x2, starting transfers between devices, exchange(): return lax.all_to_all(pieces, axes, split_axis=0, concat_axis=0, tiled=True)  16.8 us
    pallas_call x1, Pallas kernels, build_and_product(): pl.pallas_call(build_body, out_shape=[pltpu.VMEM((rows, columns), jnp.bfl...  14.6 us
    ppermute x10, starting transfers between devices, rotate(): return lax.ppermute(x, axis, [(i, (i + by) % size) for i in range(size)])  12.6 us
    pallas_call x1, Pallas kernels, kernel_product(): pl.pallas_call(product_body, out_shape=jax.ShapeDtypeStruct((columns // w...  5.34 us
    pallas_call x1, Pallas kernels, terms_of(): pl.pallas_call(functools.partial(terms_body, capacity), out_shape=[jax.Sh...  3.92 us
    pallas_call x1, Pallas kernels, build_early(): pl.pallas_call(early_body, out_shape=[HBM(shape, jnp.bfloat16)] * 2, in_s...  3.04 us
  transfers between devices with their start and end apart: 12, of which 3 were waited for; matrix products, arithmetic and copies ran while one was open for 0% of the time, Pallas kernels for 5%

profile of v6, /device:TPU:1, one launch (start us, length us, event | category | flops | bytes accessed | tf_op | source)
XLA Modules:
  0.0 110.2 jit_solution(5617282772134266354)
XLA Ops:
  0.6 3.9 %terms.1 = (f32[128,1,640]{2,1,0:T(1,128)}, f32[16,256]{1,0:T(8,128)S(1)}, f32[1,256]{1,0:T(1,128)S(1)}) custom-call(bf16[4096,128]{1,0:T(8,128)(2,1)} %bitcast.20, bf16[2048,128]{1,0:T(8,128)(2,1)} %bitcast.21, s32[8,256]{1,0:T(8,128)} %bitcast.22, s32[1,256]{1,0:T(1,128)} %bitcast.23, s32[1,256]{1,0:T(1,128)} %bitcast.24, f32[16,256]{1,0:T(8,128)} %refs_5_.1, ...), custom_call_target="tpu_custom_call" | custom-call | flops 1000000000 | bytes 1000000 | tf_op jit(solution)/shard_map/terms/pallas_call | solution.py:322
  4.6 11.5 %all-to-all-start = ((f32[128,1,640]{2,1,0:T(1,128)}), f32[128,1,640]{2,1,0:T(1,128)S(1)}, u32[]{:S(2)}, u32[]{:S(2)}) async-start(f32[128,1,640]{2,1,0:T(1,128)} %get-tuple-element.18), calls=%async_computation | async-start | bytes 655360 | tf_op jit(solution)/shard_map/all_to_all | solution.py:543
  16.1 1.1 %collective-permute-start.6 = (f32[1,16,256]{2,1,0:T(8,128)S(1)}, f32[1,16,256]{2,1,0:T(8,128)S(1)}, u32[]{:S(2)}, u32[]{:S(2)}) collective-permute-start(f32[1,16,256]{2,1,0:T(8,128)S(1)} %bitcast.11), channel_id=1, source_target_pairs={{0,16},{16,0},{1,17},{17,1},{2,18},{18,2},{3,19},{19,3},{4,20},{20... | collective-permute-start | bytes 49160 | tf_op jit(solution)/shard_map/ppermute | solution.py:32
  17.2 2.5 %collective-permute-start.2 = (f32[1,16,256]{2,1,0:T(8,128)S(1)}, f32[1,16,256]{2,1,0:T(8,128)S(1)}, u32[]{:S(2)}, u32[]{:S(2)}) collective-permute-start(f32[1,16,256]{2,1,0:T(8,128)S(1)} %bitcast.12), channel_id=1, source_target_pairs={{0,12},{4,0},{8,4},{12,8},{1,13},{5,1},{9,5},{13,9},{2,14},{6,2},{... | collective-permute-start | bytes 49160 | tf_op jit(solution)/shard_map/ppermute | solution.py:32
  19.8 0.0 collective-permute-start.1
  19.8 0.8 collective-permute-start
  20.6 0.0 collective-permute-done.6.refs_8_
  20.6 2.4 %collective-permute-start.9 = (f32[2,16,256]{2,1,0:T(8,128)S(1)}, f32[2,16,256]{2,1,0:T(8,128)S(1)}, u32[]{:S(2)}, u32[]{:S(2)}) collective-permute-start(f32[2,16,256]{2,1,0:T(8,128)S(1)} %pad_maximum_fusion.1), channel_id=1, source_target_pairs={{0,96},{32,0},{64,32},{96,64},{1,97},{33,1},{65,33},{97,65},{2,98}... | collective-permute-start | bytes 98312 | tf_op jit(solution)/shard_map/ppermute | solution.py:32
  23.1 0.5 collective-permute-start.8
  23.6 0.0 collective-permute-done.2.refs_3_
  23.6 0.6 collective-permute-start.7
  24.2 0.2 collective-permute-done.1.refs_2_
  24.5 0.2 collective-permute-done.refs_1_
  24.7 3.2 %collective-permute-start.5 = (f32[4,16,256]{2,1,0:T(8,128)S(1)}, f32[4,16,256]{2,1,0:T(8,128)S(1)}, u32[]{:S(2)}, u32[]{:S(2)}) collective-permute-start(f32[4,16,256]{2,1,0:T(8,128)S(1)} %pad_maximum_fusion), channel_id=1, source_target_pairs={{0,3},{1,0},{2,1},{3,2},{4,7},{5,4},{6,5},{7,6},{8,11},{9,8},{10,9... | collective-permute-start | bytes 196616 | tf_op jit(solution)/shard_map/ppermute | solution.py:32
  27.8 0.4 collective-permute-start.4
  28.3 0.0 collective-permute-done.9.refs_11_
  28.3 0.8 collective-permute-start.3
  29.1 1.5 %gather.1 = (f32[16,256]{1,0:T(8,128)S(1)}, f32[8,16,256]{2,1,0:T(8,128)}) custom-call(f32[128,1,640]{2,1,0:T(1,128)S(1)} %all-to-all-done.message_ref), custom_call_target="tpu_custom_call" | custom-call | flops 1000000000 | bytes 1000000 | tf_op jit(solution)/shard_map/gather/pallas_call | solution.py:408
  30.6 5.3 %all-to-all-start.1 = ((f32[8,16,256]{2,1,0:T(8,128)}), f32[8,16,256]{2,1,0:T(8,128)S(1)}, u32[]{:S(2)}, u32[]{:S(2)}) async-start(f32[8,16,256]{2,1,0:T(8,128)} %get-tuple-element.19), calls=%async_computation.1 | async-start | bytes 262144 | tf_op jit(solution)/shard_map/all_to_all | solution.py:543
  35.9 0.0 collective-permute-done.5.refs_6_
  35.9 0.0 collective-permute-done.4.refs_5_
  35.9 0.5 place.1
  36.4 3.0 %early.1 = (bf16[256,4096]{1,0:T(8,128)(2,1)}, bf16[256,4096]{1,0:T(8,128)(2,1)}) custom-call(bf16[128,4096]{1,0:T(8,128)(2,1)S(1)} %get-tuple-element.21.fi_ref, bf16[2048,128]{1,0:T(8,128)(2,1)S(1)} %get-tuple-element.22.fj_ref), custom_call_target="tpu_custom_call" | custom-call | flops 1000000000 | bytes 1000000 | tf_op jit(solution)/shard_map/early/pallas_call | solution.py:112
  39.5 1.7 %all-to-all-done.1.v_ref = f32[8,16,256]{2,1,0:T(8,128)S(1)} async-done(((f32[8,16,256]{2,1,0:T(8,128)}), f32[8,16,256]{2,1,0:T(8,128)S(1)}, u32[]{:S(2)}, u32[]{:S(2)}) %all-to-all-start.1) | async-done | bytes 131104 | tf_op jit(solution)/shard_map/all_to_all | solution.py:543
  41.1 14.6 %build.1 = (bf16[2048,4096]{1,0:T(8,128)(2,1)S(1)}, bf16[2048,4096]{1,0:T(8,128)(2,1)S(1)}, f32[16,16,256]{2,1,0:T(8,128)S(1)}) custom-call(f32[8,16,256]{2,1,0:T(8,128)S(1)} %all-to-all-done.1.v_ref, bf16[128,4096]{1,0:T(8,128)(2,1)S(1)} %get-tuple-element.21.fi_ref, bf16[2048,128]{1,0:T(8,128)(2,1)S(1)} %get-tuple-element.22.fj_ref, ...), custom_call_target="tpu_custom_call" | custom-call | flops 335544320 | bytes 33554432 | tf_op jit(solution)/shard_map/build/pallas_call | solution.py:194
  55.7 12.3 %all_to_all.30.shares_ref = f32[16,16,256]{2,1,0:T(8,128)S(1)} all-to-all(f32[16,16,256]{2,1,0:T(8,128)S(1)} %get-tuple-element.25), channel_id=1, replica_groups=mesh['row_0'=4,'row_1'=2,'col_0'=4,'col_1'=4] {'col_0','col_1'}, dimensions={0} | all-to-all | bytes 524288 | tf_op jit(solution)/shard_map/all_to_all | solution.py:543
  68.0 9.9 %all_to_all.31.v_ref = f32[8,16,256]{2,1,0:T(8,128)S(1)} all-to-all(f32[8,16,256]{2,1,0:T(8,128)S(1)} %get-tuple-element.28), channel_id=1, replica_groups=mesh['row_0'=4,'row_1'=2,'col_0'=4,'col_1'=4] {'row_0','row_1'}, dimensions={0} | all-to-all | bytes 262144 | tf_op jit(solution)/shard_map/all_to_all | solution.py:543
  77.9 5.3 %product.1 = f32[16,16,256]{2,1,0:T(8,128)S(1)} custom-call(f32[8,16,256]{2,1,0:T(8,128)S(1)} %all_to_all.31.v_ref, bf16[2048,4096]{1,0:T(8,128)(2,1)S(1)} %get-tuple-element.29.high_ref, bf16[2048,4096]{1,0:T(8,128)(2,1)S(1)} %get-tuple-element.30.low_ref), custom_call_target="tpu_custom_call" | custom-call | flops 1073741824 | bytes 33554432 | tf_op jit(solution)/shard_map/product/pallas_call | solution.py:228
  83.3 10.2 %all_to_all.32.shares_ref = f32[16,16,256]{2,1,0:T(8,128)S(1)} all-to-all(f32[16,16,256]{2,1,0:T(8,128)S(1)} %product.1), channel_id=1, replica_groups=mesh['row_0'=4,'row_1'=2,'col_0'=4,'col_1'=4] {'col_0','col_1'}, dimensions={0} | all-to-all | bytes 524288 | tf_op jit(solution)/shard_map/all_to_all | solution.py:543
  93.5 0.2 close.1
  93.7 15.1 %all_to_all.33 = f32[128,1,128]{2,1,0:T(1,128)S(1)} all-to-all(f32[128,1,128]{2,1,0:T(1,128)S(1)} %broadcast_in_dim.25), channel_id=1, replica_groups=mesh['row_0'=4,'row_1'=2,'col_0'=4,'col_1'=4] {'row_0','row_1','col_0','..., dimensions={0} | all-to-all | bytes 131072 | tf_op jit(solution)/shard_map/all_to_all | solution.py:543
  108.7 1.4 %finish.1 = (f32[16,256]{1,0:T(8,128)}, f32[16,256]{1,0:T(8,128)}) custom-call(f32[128,128]{1,0:T(8,128)S(1)} %bitcast.10, f32[16,256]{1,0:T(8,128)S(1)} %get-tuple-element.26.v_ref.rhs_ref, f32[16,256]{1,0:T(8,128)S(1)} %get-tuple-element.31.first_ref, f32[16,256]{1,0:T(8,128)S(1)} %get-tuple-element.33.second_ref), custom_call_target="tpu_custom_call" | custom-call | tf_op jit(solution)/shard_map/finish/pallas_call | solution.py:532
  (8 shorter events, 0.1 us)
Async XLA Ops:
  4.6 24.5 %all-to-all-start = ((f32[128,1,640]{2,1,0:T(1,128)}), f32[128,1,640]{2,1,0:T(1,128)S(1)}, u32[]{:S(2)}, u32[]{:S(2)}) async-start(f32[128,1,640]{2,1,0:T(1,128)} %get-tuple-element.18), calls=%async_computation | async-start | bytes 655360 | tf_op jit(solution)/shard_map/all_to_all | solution.py:543
  16.1 4.6 %collective-permute-start.6 = (f32[1,16,256]{2,1,0:T(8,128)S(1)}, f32[1,16,256]{2,1,0:T(8,128)S(1)}, u32[]{:S(2)}, u32[]{:S(2)}) collective-permute-start(f32[1,16,256]{2,1,0:T(8,128)S(1)} %bitcast.11), channel_id=1, source_target_pairs={{0,16},{16,0},{1,17},{17,1},{2,18},{18,2},{3,19},{19,3},{4,20},{20... | collective-permute-start | bytes 49160 | tf_op jit(solution)/shard_map/ppermute | solution.py:32
  17.2 6.4 %collective-permute-start.2 = (f32[1,16,256]{2,1,0:T(8,128)S(1)}, f32[1,16,256]{2,1,0:T(8,128)S(1)}, u32[]{:S(2)}, u32[]{:S(2)}) collective-permute-start(f32[1,16,256]{2,1,0:T(8,128)S(1)} %bitcast.12), channel_id=1, source_target_pairs={{0,12},{4,0},{8,4},{12,8},{1,13},{5,1},{9,5},{13,9},{2,14},{6,2},{... | collective-permute-start | bytes 49160 | tf_op jit(solution)/shard_map/ppermute | solution.py:32
  19.8 4.7 %collective-permute-start.1 = (f32[1,16,256]{2,1,0:T(8,128)S(1)}, f32[1,16,256]{2,1,0:T(8,128)S(1)}, u32[]{:S(2)}, u32[]{:S(2)}) collective-permute-start(f32[1,16,256]{2,1,0:T(8,128)S(1)} %bitcast.13), channel_id=1, source_target_pairs={{0,8},{4,12},{8,0},{12,4},{1,9},{5,13},{9,1},{13,5},{2,10},{6,14},... | collective-permute-start | bytes 49160 | tf_op jit(solution)/shard_map/ppermute | solution.py:32
  19.8 4.9 %collective-permute-start = (f32[1,16,256]{2,1,0:T(8,128)S(1)}, f32[1,16,256]{2,1,0:T(8,128)S(1)}, u32[]{:S(2)}, u32[]{:S(2)}) collective-permute-start(f32[1,16,256]{2,1,0:T(8,128)S(1)} %bitcast.14), channel_id=1, source_target_pairs={{0,4},{4,8},{8,12},{12,0},{1,5},{5,9},{9,13},{13,1},{2,6},{6,10},{... | collective-permute-start | bytes 49160 | tf_op jit(solution)/shard_map/ppermute | solution.py:32
  20.6 7.6 %collective-permute-start.9 = (f32[2,16,256]{2,1,0:T(8,128)S(1)}, f32[2,16,256]{2,1,0:T(8,128)S(1)}, u32[]{:S(2)}, u32[]{:S(2)}) collective-permute-start(f32[2,16,256]{2,1,0:T(8,128)S(1)} %pad_maximum_fusion.1), channel_id=1, source_target_pairs={{0,96},{32,0},{64,32},{96,64},{1,97},{33,1},{65,33},{97,65},{2,98}... | collective-permute-start | bytes 98312 | tf_op jit(solution)/shard_map/ppermute | solution.py:32
  23.1 12.8 %collective-permute-start.8 = (f32[2,16,256]{2,1,0:T(8,128)S(1)}, f32[2,16,256]{2,1,0:T(8,128)S(1)}, u32[]{:S(2)}, u32[]{:S(2)}) collective-permute-start(f32[2,16,256]{2,1,0:T(8,128)S(1)} %pad_maximum_fusion.1), channel_id=1, source_target_pairs={{0,64},{32,96},{64,0},{96,32},{1,65},{33,97},{65,1},{97,33},{2,66}... | collective-permute-start | bytes 98312 | tf_op jit(solution)/shard_map/ppermute | solution.py:32
  23.6 12.2 %collective-permute-start.7 = (f32[2,16,256]{2,1,0:T(8,128)S(1)}, f32[2,16,256]{2,1,0:T(8,128)S(1)}, u32[]{:S(2)}, u32[]{:S(2)}) collective-permute-start(f32[2,16,256]{2,1,0:T(8,128)S(1)} %pad_maximum_fusion.1), channel_id=1, source_target_pairs={{0,32},{32,64},{64,96},{96,0},{1,33},{33,65},{65,97},{97,1},{2,34}... | collective-permute-start | bytes 98312 | tf_op jit(solution)/shard_map/ppermute | solution.py:32
  24.7 11.2 %collective-permute-start.5 = (f32[4,16,256]{2,1,0:T(8,128)S(1)}, f32[4,16,256]{2,1,0:T(8,128)S(1)}, u32[]{:S(2)}, u32[]{:S(2)}) collective-permute-start(f32[4,16,256]{2,1,0:T(8,128)S(1)} %pad_maximum_fusion), channel_id=1, source_target_pairs={{0,3},{1,0},{2,1},{3,2},{4,7},{5,4},{6,5},{7,6},{8,11},{9,8},{10,9... | collective-permute-start | bytes 196616 | tf_op jit(solution)/shard_map/ppermute | solution.py:32
  27.8 8.1 %collective-permute-start.4 = (f32[4,16,256]{2,1,0:T(8,128)S(1)}, f32[4,16,256]{2,1,0:T(8,128)S(1)}, u32[]{:S(2)}, u32[]{:S(2)}) collective-permute-start(f32[4,16,256]{2,1,0:T(8,128)S(1)} %pad_maximum_fusion), channel_id=1, source_target_pairs={{0,2},{1,3},{2,0},{3,1},{4,6},{5,7},{6,4},{7,5},{8,10},{9,11},{10,... | collective-permute-start | bytes 196616 | tf_op jit(solution)/shard_map/ppermute | solution.py:32
  28.3 7.6 %collective-permute-start.3 = (f32[4,16,256]{2,1,0:T(8,128)S(1)}, f32[4,16,256]{2,1,0:T(8,128)S(1)}, u32[]{:S(2)}, u32[]{:S(2)}) collective-permute-start(f32[4,16,256]{2,1,0:T(8,128)S(1)} %pad_maximum_fusion), channel_id=1, source_target_pairs={{0,1},{1,2},{2,3},{3,0},{4,5},{5,6},{6,7},{7,4},{8,9},{9,10},{10,1... | collective-permute-start | bytes 196616 | tf_op jit(solution)/shard_map/ppermute | solution.py:32
  30.6 10.6 %all-to-all-start.1 = ((f32[8,16,256]{2,1,0:T(8,128)}), f32[8,16,256]{2,1,0:T(8,128)S(1)}, u32[]{:S(2)}, u32[]{:S(2)}) async-start(f32[8,16,256]{2,1,0:T(8,128)} %get-tuple-element.19), calls=%async_computation.1 | async-start | bytes 262144 | tf_op jit(solution)/shard_map/all_to_all | solution.py:543

commit v7 on v6

--- a/solution.py
+++ b/solution.py
@@ -80,14 +80,26 @@
         vv_ref[members:, columns] = low.astype(jnp.bfloat16)
 
 
-def split_value(squared):
-    value = value_of(squared)
+def split_value(value):
     high = value.astype(jnp.bfloat16)
     return high, (value - high.astype(jnp.float32)).astype(jnp.bfloat16)
 
 
-def early_body(fi_ref, fj_ref, high_out_ref, low_out_ref, high_ref, low_ref, sems):
-    tall, columns = high_ref.shape
+def half_of(sides, columns):
+    half = sides[0].shape[1]
+    at = columns.start // half
+    return sides[at], slice(columns.start - at * half, columns.stop - at * half)
+
+
+def product(vv, value):
+    high, low = split_value(value)
+    return jnp.dot(vv, high, preferred_element_type=jnp.float32) + jnp.dot(
+        vv, low, preferred_element_type=jnp.float32
+    )
+
+
+def early_body(fi_ref, fj_ref, sent_ref, value_ref, sems):
+    tall, columns = value_ref.shape
     last = slice(fj_ref.shape[0] - tall, fj_ref.shape[0])
     chunk = columns // EARLY_COPIES
     copies = []
@@ -97,12 +109,12 @@
             squared = jnp.dot(
                 fj_ref[last, :], fi_ref[:, at], preferred_element_type=jnp.float32
             )
-            high_ref[:, at], low_ref[:, at] = split_value(squared)
+            value_ref[:, at] = value_of(squared)
         at = slice(part * chunk, (part + 1) * chunk)
-        for n, (source, target) in enumerate(((high_ref, high_out_ref), (low_ref, low_out_ref))):
-            copy = pltpu.make_async_copy(source.at[:, at], target.at[:, at], sems.at[2 * part + n])
-            copy.start()
-            copies.append(copy)
+        copies.append(
+            pltpu.make_async_copy(value_ref.at[:, at], sent_ref.at[:, at], sems.at[part])
+        )
+        copies[-1].start()
     for copy in copies:
         copy.wait()
 
@@ -111,11 +123,13 @@
     shape = (EARLY, fi.shape[1])
     return pl.pallas_call(
         early_body,
-        out_shape=[HBM(shape, jnp.bfloat16)] * 2,
+        out_shape=HBM(shape, jnp.float32),
         in_specs=[pl.BlockSpec(memory_space=VMEM)] * 2,
-        out_specs=[pl.BlockSpec(memory_space=HBM)] * 2,
-        scratch_shapes=[pltpu.VMEM(shape, jnp.bfloat16)] * 2
-        + [pltpu.SemaphoreType.DMA((2 * EARLY_COPIES,))],
+        out_specs=pl.BlockSpec(memory_space=HBM),
+        scratch_shapes=[
+            pltpu.VMEM(shape, jnp.float32),
+            pltpu.SemaphoreType.DMA((EARLY_COPIES,)),
+        ],
         compiler_params=pltpu.CompilerParams(vmem_limit_bytes=20 * MIB),
         cost_estimate=pl.CostEstimate(flops=10**9, bytes_accessed=10**6, transcendentals=0),
         name="early",
@@ -126,10 +140,9 @@
     v_ref,
     fi_ref,
     fj_ref,
-    high_in_ref,
-    low_in_ref,
-    high_ref,
-    low_ref,
+    early_ref,
+    left_ref,
+    right_ref,
     out_ref,
     vv_ref,
     acc_ref,
@@ -140,9 +153,10 @@
     tall, wide = TALL, WIDE
     tiles, steps = fi_ref.shape[1] // wide, (fj_ref.shape[0] - EARLY) // tall
     last = slice(fj_ref.shape[0] - EARLY, fj_ref.shape[0])
+    half = left_ref.shape[1]
     copies = [
-        pltpu.make_async_copy(source, target.at[last, :], sems.at[n])
-        for n, (source, target) in enumerate(((high_in_ref, high_ref), (low_in_ref, low_ref)))
+        pltpu.make_async_copy(early_ref.at[:, :half], left_ref.at[last, :], sems.at[0]),
+        pltpu.make_async_copy(early_ref.at[:, half:], right_ref.at[last, :], sems.at[1]),
     ]
     for copy in copies:
         copy.start()
@@ -156,11 +170,6 @@
     def squares(step, tile):
         rows, columns = place(step, tile)
         return jnp.dot(fj_ref[rows, :], fi_ref[:, columns], preferred_element_type=jnp.float32)
-
-    def product(vv, high, low):
-        return jnp.dot(vv, high, preferred_element_type=jnp.float32) + jnp.dot(
-            vv, low, preferred_element_type=jnp.float32
-        )
 
     ahead_ref[...] = squares(0, 0)
 
@@ -173,29 +182,33 @@
             else:
                 ahead = squares(jnp.minimum(step + 1, steps - 1), 0)
             rows, columns = place(step, tile)
-            high, low = split_value(squared)
-            high_ref[rows, columns] = high
-            low_ref[rows, columns] = low
-            acc_ref[:, columns] += product(vv_ref[:, rows], high, low)
+            value = value_of(squared)
+            side, within = half_of((left_ref, right_ref), columns)
+            side[rows, within] = value
+            acc_ref[:, columns] += product(vv_ref[:, rows], value)
             squared = ahead
         ahead_ref[...] = squared
 
     for copy in copies:
         copy.wait()
-    acc = acc_ref[...] + product(vv_ref[:, last], high_ref[last, :], low_ref[last, :])
-    total = FACTOR * (acc[:members] + acc[members:])
     for c in range(out_ref.shape[0]):
-        out_ref[c] = total[:, c * width : (c + 1) * width]
-
-
-def build_and_product(v, fi, fj, high, low):
+        columns = slice(c * width, (c + 1) * width)
+        side, within = half_of((left_ref, right_ref), columns)
+        acc = acc_ref[:, columns] + product(vv_ref[:, last], side[last, within])
+        out_ref[c] = FACTOR * (acc[:members] + acc[members:])
+
+
+def build_and_product(v, fi, fj, early):
     members, width = v.shape[1:]
     rows, columns = fj.shape[0], fi.shape[1]
     return pl.pallas_call(
         build_body,
-        out_shape=[pltpu.VMEM((rows, columns), jnp.bfloat16)] * 2
-        + [jax.ShapeDtypeStruct((columns // width, members, width), jnp.float32)],
-        in_specs=[pl.BlockSpec(memory_space=VMEM)] * 3 + [pl.BlockSpec(memory_space=HBM)] * 2,
+        out_shape=[
+            pltpu.VMEM((rows, columns // 2), jnp.float32),
+            pltpu.VMEM((rows, columns // 2), jnp.float32),
+            jax.ShapeDtypeStruct((columns // width, members, width), jnp.float32),
+        ],
+        in_specs=[pl.BlockSpec(memory_space=VMEM)] * 3 + [pl.BlockSpec(memory_space=HBM)],
         out_specs=[pl.BlockSpec(memory_space=VMEM)] * 3,
         scratch_shapes=[
             pltpu.VMEM((2 * members, rows), jnp.bfloat16),
@@ -208,23 +221,25 @@
             flops=40 * rows * columns, bytes_accessed=4 * rows * columns, transcendentals=0
         ),
         name="build",
-    )(v, fi, fj, *(pltpu.with_memory_space_constraint(x, HBM) for x in (high, low)))
-
-
-def product_body(v_ref, high_ref, low_ref, out_ref, vv_ref):
-    _, members, width = v_ref.shape
+    )(v, fi, fj, pltpu.with_memory_space_constraint(early, HBM))
+
+
+def product_body(v_ref, left_ref, right_ref, out_ref, vv_ref):
+    count, members, width = v_ref.shape
     split_vector(v_ref, vv_ref)
-    vv = vv_ref[...]
-    both = jnp.dot(vv, high_ref[...], preferred_element_type=jnp.float32)
-    both += jnp.dot(vv, low_ref[...], preferred_element_type=jnp.float32)
-    total = FACTOR * (both[:members] + both[members:])
     for c in range(out_ref.shape[0]):
-        out_ref[c] = total[:, c * width : (c + 1) * width]
-
-
-def kernel_product(v, high, low):
+        columns = slice(c * width, (c + 1) * width)
+        side, within = half_of((left_ref, right_ref), columns)
+        acc = jnp.zeros((2 * members, width), jnp.float32)
+        for r in range(count):
+            rows = slice(r * width, (r + 1) * width)
+            acc += product(vv_ref[:, rows], side[rows, within])
+        out_ref[c] = FACTOR * (acc[:members] + acc[members:])
+
+
+def kernel_product(v, left, right):
     _, members, width = v.shape
-    rows, columns = high.shape
+    rows, columns = left.shape[0], 2 * left.shape[1]
     return pl.pallas_call(
         product_body,
         out_shape=jax.ShapeDtypeStruct((columns // width, members, width), jnp.float32),
@@ -236,7 +251,7 @@
             flops=128 * rows * columns, bytes_accessed=4 * rows * columns, transcendentals=0
         ),
         name="product",
-    )(v, high, low)
+    )(v, left, right)
 
 
 def to_column(row, size):
@@ -479,16 +494,16 @@
     for at, column in enumerate(sums):
         here = lane == row + at * members
         spaced += jnp.where(here, jnp.broadcast_to(column, shape), 0.0)
-    sums_ref[...] = jnp.sum(spaced, axis=0, keepdims=True)
-
-
-def close(shares, rhs, first, nugget):
+    sums_ref[...] = jnp.broadcast_to(jnp.sum(spaced, axis=0, keepdims=True), sums_ref.shape)
+
+
+def close(shares, rhs, first, nugget, devices):
     members = rhs.shape[0]
     return pl.pallas_call(
         close_body,
         out_shape=[
             jax.ShapeDtypeStruct(rhs.shape, jnp.float32),
-            jax.ShapeDtypeStruct((1, 8 * members), jnp.float32),
+            jax.ShapeDtypeStruct((devices, 8 * members), jnp.float32),
         ],
         in_specs=[pl.BlockSpec(memory_space=VMEM)] * 4,
         out_specs=[pl.BlockSpec(memory_space=VMEM)] * 2,
@@ -574,17 +589,16 @@
     row_far = ring(row_joined, COL[1])
     column_far = ring(column_joined, ROW[0])
     fi, fj = place(row_near + row_far, column_near + column_far)
-    high, low = build_early(fi, fj)
+    early = build_early(fi, fj)
     message = exchange(message, ALL)
     rhs, copies = gather_terms(message, (members, stations), lax.axis_size(ROW), capacity, slots)
     gathered = exchange(copies, ROW)
-    high, low, partial_value = build_and_product(gathered, fi, fj, high, low)
+    left, right, partial_value = build_and_product(gathered, fi, fj, early)
     shares = exchange(partial_value, COL)
     first, copies = total_of(shares, rhs, nugget, lax.axis_size(ROW))
-    shares = exchange(kernel_product(exchange(copies, ROW), high, low), COL)
-    second, sums = close(shares, rhs, first, nugget)
-    copies = jnp.broadcast_to(sums[None], (devices,) + sums.shape)
-    sums = exchange(copies, ALL).reshape(devices, sums.shape[1])
+    shares = exchange(kernel_product(exchange(copies, ROW), left, right), COL)
+    second, sums = close(shares, rhs, first, nugget, devices)
+    sums = exchange(sums[:, None, :], ALL)[:, 0, :]
     return finish(sums, rhs, first, second)
 
 

time: 111 us -> 110 us (level)
  Pallas kernels: 30.5 us -> 29.3 us
    pallas_call x2, Pallas kernels: 17.6 us -> 16.2 us  [the longest x1 13.7 us: build_and_product(): pl.pallas_call(build_body, out_shape=[pltpu.VMEM((rows, columns // 2), jn...]
  transfers between devices with their start and end apart: 12 -> 12, of which waited for: 3 -> 3; matrix products, arithmetic and copies ran while one was open for 0% -> 0% of each run, Pallas kernels for 5% -> 4%
where the time goes in v7:
time: 110 us; the launch traced here: 109 us
  blocking collectives  47.4 us (43%)
  starting transfers between devices  29.4 us (27%)
  Pallas kernels  29.3 us (27%)
  waiting for transfers between devices  2.58 us (2%)
    all_to_all x4, blocking collectives, exchange(): return lax.all_to_all(pieces, axes, split_axis=0, concat_axis=0, tiled=True)  47.4 us
    all_to_all x2, starting transfers between devices, exchange(): return lax.all_to_all(pieces, axes, split_axis=0, concat_axis=0, tiled=True)  16.8 us
    pallas_call x1, Pallas kernels, build_and_product(): pl.pallas_call(build_body, out_shape=[pltpu.VMEM((rows, columns // 2), jn...  13.7 us
    ppermute x10, starting transfers between devices, rotate(): return lax.ppermute(x, axis, [(i, (i + by) % size) for i in range(size)])  12.6 us
    pallas_call x1, Pallas kernels, kernel_product(): pl.pallas_call(product_body, out_shape=jax.ShapeDtypeStruct((columns // w...  5.57 us
    pallas_call x1, Pallas kernels, terms_of(): pl.pallas_call(functools.partial(terms_body, capacity), out_shape=[jax.Sh...  3.91 us
    pallas_call x1, Pallas kernels, build_early(): pl.pallas_call(early_body, out_shape=HBM(shape, jnp.float32), in_specs=[p...  2.56 us
  transfers between devices with their start and end apart: 12, of which 3 were waited for; matrix products, arithmetic and copies ran while one was open for 0% of the time, Pallas kernels for 4%

profile of v7, /device:TPU:1, one launch (start us, length us, event | category | flops | bytes accessed | tf_op | source)
XLA Modules:
  0.0 109.4 jit_solution(140517319692790419)
XLA Ops:
  0.6 3.9 %terms.1 = (f32[128,1,640]{2,1,0:T(1,128)}, f32[16,256]{1,0:T(8,128)S(1)}, f32[1,256]{1,0:T(1,128)S(1)}) custom-call(bf16[4096,128]{1,0:T(8,128)(2,1)} %bitcast.22, bf16[2048,128]{1,0:T(8,128)(2,1)} %bitcast.23, s32[8,256]{1,0:T(8,128)} %bitcast.24, s32[1,256]{1,0:T(1,128)} %bitcast.25, s32[1,256]{1,0:T(1,128)} %bitcast.26, f32[16,256]{1,0:T(8,128)} %refs_5_.1, ...), custom_call_target="tpu_custom_call" | custom-call | flops 1000000000 | bytes 1000000 | tf_op jit(solution)/shard_map/terms/pallas_call | solution.py:337
  4.5 11.5 %all-to-all-start = ((f32[128,1,640]{2,1,0:T(1,128)}), f32[128,1,640]{2,1,0:T(1,128)S(1)}, u32[]{:S(2)}, u32[]{:S(2)}) async-start(f32[128,1,640]{2,1,0:T(1,128)} %get-tuple-element.16), calls=%async_computation | async-start | bytes 655360 | tf_op jit(solution)/shard_map/all_to_all | solution.py:558
  16.0 1.1 %collective-permute-start.6 = (f32[1,16,256]{2,1,0:T(8,128)S(1)}, f32[1,16,256]{2,1,0:T(8,128)S(1)}, u32[]{:S(2)}, u32[]{:S(2)}) collective-permute-start(f32[1,16,256]{2,1,0:T(8,128)S(1)} %bitcast.14), channel_id=1, source_target_pairs={{0,16},{16,0},{1,17},{17,1},{2,18},{18,2},{3,19},{19,3},{4,20},{20... | collective-permute-start | bytes 49160 | tf_op jit(solution)/shard_map/ppermute | solution.py:32
  17.2 2.5 %collective-permute-start.2 = (f32[1,16,256]{2,1,0:T(8,128)S(1)}, f32[1,16,256]{2,1,0:T(8,128)S(1)}, u32[]{:S(2)}, u32[]{:S(2)}) collective-permute-start(f32[1,16,256]{2,1,0:T(8,128)S(1)} %bitcast.15), channel_id=1, source_target_pairs={{0,12},{4,0},{8,4},{12,8},{1,13},{5,1},{9,5},{13,9},{2,14},{6,2},{... | collective-permute-start | bytes 49160 | tf_op jit(solution)/shard_map/ppermute | solution.py:32
  19.7 0.0 collective-permute-start.1
  19.8 0.8 collective-permute-start
  20.6 0.0 collective-permute-done.6.refs_8_
  20.6 2.4 %collective-permute-start.9 = (f32[2,16,256]{2,1,0:T(8,128)S(1)}, f32[2,16,256]{2,1,0:T(8,128)S(1)}, u32[]{:S(2)}, u32[]{:S(2)}) collective-permute-start(f32[2,16,256]{2,1,0:T(8,128)S(1)} %pad_maximum_fusion.1), channel_id=1, source_target_pairs={{0,96},{32,0},{64,32},{96,64},{1,97},{33,1},{65,33},{97,65},{2,98}... | collective-permute-start | bytes 98312 | tf_op jit(solution)/shard_map/ppermute | solution.py:32
  23.1 0.5 collective-permute-start.8
  23.6 0.6 collective-permute-start.7
  24.2 0.2 collective-permute-done.1.refs_2_
  24.4 0.2 collective-permute-done.refs_1_
  24.6 3.2 %collective-permute-start.5 = (f32[4,16,256]{2,1,0:T(8,128)S(1)}, f32[4,16,256]{2,1,0:T(8,128)S(1)}, u32[]{:S(2)}, u32[]{:S(2)}) collective-permute-start(f32[4,16,256]{2,1,0:T(8,128)S(1)} %pad_maximum_fusion), channel_id=1, source_target_pairs={{0,3},{1,0},{2,1},{3,2},{4,7},{5,4},{6,5},{7,6},{8,11},{9,8},{10,9... | collective-permute-start | bytes 196616 | tf_op jit(solution)/shard_map/ppermute | solution.py:32
  27.8 0.4 collective-permute-start.4
  28.3 0.0 collective-permute-done.9.refs_11_
  28.3 0.8 collective-permute-start.3
  29.1 1.5 %gather.1 = (f32[16,256]{1,0:T(8,128)S(1)}, f32[8,16,256]{2,1,0:T(8,128)}) custom-call(f32[128,1,640]{2,1,0:T(1,128)S(1)} %all-to-all-done.message_ref), custom_call_target="tpu_custom_call" | custom-call | flops 1000000000 | bytes 1000000 | tf_op jit(solution)/shard_map/gather/pallas_call | solution.py:423
  30.5 5.3 %all-to-all-start.1 = ((f32[8,16,256]{2,1,0:T(8,128)}), f32[8,16,256]{2,1,0:T(8,128)S(1)}, u32[]{:S(2)}, u32[]{:S(2)}) async-start(f32[8,16,256]{2,1,0:T(8,128)} %get-tuple-element.17), calls=%async_computation.1 | async-start | bytes 262144 | tf_op jit(solution)/shard_map/all_to_all | solution.py:558
  35.9 0.0 collective-permute-done.8.refs_10_
  35.9 0.0 collective-permute-done.5.refs_6_
  35.9 0.0 collective-permute-done.3.refs_4_
  35.9 0.5 place.1
  36.4 2.6 %early.1.early_ref = f32[256,4096]{1,0:T(8,128)} custom-call(bf16[128,4096]{1,0:T(8,128)(2,1)S(1)} %get-tuple-element.19.fi_ref, bf16[2048,128]{1,0:T(8,128)(2,1)S(1)} %get-tuple-element.20.fj_ref), custom_call_target="tpu_custom_call" | custom-call | flops 1000000000 | bytes 1000000 | tf_op jit(solution)/shard_map/early/pallas_call | solution.py:124
  39.0 2.1 %all-to-all-done.1.v_ref = f32[8,16,256]{2,1,0:T(8,128)S(1)} async-done(((f32[8,16,256]{2,1,0:T(8,128)}), f32[8,16,256]{2,1,0:T(8,128)S(1)}, u32[]{:S(2)}, u32[]{:S(2)}) %all-to-all-start.1) | async-done | bytes 131104 | tf_op jit(solution)/shard_map/all_to_all | solution.py:558
  41.1 13.7 %build.1 = (f32[2048,2048]{1,0:T(8,128)S(1)}, f32[2048,2048]{1,0:T(8,128)S(1)}, f32[16,16,256]{2,1,0:T(8,128)S(1)}) custom-call(f32[8,16,256]{2,1,0:T(8,128)S(1)} %all-to-all-done.1.v_ref, bf16[128,4096]{1,0:T(8,128)(2,1)S(1)} %get-tuple-element.19.fi_ref, bf16[2048,128]{1,0:T(8,128)(2,1)S(1)} %get-tuple-element.20.fj_ref, f32[256,4096]{1,0:T(8,128)} %early.1.early_ref), custom_call_target="tpu_custom_call" | custom-call | flops 335544320 | bytes 33554432 | tf_op jit(solution)/shard_map/build/pallas_call | solution.py:204
  54.8 12.3 %all_to_all.30.shares_ref = f32[16,16,256]{2,1,0:T(8,128)S(1)} all-to-all(f32[16,16,256]{2,1,0:T(8,128)S(1)} %get-tuple-element.21), channel_id=1, replica_groups=mesh['row_0'=4,'row_1'=2,'col_0'=4,'col_1'=4] {'col_0','col_1'}, dimensions={0} | all-to-all | bytes 524288 | tf_op jit(solution)/shard_map/all_to_all | solution.py:558
  67.1 9.9 %all_to_all.31.v_ref = f32[8,16,256]{2,1,0:T(8,128)S(1)} all-to-all(f32[8,16,256]{2,1,0:T(8,128)S(1)} %get-tuple-element.24), channel_id=1, replica_groups=mesh['row_0'=4,'row_1'=2,'col_0'=4,'col_1'=4] {'row_0','row_1'}, dimensions={0} | all-to-all | bytes 262144 | tf_op jit(solution)/shard_map/all_to_all | solution.py:558
  77.0 5.6 %product.1 = f32[16,16,256]{2,1,0:T(8,128)S(1)} custom-call(f32[8,16,256]{2,1,0:T(8,128)S(1)} %all_to_all.31.v_ref, f32[2048,2048]{1,0:T(8,128)S(1)} %get-tuple-element.25.left_ref, f32[2048,2048]{1,0:T(8,128)S(1)} %get-tuple-element.26.right_ref), custom_call_target="tpu_custom_call" | custom-call | flops 1073741824 | bytes 33554432 | tf_op jit(solution)/shard_map/product/pallas_call | solution.py:243
  82.6 10.2 %all_to_all.32.shares_ref = f32[16,16,256]{2,1,0:T(8,128)S(1)} all-to-all(f32[16,16,256]{2,1,0:T(8,128)S(1)} %product.1), channel_id=1, replica_groups=mesh['row_0'=4,'row_1'=2,'col_0'=4,'col_1'=4] {'col_0','col_1'}, dimensions={0} | all-to-all | bytes 524288 | tf_op jit(solution)/shard_map/all_to_all | solution.py:558
  92.7 0.2 close.1
  92.9 15.1 %all_to_all.33 = f32[128,1,128]{2,1,0:T(1,128)S(1)} all-to-all(f32[128,1,128]{2,1,0:T(1,128)S(1)} %bitcast.13), channel_id=1, replica_groups=mesh['row_0'=4,'row_1'=2,'col_0'=4,'col_1'=4] {'row_0','row_1','col_0','..., dimensions={0} | all-to-all | bytes 131072 | tf_op jit(solution)/shard_map/all_to_all | solution.py:558
  108.0 1.4 %finish.1 = (f32[16,256]{1,0:T(8,128)}, f32[16,256]{1,0:T(8,128)}) custom-call(f32[128,128]{1,0:T(8,128)S(1)} %bitcast.12, f32[16,256]{1,0:T(8,128)S(1)} %get-tuple-element.22.v_ref.rhs_ref, f32[16,256]{1,0:T(8,128)S(1)} %get-tuple-element.27.first_ref, f32[16,256]{1,0:T(8,128)S(1)} %get-tuple-element.29.second_ref), custom_call_target="tpu_custom_call" | custom-call | tf_op jit(solution)/shard_map/finish/pallas_call | solution.py:547
  (7 shorter events, 0.0 us)
Async XLA Ops:
  4.5 24.5 %all-to-all-start = ((f32[128,1,640]{2,1,0:T(1,128)}), f32[128,1,640]{2,1,0:T(1,128)S(1)}, u32[]{:S(2)}, u32[]{:S(2)}) async-start(f32[128,1,640]{2,1,0:T(1,128)} %get-tuple-element.16), calls=%async_computation | async-start | bytes 655360 | tf_op jit(solution)/shard_map/all_to_all | solution.py:558
  16.0 4.6 %collective-permute-start.6 = (f32[1,16,256]{2,1,0:T(8,128)S(1)}, f32[1,16,256]{2,1,0:T(8,128)S(1)}, u32[]{:S(2)}, u32[]{:S(2)}) collective-permute-start(f32[1,16,256]{2,1,0:T(8,128)S(1)} %bitcast.14), channel_id=1, source_target_pairs={{0,16},{16,0},{1,17},{17,1},{2,18},{18,2},{3,19},{19,3},{4,20},{20... | collective-permute-start | bytes 49160 | tf_op jit(solution)/shard_map/ppermute | solution.py:32
  17.2 6.4 %collective-permute-start.2 = (f32[1,16,256]{2,1,0:T(8,128)S(1)}, f32[1,16,256]{2,1,0:T(8,128)S(1)}, u32[]{:S(2)}, u32[]{:S(2)}) collective-permute-start(f32[1,16,256]{2,1,0:T(8,128)S(1)} %bitcast.15), channel_id=1, source_target_pairs={{0,12},{4,0},{8,4},{12,8},{1,13},{5,1},{9,5},{13,9},{2,14},{6,2},{... | collective-permute-start | bytes 49160 | tf_op jit(solution)/shard_map/ppermute | solution.py:32
  19.7 4.7 %collective-permute-start.1 = (f32[1,16,256]{2,1,0:T(8,128)S(1)}, f32[1,16,256]{2,1,0:T(8,128)S(1)}, u32[]{:S(2)}, u32[]{:S(2)}) collective-permute-start(f32[1,16,256]{2,1,0:T(8,128)S(1)} %bitcast.16), channel_id=1, source_target_pairs={{0,8},{4,12},{8,0},{12,4},{1,9},{5,13},{9,1},{13,5},{2,10},{6,14},... | collective-permute-start | bytes 49160 | tf_op jit(solution)/shard_map/ppermute | solution.py:32
  19.8 4.9 %collective-permute-start = (f32[1,16,256]{2,1,0:T(8,128)S(1)}, f32[1,16,256]{2,1,0:T(8,128)S(1)}, u32[]{:S(2)}, u32[]{:S(2)}) collective-permute-start(f32[1,16,256]{2,1,0:T(8,128)S(1)} %bitcast.17), channel_id=1, source_target_pairs={{0,4},{4,8},{8,12},{12,0},{1,5},{5,9},{9,13},{13,1},{2,6},{6,10},{... | collective-permute-start | bytes 49160 | tf_op jit(solution)/shard_map/ppermute | solution.py:32
  20.6 7.6 %collective-permute-start.9 = (f32[2,16,256]{2,1,0:T(8,128)S(1)}, f32[2,16,256]{2,1,0:T(8,128)S(1)}, u32[]{:S(2)}, u32[]{:S(2)}) collective-permute-start(f32[2,16,256]{2,1,0:T(8,128)S(1)} %pad_maximum_fusion.1), channel_id=1, source_target_pairs={{0,96},{32,0},{64,32},{96,64},{1,97},{33,1},{65,33},{97,65},{2,98}... | collective-permute-start | bytes 98312 | tf_op jit(solution)/shard_map/ppermute | solution.py:32
  23.1 12.8 %collective-permute-start.8 = (f32[2,16,256]{2,1,0:T(8,128)S(1)}, f32[2,16,256]{2,1,0:T(8,128)S(1)}, u32[]{:S(2)}, u32[]{:S(2)}) collective-permute-start(f32[2,16,256]{2,1,0:T(8,128)S(1)} %pad_maximum_fusion.1), channel_id=1, source_target_pairs={{0,64},{32,96},{64,0},{96,32},{1,65},{33,97},{65,1},{97,33},{2,66}... | collective-permute-start | bytes 98312 | tf_op jit(solution)/shard_map/ppermute | solution.py:32
  23.6 12.2 %collective-permute-start.7 = (f32[2,16,256]{2,1,0:T(8,128)S(1)}, f32[2,16,256]{2,1,0:T(8,128)S(1)}, u32[]{:S(2)}, u32[]{:S(2)}) collective-permute-start(f32[2,16,256]{2,1,0:T(8,128)S(1)} %pad_maximum_fusion.1), channel_id=1, source_target_pairs={{0,32},{32,64},{64,96},{96,0},{1,33},{33,65},{65,97},{97,1},{2,34}... | collective-permute-start | bytes 98312 | tf_op jit(solution)/shard_map/ppermute | solution.py:32
  24.6 11.2 %collective-permute-start.5 = (f32[4,16,256]{2,1,0:T(8,128)S(1)}, f32[4,16,256]{2,1,0:T(8,128)S(1)}, u32[]{:S(2)}, u32[]{:S(2)}) collective-permute-start(f32[4,16,256]{2,1,0:T(8,128)S(1)} %pad_maximum_fusion), channel_id=1, source_target_pairs={{0,3},{1,0},{2,1},{3,2},{4,7},{5,4},{6,5},{7,6},{8,11},{9,8},{10,9... | collective-permute-start | bytes 196616 | tf_op jit(solution)/shard_map/ppermute | solution.py:32
  27.8 8.1 %collective-permute-start.4 = (f32[4,16,256]{2,1,0:T(8,128)S(1)}, f32[4,16,256]{2,1,0:T(8,128)S(1)}, u32[]{:S(2)}, u32[]{:S(2)}) collective-permute-start(f32[4,16,256]{2,1,0:T(8,128)S(1)} %pad_maximum_fusion), channel_id=1, source_target_pairs={{0,2},{1,3},{2,0},{3,1},{4,6},{5,7},{6,4},{7,5},{8,10},{9,11},{10,... | collective-permute-start | bytes 196616 | tf_op jit(solution)/shard_map/ppermute | solution.py:32
  28.3 7.6 %collective-permute-start.3 = (f32[4,16,256]{2,1,0:T(8,128)S(1)}, f32[4,16,256]{2,1,0:T(8,128)S(1)}, u32[]{:S(2)}, u32[]{:S(2)}) collective-permute-start(f32[4,16,256]{2,1,0:T(8,128)S(1)} %pad_maximum_fusion), channel_id=1, source_target_pairs={{0,1},{1,2},{2,3},{3,0},{4,5},{5,6},{6,7},{7,4},{8,9},{9,10},{10,1... | collective-permute-start | bytes 196616 | tf_op jit(solution)/shard_map/ppermute | solution.py:32
  30.5 10.6 %all-to-all-start.1 = ((f32[8,16,256]{2,1,0:T(8,128)}), f32[8,16,256]{2,1,0:T(8,128)S(1)}, u32[]{:S(2)}, u32[]{:S(2)}) async-start(f32[8,16,256]{2,1,0:T(8,128)} %get-tuple-element.17), calls=%async_computation.1 | async-start | bytes 262144 | tf_op jit(solution)/shard_map/all_to_all | solution.py:558

commit v8 on v7

--- a/solution.py
+++ b/solution.py
@@ -512,7 +512,9 @@
     )(shares, rhs, first, nugget)
 
 
-def finish_body(sums_ref, rhs_ref, first_ref, second_ref, solved_ref, residual_ref):
+def finish_body(
+    sums_ref, rhs_ref, first_ref, second_ref, solved_out_ref, residual_out_ref, held_ref, sems
+):
     rhs, first, second = rhs_ref[...], first_ref[...], second_ref[...]
     members = rhs.shape[0]
     norm, energy, rr, rf, ff, ra, rs, fs = (
@@ -539,8 +541,16 @@
     residual = rhs - alpha0 * first
     direction = residual + ratio * rhs
     along = (first - alpha0 * second) + ratio * first
-    solved_ref[...] = alpha0 * rhs + alpha1 * direction
-    residual_ref[...] = residual - alpha1 * along
+    held_ref[0] = alpha0 * rhs + alpha1 * direction
+    held_ref[1] = residual - alpha1 * along
+    copies = [
+        pltpu.make_async_copy(held_ref.at[n], target, sems.at[n])
+        for n, target in enumerate((solved_out_ref, residual_out_ref))
+    ]
+    for copy in copies:
+        copy.start()
+    for copy in copies:
+        copy.wait()
 
 
 def finish(sums, rhs, first, second):
@@ -548,7 +558,11 @@
         finish_body,
         out_shape=[jax.ShapeDtypeStruct(rhs.shape, jnp.float32)] * 2,
         in_specs=[pl.BlockSpec(memory_space=VMEM)] * 4,
-        out_specs=[pl.BlockSpec(memory_space=VMEM)] * 2,
+        out_specs=[pl.BlockSpec(memory_space=HBM)] * 2,
+        scratch_shapes=[
+            pltpu.VMEM((2,) + rhs.shape, jnp.float32),
+            pltpu.SemaphoreType.DMA((2,)),
+        ],
         compiler_params=pltpu.CompilerParams(vmem_limit_bytes=4 * MIB),
         name="finish",
     )(sums, rhs, first, second)

time: 110 us -> 110 us (level)
  no operation moved by 1% of the time
where the time goes in v8:
time: 110 us
  blocking collectives  47.4 us (43%)
  starting transfers between devices  29.4 us (27%)
  Pallas kernels  29.3 us (27%)
  waiting for transfers between devices  2.58 us (2%)
    all_to_all x4, blocking collectives, exchange(): return lax.all_to_all(pieces, axes, split_axis=0, concat_axis=0, tiled=True)  47.4 us
    all_to_all x2, starting transfers between devices, exchange(): return lax.all_to_all(pieces, axes, split_axis=0, concat_axis=0, tiled=True)  16.8 us
    pallas_call x1, Pallas kernels, build_and_product(): pl.pallas_call(build_body, out_shape=[pltpu.VMEM((rows, columns // 2), jn...  13.7 us
    ppermute x10, starting transfers between devices, rotate(): return lax.ppermute(x, axis, [(i, (i + by) % size) for i in range(size)])  12.6 us
    pallas_call x1, Pallas kernels, kernel_product(): pl.pallas_call(product_body, out_shape=jax.ShapeDtypeStruct((columns // w...  5.57 us
    pallas_call x1, Pallas kernels, terms_of(): pl.pallas_call(functools.partial(terms_body, capacity), out_shape=[jax.Sh...  3.91 us
    pallas_call x1, Pallas kernels, build_early(): pl.pallas_call(early_body, out_shape=HBM(shape, jnp.float32), in_specs=[p...  2.56 us
  transfers between devices with their start and end apart: 12, of which 3 were waited for; matrix products, arithmetic and copies ran while one was open for 0% of the time, Pallas kernels for 4%

profile of v8, /device:TPU:1, one launch (start us, length us, event | category | flops | bytes accessed | tf_op | source)
XLA Modules:
  0.0 109.6 jit_solution(14037308872202376368)
XLA Ops:
  0.6 3.9 %terms.1 = (f32[128,1,640]{2,1,0:T(1,128)}, f32[16,256]{1,0:T(8,128)S(1)}, f32[1,256]{1,0:T(1,128)S(1)}) custom-call(bf16[4096,128]{1,0:T(8,128)(2,1)} %bitcast.22, bf16[2048,128]{1,0:T(8,128)(2,1)} %bitcast.23, s32[8,256]{1,0:T(8,128)} %bitcast.24, s32[1,256]{1,0:T(1,128)} %bitcast.25, s32[1,256]{1,0:T(1,128)} %bitcast.26, f32[16,256]{1,0:T(8,128)} %refs_5_.1, ...), custom_call_target="tpu_custom_call" | custom-call | flops 1000000000 | bytes 1000000 | tf_op jit(solution)/shard_map/terms/pallas_call | solution.py:337
  4.5 11.5 %all-to-all-start = ((f32[128,1,640]{2,1,0:T(1,128)}), f32[128,1,640]{2,1,0:T(1,128)S(1)}, u32[]{:S(2)}, u32[]{:S(2)}) async-start(f32[128,1,640]{2,1,0:T(1,128)} %get-tuple-element.16), calls=%async_computation | async-start | bytes 655360 | tf_op jit(solution)/shard_map/all_to_all | solution.py:572
  16.0 1.1 %collective-permute-start.6 = (f32[1,16,256]{2,1,0:T(8,128)S(1)}, f32[1,16,256]{2,1,0:T(8,128)S(1)}, u32[]{:S(2)}, u32[]{:S(2)}) collective-permute-start(f32[1,16,256]{2,1,0:T(8,128)S(1)} %bitcast.14), channel_id=1, source_target_pairs={{0,16},{16,0},{1,17},{17,1},{2,18},{18,2},{3,19},{19,3},{4,20},{20... | collective-permute-start | bytes 49160 | tf_op jit(solution)/shard_map/ppermute | solution.py:32
  17.2 2.5 %collective-permute-start.2 = (f32[1,16,256]{2,1,0:T(8,128)S(1)}, f32[1,16,256]{2,1,0:T(8,128)S(1)}, u32[]{:S(2)}, u32[]{:S(2)}) collective-permute-start(f32[1,16,256]{2,1,0:T(8,128)S(1)} %bitcast.15), channel_id=1, source_target_pairs={{0,12},{4,0},{8,4},{12,8},{1,13},{5,1},{9,5},{13,9},{2,14},{6,2},{... | collective-permute-start | bytes 49160 | tf_op jit(solution)/shard_map/ppermute | solution.py:32
  19.7 0.0 collective-permute-start.1
  19.8 0.8 collective-permute-start
  20.6 0.0 collective-permute-done.6.refs_8_
  20.6 2.4 %collective-permute-start.9 = (f32[2,16,256]{2,1,0:T(8,128)S(1)}, f32[2,16,256]{2,1,0:T(8,128)S(1)}, u32[]{:S(2)}, u32[]{:S(2)}) collective-permute-start(f32[2,16,256]{2,1,0:T(8,128)S(1)} %pad_maximum_fusion.1), channel_id=1, source_target_pairs={{0,96},{32,0},{64,32},{96,64},{1,97},{33,1},{65,33},{97,65},{2,98}... | collective-permute-start | bytes 98312 | tf_op jit(solution)/shard_map/ppermute | solution.py:32
  23.1 0.5 collective-permute-start.8
  23.6 0.6 collective-permute-start.7
  24.2 0.2 collective-permute-done.1.refs_2_
  24.4 0.2 collective-permute-done.refs_1_
  24.6 3.2 %collective-permute-start.5 = (f32[4,16,256]{2,1,0:T(8,128)S(1)}, f32[4,16,256]{2,1,0:T(8,128)S(1)}, u32[]{:S(2)}, u32[]{:S(2)}) collective-permute-start(f32[4,16,256]{2,1,0:T(8,128)S(1)} %pad_maximum_fusion), channel_id=1, source_target_pairs={{0,3},{1,0},{2,1},{3,2},{4,7},{5,4},{6,5},{7,6},{8,11},{9,8},{10,9... | collective-permute-start | bytes 196616 | tf_op jit(solution)/shard_map/ppermute | solution.py:32
  27.8 0.4 collective-permute-start.4
  28.3 0.0 collective-permute-done.9.refs_11_
  28.3 0.8 collective-permute-start.3
  29.1 1.5 %gather.1 = (f32[16,256]{1,0:T(8,128)S(1)}, f32[8,16,256]{2,1,0:T(8,128)}) custom-call(f32[128,1,640]{2,1,0:T(1,128)S(1)} %all-to-all-done.message_ref), custom_call_target="tpu_custom_call" | custom-call | flops 1000000000 | bytes 1000000 | tf_op jit(solution)/shard_map/gather/pallas_call | solution.py:423
  30.5 5.3 %all-to-all-start.1 = ((f32[8,16,256]{2,1,0:T(8,128)}), f32[8,16,256]{2,1,0:T(8,128)S(1)}, u32[]{:S(2)}, u32[]{:S(2)}) async-start(f32[8,16,256]{2,1,0:T(8,128)} %get-tuple-element.17), calls=%async_computation.1 | async-start | bytes 262144 | tf_op jit(solution)/shard_map/all_to_all | solution.py:572
  35.9 0.0 collective-permute-done.8.refs_10_
  35.9 0.0 collective-permute-done.5.refs_6_
  35.9 0.0 collective-permute-done.3.refs_4_
  35.9 0.5 place.1
  36.4 2.6 %early.1.early_ref = f32[256,4096]{1,0:T(8,128)} custom-call(bf16[128,4096]{1,0:T(8,128)(2,1)S(1)} %get-tuple-element.19.fi_ref, bf16[2048,128]{1,0:T(8,128)(2,1)S(1)} %get-tuple-element.20.fj_ref), custom_call_target="tpu_custom_call" | custom-call | flops 1000000000 | bytes 1000000 | tf_op jit(solution)/shard_map/early/pallas_call | solution.py:124
  39.0 2.1 %all-to-all-done.1.v_ref = f32[8,16,256]{2,1,0:T(8,128)S(1)} async-done(((f32[8,16,256]{2,1,0:T(8,128)}), f32[8,16,256]{2,1,0:T(8,128)S(1)}, u32[]{:S(2)}, u32[]{:S(2)}) %all-to-all-start.1) | async-done | bytes 131104 | tf_op jit(solution)/shard_map/all_to_all | solution.py:572
  41.1 13.7 %build.1 = (f32[2048,2048]{1,0:T(8,128)S(1)}, f32[2048,2048]{1,0:T(8,128)S(1)}, f32[16,16,256]{2,1,0:T(8,128)S(1)}) custom-call(f32[8,16,256]{2,1,0:T(8,128)S(1)} %all-to-all-done.1.v_ref, bf16[128,4096]{1,0:T(8,128)(2,1)S(1)} %get-tuple-element.19.fi_ref, bf16[2048,128]{1,0:T(8,128)(2,1)S(1)} %get-tuple-element.20.fj_ref, f32[256,4096]{1,0:T(8,128)} %early.1.early_ref), custom_call_target="tpu_custom_call" | custom-call | flops 335544320 | bytes 33554432 | tf_op jit(solution)/shard_map/build/pallas_call | solution.py:204
  54.8 12.3 %all_to_all.30.shares_ref = f32[16,16,256]{2,1,0:T(8,128)S(1)} all-to-all(f32[16,16,256]{2,1,0:T(8,128)S(1)} %get-tuple-element.21), channel_id=1, replica_groups=mesh['row_0'=4,'row_1'=2,'col_0'=4,'col_1'=4] {'col_0','col_1'}, dimensions={0} | all-to-all | bytes 524288 | tf_op jit(solution)/shard_map/all_to_all | solution.py:572
  67.1 9.9 %all_to_all.31.v_ref = f32[8,16,256]{2,1,0:T(8,128)S(1)} all-to-all(f32[8,16,256]{2,1,0:T(8,128)S(1)} %get-tuple-element.24), channel_id=1, replica_groups=mesh['row_0'=4,'row_1'=2,'col_0'=4,'col_1'=4] {'row_0','row_1'}, dimensions={0} | all-to-all | bytes 262144 | tf_op jit(solution)/shard_map/all_to_all | solution.py:572
  77.0 5.6 %product.1 = f32[16,16,256]{2,1,0:T(8,128)S(1)} custom-call(f32[8,16,256]{2,1,0:T(8,128)S(1)} %all_to_all.31.v_ref, f32[2048,2048]{1,0:T(8,128)S(1)} %get-tuple-element.25.left_ref, f32[2048,2048]{1,0:T(8,128)S(1)} %get-tuple-element.26.right_ref), custom_call_target="tpu_custom_call" | custom-call | flops 1073741824 | bytes 33554432 | tf_op jit(solution)/shard_map/product/pallas_call | solution.py:243
  82.6 10.2 %all_to_all.32.shares_ref = f32[16,16,256]{2,1,0:T(8,128)S(1)} all-to-all(f32[16,16,256]{2,1,0:T(8,128)S(1)} %product.1), channel_id=1, replica_groups=mesh['row_0'=4,'row_1'=2,'col_0'=4,'col_1'=4] {'col_0','col_1'}, dimensions={0} | all-to-all | bytes 524288 | tf_op jit(solution)/shard_map/all_to_all | solution.py:572
  92.7 0.2 close.1
  92.9 15.1 %all_to_all.33 = f32[128,1,128]{2,1,0:T(1,128)S(1)} all-to-all(f32[128,1,128]{2,1,0:T(1,128)S(1)} %bitcast.13), channel_id=1, replica_groups=mesh['row_0'=4,'row_1'=2,'col_0'=4,'col_1'=4] {'row_0','row_1','col_0','..., dimensions={0} | all-to-all | bytes 131072 | tf_op jit(solution)/shard_map/all_to_all | solution.py:572
  108.0 1.4 %finish.1 = (f32[16,256]{1,0:T(8,128)}, f32[16,256]{1,0:T(8,128)}) custom-call(f32[128,128]{1,0:T(8,128)S(1)} %bitcast.12, f32[16,256]{1,0:T(8,128)S(1)} %get-tuple-element.22.v_ref.rhs_ref, f32[16,256]{1,0:T(8,128)S(1)} %get-tuple-element.27.first_ref, f32[16,256]{1,0:T(8,128)S(1)} %get-tuple-element.29.second_ref), custom_call_target="tpu_custom_call" | custom-call | tf_op jit(solution)/shard_map/finish/pallas_call | solution.py:557
  (7 shorter events, 0.0 us)
Async XLA Ops:
  4.5 24.5 %all-to-all-start = ((f32[128,1,640]{2,1,0:T(1,128)}), f32[128,1,640]{2,1,0:T(1,128)S(1)}, u32[]{:S(2)}, u32[]{:S(2)}) async-start(f32[128,1,640]{2,1,0:T(1,128)} %get-tuple-element.16), calls=%async_computation | async-start | bytes 655360 | tf_op jit(solution)/shard_map/all_to_all | solution.py:572
  16.0 4.6 %collective-permute-start.6 = (f32[1,16,256]{2,1,0:T(8,128)S(1)}, f32[1,16,256]{2,1,0:T(8,128)S(1)}, u32[]{:S(2)}, u32[]{:S(2)}) collective-permute-start(f32[1,16,256]{2,1,0:T(8,128)S(1)} %bitcast.14), channel_id=1, source_target_pairs={{0,16},{16,0},{1,17},{17,1},{2,18},{18,2},{3,19},{19,3},{4,20},{20... | collective-permute-start | bytes 49160 | tf_op jit(solution)/shard_map/ppermute | solution.py:32
  17.2 6.4 %collective-permute-start.2 = (f32[1,16,256]{2,1,0:T(8,128)S(1)}, f32[1,16,256]{2,1,0:T(8,128)S(1)}, u32[]{:S(2)}, u32[]{:S(2)}) collective-permute-start(f32[1,16,256]{2,1,0:T(8,128)S(1)} %bitcast.15), channel_id=1, source_target_pairs={{0,12},{4,0},{8,4},{12,8},{1,13},{5,1},{9,5},{13,9},{2,14},{6,2},{... | collective-permute-start | bytes 49160 | tf_op jit(solution)/shard_map/ppermute | solution.py:32
  19.7 4.7 %collective-permute-start.1 = (f32[1,16,256]{2,1,0:T(8,128)S(1)}, f32[1,16,256]{2,1,0:T(8,128)S(1)}, u32[]{:S(2)}, u32[]{:S(2)}) collective-permute-start(f32[1,16,256]{2,1,0:T(8,128)S(1)} %bitcast.16), channel_id=1, source_target_pairs={{0,8},{4,12},{8,0},{12,4},{1,9},{5,13},{9,1},{13,5},{2,10},{6,14},... | collective-permute-start | bytes 49160 | tf_op jit(solution)/shard_map/ppermute | solution.py:32
  19.8 4.9 %collective-permute-start = (f32[1,16,256]{2,1,0:T(8,128)S(1)}, f32[1,16,256]{2,1,0:T(8,128)S(1)}, u32[]{:S(2)}, u32[]{:S(2)}) collective-permute-start(f32[1,16,256]{2,1,0:T(8,128)S(1)} %bitcast.17), channel_id=1, source_target_pairs={{0,4},{4,8},{8,12},{12,0},{1,5},{5,9},{9,13},{13,1},{2,6},{6,10},{... | collective-permute-start | bytes 49160 | tf_op jit(solution)/shard_map/ppermute | solution.py:32
  20.6 7.6 %collective-permute-start.9 = (f32[2,16,256]{2,1,0:T(8,128)S(1)}, f32[2,16,256]{2,1,0:T(8,128)S(1)}, u32[]{:S(2)}, u32[]{:S(2)}) collective-permute-start(f32[2,16,256]{2,1,0:T(8,128)S(1)} %pad_maximum_fusion.1), channel_id=1, source_target_pairs={{0,96},{32,0},{64,32},{96,64},{1,97},{33,1},{65,33},{97,65},{2,98}... | collective-permute-start | bytes 98312 | tf_op jit(solution)/shard_map/ppermute | solution.py:32
  23.1 12.8 %collective-permute-start.8 = (f32[2,16,256]{2,1,0:T(8,128)S(1)}, f32[2,16,256]{2,1,0:T(8,128)S(1)}, u32[]{:S(2)}, u32[]{:S(2)}) collective-permute-start(f32[2,16,256]{2,1,0:T(8,128)S(1)} %pad_maximum_fusion.1), channel_id=1, source_target_pairs={{0,64},{32,96},{64,0},{96,32},{1,65},{33,97},{65,1},{97,33},{2,66}... | collective-permute-start | bytes 98312 | tf_op jit(solution)/shard_map/ppermute | solution.py:32
  23.6 12.2 %collective-permute-start.7 = (f32[2,16,256]{2,1,0:T(8,128)S(1)}, f32[2,16,256]{2,1,0:T(8,128)S(1)}, u32[]{:S(2)}, u32[]{:S(2)}) collective-permute-start(f32[2,16,256]{2,1,0:T(8,128)S(1)} %pad_maximum_fusion.1), channel_id=1, source_target_pairs={{0,32},{32,64},{64,96},{96,0},{1,33},{33,65},{65,97},{97,1},{2,34}... | collective-permute-start | bytes 98312 | tf_op jit(solution)/shard_map/ppermute | solution.py:32
  24.6 11.2 %collective-permute-start.5 = (f32[4,16,256]{2,1,0:T(8,128)S(1)}, f32[4,16,256]{2,1,0:T(8,128)S(1)}, u32[]{:S(2)}, u32[]{:S(2)}) collective-permute-start(f32[4,16,256]{2,1,0:T(8,128)S(1)} %pad_maximum_fusion), channel_id=1, source_target_pairs={{0,3},{1,0},{2,1},{3,2},{4,7},{5,4},{6,5},{7,6},{8,11},{9,8},{10,9... | collective-permute-start | bytes 196616 | tf_op jit(solution)/shard_map/ppermute | solution.py:32
  27.8 8.1 %collective-permute-start.4 = (f32[4,16,256]{2,1,0:T(8,128)S(1)}, f32[4,16,256]{2,1,0:T(8,128)S(1)}, u32[]{:S(2)}, u32[]{:S(2)}) collective-permute-start(f32[4,16,256]{2,1,0:T(8,128)S(1)} %pad_maximum_fusion), channel_id=1, source_target_pairs={{0,2},{1,3},{2,0},{3,1},{4,6},{5,7},{6,4},{7,5},{8,10},{9,11},{10,... | collective-permute-start | bytes 196616 | tf_op jit(solution)/shard_map/ppermute | solution.py:32
  28.3 7.6 %collective-permute-start.3 = (f32[4,16,256]{2,1,0:T(8,128)S(1)}, f32[4,16,256]{2,1,0:T(8,128)S(1)}, u32[]{:S(2)}, u32[]{:S(2)}) collective-permute-start(f32[4,16,256]{2,1,0:T(8,128)S(1)} %pad_maximum_fusion), channel_id=1, source_target_pairs={{0,1},{1,2},{2,3},{3,0},{4,5},{5,6},{6,7},{7,4},{8,9},{9,10},{10,1... | collective-permute-start | bytes 196616 | tf_op jit(solution)/shard_map/ppermute | solution.py:32
  30.5 10.6 %all-to-all-start.1 = ((f32[8,16,256]{2,1,0:T(8,128)}), f32[8,16,256]{2,1,0:T(8,128)S(1)}, u32[]{:S(2)}, u32[]{:S(2)}) async-start(f32[8,16,256]{2,1,0:T(8,128)} %get-tuple-element.17), calls=%async_computation.1 | async-start | bytes 262144 | tf_op jit(solution)/shard_map/all_to_all | solution.py:572
